TPU v7x, 128 devices: a whole 4x4x4 slice. The times are simulated.
128 devices in a mesh: seq: 4 (over x), head: 32 (over y, z, core).
Axes of the slice: x: 4, y: 4, z: 4, core: 2. Of those that a mesh axis runs over, the one named last changes fastest.
Arguments:
- queries: bfloat16 [32768, 4096], P(('seq', 'head')), may hold values from -6 to 6
- key_vectors: bfloat16 [32768, 4096], P(('seq', 'head')), may hold values from -0.375 to 0.375
- values: bfloat16 [32768, 8192], P(('seq', 'head')), may hold values from -6 to 6
- decay_log: bfloat16 [32768, 16], P(('seq', 'head')), may hold values from -0.8 to 0, as said below
- gate_input: bfloat16 [32768, 8192], P(('seq', 'head')), may hold values from -6 to 6
Outputs:
- retention_out: bfloat16 [32768, 8192], P(('seq', 'head'))
Inputs may be any that keep to these rules, and one draw needn't show every extreme that they name: `decay_log`: every entry is negative.
All inputs are finite; a program needn't handle non-finite values.
Results may differ from a plain program's by a relative error of at most 0.0063.
Values may be sent and summed in bfloat16 or wider, within the bound.
No kernel may reach another device: no remote copies, remote signals or barrier semaphores. Data moves between devices by JAX's collectives and lax.ppermute only.
A program may use at most 128 MiB of HBM per device.

v0:
```python
import math

import jax
import jax.numpy as jnp
from jax import lax
from jax.sharding import PartitionSpec as P

BLOCK = 512


def sent_to_all(shard, axis):
    count = lax.axis_size(axis)
    return lax.all_to_all(
        jnp.broadcast_to(shard[None], (count, *shard.shape)), axis, 0, 0, tiled=True
    )


def laid_out(tiles, dim):
    tiles = jnp.moveaxis(tiles, 0, dim)
    dims = tiles.shape
    return tiles.reshape(*dims[:dim], dims[dim] * dims[dim + 1], *dims[dim + 2 :])


def gather_directly(shard, axis, dim):
    tiles = sent_to_all(shard, axis)
    return laid_out(tiles, dim)


def sent_together(arrays, axis, dim, along):
    widths = [math.prod(a.shape[along:]) for a in arrays]
    both = jnp.concatenate(
        [a.reshape(*a.shape[:along], w) for a, w in zip(arrays, widths)], axis=along
    )
    result = gather_directly(both, axis, dim)
    tiles = jnp.split(result, [sum(widths[:k]) for k in range(1, len(widths))], axis=along)
    return tuple(
        (b.reshape(*result.shape[:along], *a.shape[along:]) for a, b in zip(arrays, tiles))
    )


def cut_along(shard, dim, count):
    before, after = (shard.shape[:dim], shard.shape[dim + 1 :])
    return jnp.moveaxis(shard.reshape(*before, count, -1, *after), dim, 0)


def cut_rows(length, count):
    unit = 8 if length >= 8 * count else 1
    return [length // unit * k // count * unit for k in range(1, count)]


def exchange_in_pieces(shard, axis, pieces, split_dim, concat_dim):
    tiles = cut_along(shard, split_dim, lax.axis_size(axis))
    cut = max(range(1, max(2, tiles.ndim - 1)), key=lambda d: tiles.shape[d])
    done = []
    for piece in jnp.split(tiles, cut_rows(tiles.shape[cut], pieces), axis=cut):
        if piece.size:
            done.append(lax.all_to_all(piece, axis, split_axis=0, concat_axis=0, tiled=True))
    return laid_out(jnp.concatenate(done, axis=cut), concat_dim)


def side_by_side(arrays, axis, split_dim, concat_dim, along):
    columns = [a.reshape(*a.shape[:along], -1) for a in arrays]
    both = jnp.concatenate(columns, axis=along)
    result, at, done = (
        lax.all_to_all(both, axis, split_axis=split_dim, concat_axis=concat_dim, tiled=True),
        0,
        [],
    )
    for a, column in zip(arrays, columns):
        piece = result[..., at : at + column.shape[along]]
        done.append(piece.reshape(*piece.shape[:along], *a.shape[along:]))
        at += column.shape[along]
    return tuple(done)


def partner_2(value, axis, apart):
    mask = 2**apart
    pairs = [(source, source ^ mask) for source in range(lax.axis_size(axis))]
    return lax.ppermute(value, axis, pairs)


def prefix_state(damping, closing):
    gathered = sent_together((damping[None], closing[None]), "seq", 0, 2)
    my_index = lax.axis_index("seq")

    def absorb(source, running_state):
        rate_row = lax.dynamic_index_in_dim(gathered[0], source, 0, keepdims=False)
        state_row = lax.dynamic_index_in_dim(gathered[1], source, 0, keepdims=False)
        stepped = rate_row[:, None, None] * running_state + state_row
        return jnp.where(source < my_index, stepped, running_state)

    incoming = lax.fori_loop(0, lax.axis_size("seq"), absorb, jnp.zeros_like(closing))
    return incoming


def retain_items(query_part, key_part, value_part, decay_part, carry_in):
    length, count, key_width = query_part.shape
    width = value_part.shape[2]
    blocks = length // BLOCK
    running = jnp.cumsum(decay_part.astype(jnp.float32).reshape(blocks, BLOCK, count), axis=1)
    block_decay = running[:, -1, :]
    query_blocks = query_part.reshape(blocks, BLOCK, count, key_width)
    key_blocks = key_part.reshape(blocks, BLOCK, count, key_width)
    value_blocks = value_part.reshape(blocks, BLOCK, count, width)
    faded = (
        key_blocks.astype(jnp.float32) * jnp.exp(block_decay[:, None, :] - running)[..., None]
    ).astype(jnp.bfloat16)
    additions = jnp.einsum(
        "bjnd,bjnw->bndw", faded, value_blocks, preferred_element_type=jnp.float32
    )

    def advance(carried_state, pieces):
        rate_row, addition = pieces
        return (jnp.exp(rate_row)[:, None, None] * carried_state + addition, carried_state)

    initial = jnp.zeros((count, key_width, width), jnp.float32)
    closing, local_starts = lax.scan(advance, initial, (block_decay, additions))
    damping = jnp.exp(jnp.sum(block_decay, axis=0))
    incoming = carry_in(damping, closing)
    before = jnp.cumsum(block_decay, axis=0) - block_decay
    starts = local_starts + jnp.exp(before)[:, :, None, None] * incoming[None]
    causal = jnp.arange(BLOCK)[:, None] >= jnp.arange(BLOCK)[None, :]

    def emit_block(pieces):
        query_block, key_block, value_block, running_block, start_state = pieces
        scores = jnp.einsum(
            "ind,jnd->nij", query_block, key_block, preferred_element_type=jnp.float32
        )
        spread = running_block.T[:, :, None] - running_block.T[:, None, :]
        factor = jnp.exp(jnp.where(causal[None], spread, -jnp.inf))
        weights = (scores * factor).astype(jnp.bfloat16)
        within = jnp.einsum(
            "nij,jnw->inw", weights, value_block, preferred_element_type=jnp.float32
        )
        across = jnp.einsum(
            "ind,ndw->inw",
            query_block,
            start_state.astype(jnp.bfloat16),
            preferred_element_type=jnp.float32,
        )
        across = across * jnp.exp(running_block)[:, :, None]
        return (within + across).astype(jnp.bfloat16)

    retained = lax.map(emit_block, (query_blocks, key_blocks, value_blocks, running, starts))
    return retained.reshape(length, count, width)


def send_back(retained):
    return exchange_in_pieces(retained[:, None], "head", 2, 0, 1)


def shards(queries, key_vectors, values, decay_log, gate_input):
    rows_here = queries.shape[0]
    head_count = decay_log.shape[1]
    key_width = queries.shape[1] // head_count
    value_width = values.shape[1] // head_count
    half_width = value_width // 2
    groups = lax.axis_size("head")
    per_device = 2 * head_count // groups
    value_items = values.reshape(rows_here, groups, per_device, half_width)
    decay_items = jnp.repeat(decay_log, 2, axis=1).reshape(rows_here, groups, per_device)
    paired = jnp.stack(
        (
            queries.reshape(rows_here, head_count, key_width),
            key_vectors.reshape(rows_here, head_count, key_width),
        ),
        axis=2,
    )
    paired = paired.reshape(rows_here, groups, per_device, key_width)
    paired_got, value_got, decay_got = side_by_side(
        (paired, value_items, decay_items), "head", 1, 0, 3
    )
    paired_got = paired_got[:, 0]
    value_got = value_got[:, 0]
    decay_got = decay_got[:, 0]
    length = paired_got.shape[0]
    partner = partner_2(paired_got, "head", 0)
    is_first = lax.axis_index("head") % 2 == 0
    query_sel = jnp.where(is_first, paired_got, partner)
    key_sel = jnp.where(is_first, partner, paired_got)
    retained = retain_items(query_sel, key_sel, value_got, decay_got, prefix_state)
    gathered_out = send_back(retained)
    retained_all = gathered_out.reshape(rows_here, head_count, value_width).astype(jnp.float32)
    average = jnp.mean(retained_all, axis=2, keepdims=True)
    centered = retained_all - average
    variance = jnp.mean(centered * centered, axis=2, keepdims=True)
    normed = centered / jnp.sqrt(variance + 1e-06)
    gated = (
        jax.nn.silu(gate_input.astype(jnp.float32).reshape(rows_here, head_count, value_width))
        * normed
    )
    return gated.astype(jnp.bfloat16).reshape(rows_here, head_count * value_width)


def solution(mesh):
    in_specs = (
        P(("seq", "head"), None),
        P(("seq", "head"), None),
        P(("seq", "head"), None),
        P(("seq", "head"), None),
        P(("seq", "head"), None),
    )
    out_specs = P(("seq", "head"), None)
    return jax.shard_map(shards, mesh=mesh, in_specs=in_specs, out_specs=out_specs, check_vma=False)
```

profile of v0, /device:TPU:1, one launch (start us, length us, event | category | flops | bytes accessed | tf_op | source)
XLA Modules:
  0.0 395.2 jit_solution(3180133201213793007)
XLA Ops:
  0.0 3.3 copy.95
  3.3 4.1 %copy.96 = bf16[256,4096]{0,1:T(8,128)(2,1)} copy(bf16[256,4096]{1,0:T(8,128)(2,1)} %param.12) | data formatting | bytes 4194304 | tf_op jit(solution)/shard_map/stack;reshape | solution.py:162
  7.4 6.4 %copy.74 = bf16[256,8192]{0,1:T(8,128)(2,1)} copy(bf16[256,8192]{1,0:T(8,128)(2,1)} %param.13) | data formatting | bytes 8388608 | tf_op args[2]
  13.8 2.1 pad_maximum_fusion.1
  17.2 107.1 %all_to_all.33 = bf16[256,32,1,513]{0,3,2,1:T(8,128)(2,1)} all-to-all(bf16[256,32,1,513]{0,3,2,1:T(8,128)(2,1)S(1)} %pad_maximum_fusion), channel_id=1, replica_groups=mesh['seq'=4,'head'=32] {'head'}, dimensions={1} | all-to-all | bytes 16809984 | tf_op jit(solution)/shard_map/all_to_all | solution.py:65
  124.3 13.5 %copy.76 = bf16[32,256,1,1,513]{4,1,0,3,2:T(8,128)(2,1)} copy(bf16[32,256,1,1,513]{1,4,0,3,2:T(8,128)(2,1)} %bitcast.175) | data formatting | bytes 16809984 | tf_op jit(solution)/shard_map/all_to_all | solution.py:65
  137.8 5.9 %slice_bitcast_fusion = (bf16[8192,1,256]{2,0,1:T(8,128)(2,1)}, bf16[8192,1,1,256]{3,0,2,1:T(8,128)(2,1)}) fusion(bf16[8192,1,1,513]{3,0,2,1:T(8,128)(2,1)} %bitcast.172), kind=kLoop, calls=%fused_computation.54 | loop fusion | bytes 16777216 | tf_op jit(solution)/shard_map/squeeze | solution.py:173
  144.1 2.2 convert_reduce_fusion
  149.6 1.6 collective-permute-done
  151.2 5.1 %broadcast_select_fusion = (bf16[8192,1,256]{2,0,1:T(8,128)(2,1)S(1)}, bf16[8192,1,256]{2,0,1:T(8,128)(2,1)}) fusion(bf16[8192,1,256]{2,0,1:T(8,128)(2,1)} %collective-permute-done, pred[]{:T(512)S(6)} %eq.5, bf16[8192,1,1,513]{3,0,2,1:T(8,128)(2,1)} %bitcast.174), kind=kLoop, calls=%fused_computation.60 | loop fusion | flops 4194304 | bytes 16777216 | tf_op jit(solution)/shard_map/jit(_where)/select_n | solution.py:180
  156.3 4.3 %fusion.44 = f32[16,1,256,256]{3,2,1,0:T(8,128)} fusion(bf16[16,512,256]{2,1,0:T(8,128)(2,1)S(1)} %bitcast.179, bf16[16,512,256]{2,1,0:T(8,128)(2,1)S(1)} %bitcast.176, f32[16,512]{1,0:T(8,128)S(1)} %fusion.48), kind=kOutput, calls=%fused_computation.62 | convolution fusion | flops 1080033280 | bytes 12615680 | tf_op jit(solution)/shard_map/bjnd,bjnw->bndw/dot_general | solution.py:108
  160.6 48.5 %while.39 = (s32[]{:T(128)}, f32[1,256,256]{2,1,0:T(8,128)S(1)}, f32[16,1,256,256]{3,2,1,0:T(8,128)}, f32[16,1]{0,1:T(1,128)S(1)}, f32[16,1,256,256]{3,2,1,0:T(8,128)}, /*index=5*/s32[]{:T(128)}, s32[]{:T(128)}) while((s32[]{:T(128)}, f32[1,256,256]{2,1,0:T(8,128)S(1)}, f32[16,1,256,256]{3,2,1,0:T(8,128)}, f32[16,1]{0,1:T(1,128)S(1)}, ...), condition=%wide.region_3.4_spmd.clone, body=%wide.region_2.3_spmd.clone.sunk | while | flops 262147 | bytes 1311340 | solution.py:117
  162.0 1.7 bitcast_add_fusion.4
  165.0 1.7 bitcast_add_fusion.4
  168.0 1.7 bitcast_add_fusion.4
  171.1 1.7 bitcast_add_fusion.4
  174.1 1.7 bitcast_add_fusion.4
  177.1 1.7 bitcast_add_fusion.4
  180.2 1.7 bitcast_add_fusion.4
  183.2 1.7 bitcast_add_fusion.4
  186.2 1.7 bitcast_add_fusion.4
  189.2 1.7 bitcast_add_fusion.4
  192.3 1.7 bitcast_add_fusion.4
  195.3 1.7 bitcast_add_fusion.4
  198.3 1.7 bitcast_add_fusion.4
  201.4 1.7 bitcast_add_fusion.4
  204.4 1.7 bitcast_add_fusion.4
  207.4 1.7 bitcast_add_fusion.4
  210.1 1.5 broadcast_in_dim.46
  211.6 4.0 %all-to-all-start.1 = ((f32[4,1,1,65537]{3,2,1,0:T(1,128)}), f32[4,1,1,65537]{3,2,1,0:T(1,128)S(1)}, u32[]{:S(2)}, u32[]{:S(2)}) async-start(f32[4,1,1,65537]{3,2,1,0:T(1,128)} %broadcast_in_dim.46), calls=%async_computation.1 | async-start | bytes 2101248 | tf_op jit(solution)/shard_map/all_to_all | solution.py:13
  215.8 14.4 %all-to-all-done.1 = f32[4,1,1,65537]{3,2,1,0:T(1,128)S(1)} async-done(((f32[4,1,1,65537]{3,2,1,0:T(1,128)}), f32[4,1,1,65537]{3,2,1,0:T(1,128)S(1)}, u32[]{:S(2)}, u32[]{:S(2)}) %all-to-all-start.1) | async-done | bytes 1048624 | tf_op jit(solution)/shard_map/all_to_all | solution.py:13
  230.2 3.4 slice_reduce_fusion
  233.9 5.8 %while.40 = (s32[]{:T(128)}, f32[1,256,256]{2,1,0:T(8,128)S(1)}, s32[]{:T(128)}, f32[4,1]{0,1:T(1,128)S(1)}, f32[4,1,256,256]{3,2,1,0:T(8,128)S(1)}, /*index=5*/s32[]{:T(128)}, s32[]{:T(128)}) while((s32[]{:T(128)}, f32[1,256,256]{2,1,0:T(8,128)S(1)}, s32[]{:T(128)}, f32[4,1]{0,1:T(1,128)S(1)}, f32[4,1,256,256]{3,2,1,0:T(8,128)S(1)}, ...), condition=%wide.region_7.8_spmd.clone, body=%wide.region_6.7_spmd.clone.sunk | while | flops 262148 | bytes 786549 | solution.py:92
  239.7 2.7 multiply_add_fusion
  242.4 61.1 %while.38 = (s32[]{:T(128)}, bf16[16,512,1,256]{3,1,0,2:T(8,128)(2,1)}, bf16[16,512,1,256]{3,1,2,0:T(8,128)(2,1)}, bf16[16,512,1,256]{3,1,2,0:T(8,128)(2,1)}, bf...) while((s32[]{:T(128)}, ...), condition=%wide.region_9.10_spmd.clone, body=%wide.region_8.9_spmd.clone.sunk | while | flops 337248256 | bytes 3556441 | solution.py:144
  242.5 1.7 convolution_bitcast_fusion.3
  244.2 1.2 fusion.64
  246.3 1.7 convolution_bitcast_fusion.3
  250.1 1.7 convolution_bitcast_fusion.3
  253.9 1.7 convolution_bitcast_fusion.3
  257.8 1.7 convolution_bitcast_fusion.3
  261.6 1.7 convolution_bitcast_fusion.3
  265.4 1.7 convolution_bitcast_fusion.3
  269.2 1.7 convolution_bitcast_fusion.3
  273.0 1.7 convolution_bitcast_fusion.3
  276.8 1.7 convolution_bitcast_fusion.3
  280.6 1.7 convolution_bitcast_fusion.3
  284.5 1.7 convolution_bitcast_fusion.3
  288.3 1.7 convolution_bitcast_fusion.3
  292.1 1.7 convolution_bitcast_fusion.3
  295.9 1.7 convolution_bitcast_fusion.3
  297.6 1.2 fusion.64
  299.7 1.7 convolution_bitcast_fusion.3
  303.5 4.0 %slice_bitcast_fusion.2 = (bf16[32,128,1,1,256]{4,1,3,2,0:T(8,128)(2,1)S(1)}, bf16[32,128,1,1,256]{4,1,3,2,0:T(8,128)(2,1)}) fusion(bf16[32,256,1,1,256]{4,1,0,3,2:T(8,128)(2,1)} %bitcast.189), kind=kLoop, calls=%fused_computation.64 | loop fusion | bytes 8388608 | tf_op jit(solution)/shard_map/split | solution.py:55
  307.5 33.1 %all_to_all.34 = bf16[32,128,1,1,256]{4,1,3,2,0:T(8,128)(2,1)} all-to-all(bf16[32,128,1,1,256]{4,1,3,2,0:T(8,128)(2,1)S(1)} %get-tuple-element.328), channel_id=1, replica_groups=mesh['seq'=4,'head'=32] {'head'}, dimensions={0} | all-to-all | bytes 4194304 | tf_op jit(solution)/shard_map/all_to_all | solution.py:57
  340.6 4.5 %all-to-all-start.3 = ((bf16[32,128,1,1,256]{4,1,3,2,0:T(8,128)(2,1)}), bf16[32,128,1,1,256]{4,1,3,2,0:T(8,128)(2,1)}, u32[]{:S(2)}, u32[]{:S(2)}) async-start(bf16[32,128,1,1,256]{4,1,3,2,0:T(8,128)(2,1)} %get-tuple-element.329), calls=%async_computation.3 | async-start | bytes 4194304 | tf_op jit(solution)/shard_map/all_to_all | solution.py:57
  345.2 6.4 %copy.71 = bf16[256,8192]{0,1:T(8,128)(2,1)} copy(bf16[256,8192]{1,0:T(8,128)(2,1)} %param.15) | data formatting | bytes 8388608 | tf_op args[4]
  351.6 3.2 copy.91
  354.8 18.8 %all-to-all-done.3 = bf16[32,128,1,1,256]{4,1,3,2,0:T(8,128)(2,1)} async-done(((bf16[32,128,1,1,256]{4,1,3,2,0:T(8,128)(2,1)}), bf16[32,128,1,1,256]{4,1,3,2,0:T(8,128)(2,1)}, u32[]{:S(2)}, u32[]{:S(2)}) %all-to-all-start.3) | async-done | bytes 2097184 | tf_op jit(solution)/shard_map/all_to_all | solution.py:57
  373.6 4.1 %copy.92 = bf16[32,128,1,1,256]{1,4,0,3,2:T(8,128)(2,1)} copy(bf16[32,128,1,1,256]{4,1,3,2,0:T(8,128)(2,1)} %all-to-all-done.3) | data formatting | bytes 4194304 | tf_op jit(solution)/shard_map/all_to_all | solution.py:57
  377.7 2.4 bitcast_reduce_fusion
  380.2 2.4 fusion.39
  382.7 6.2 %fusion.40 = bf16[256,8192]{0,1:T(8,128)(2,1)} fusion(bf16[256,8192]{0,1:T(8,128)(2,1)} %copy.71, f32[256,16]{0,1:T(8,128)S(1)} %add_sqrt_fusion, f32[256,16]{0,1:T(8,128)S(1)} %broadcast_multiply_fusion, bf16[32,128,1,1,256]{1,4,0,3,2:T(8,128)(2,1)} %copy.92, bf16[32,128,1,1,256]{1,4,0,3,2:T(8,128)(2,1)S(1)} %copy.91), kind=kLoop, calls=%fused_computation.52 | loop fusion | flops 27262976 | bytes 12615680 | tf_op jit(solution)/shard_map/convert_element_type | solution.py:192
  388.9 6.3 %copy.93 = bf16[256,8192]{1,0:T(8,128)(2,1)} copy(bf16[256,8192]{0,1:T(8,128)(2,1)} %fusion.40) | data formatting | bytes 8388608 | tf_op jit(solution)/shard_map/convert_element_type | solution.py:192
  (161 shorter events, 64.1 us)
Async XLA Ops:
  7.4 6.4 %copy-start.3 = (bf16[256,16]{0,1:T(8,128)(2,1)S(1)}, bf16[256,16]{0,1:T(8,128)(2,1)}, u32[]{:S(2)}) copy-start(bf16[256,16]{0,1:T(8,128)(2,1)} %param.14) | copy-start | bytes 24580
  13.8 2.8 copy-start.2
  143.7 7.5 %collective-permute-start = (bf16[8192,1,256]{2,0,1:T(8,128)(2,1)}, bf16[8192,1,256]{2,0,1:T(8,128)(2,1)}, u32[]{:S(2)}, u32[]{:S(2)}) collective-permute-start(bf16[8192,1,256]{2,0,1:T(8,128)(2,1)} %get-tuple-element.326), channel_id=1, source_target_pairs={{0,1},{1,0},{2,3},{3,2},{4,5},{5,4},{6,7},{7,6},{8,9},{9,8},{10,11... | collective-permute-start | bytes 12582920 | tf_op jit(solution)/shard_map/ppermute | solution.py:79
  149.6 6.8 %copy-start.1 = (bf16[8192,1,1,256]{3,0,2,1:T(8,128)(2,1)S(1)}, bf16[8192,1,1,256]{3,0,2,1:T(8,128)(2,1)}, u32[]{:S(2)}) copy-start(bf16[8192,1,1,256]{3,0,2,1:T(8,128)(2,1)} %get-tuple-element.327) | copy-start | bytes 12582916
  156.3 4.3 %copy-start = (bf16[8192,1,256]{2,0,1:T(8,128)(2,1)}, bf16[8192,1,256]{2,0,1:T(8,128)(2,1)S(1)}, u32[]{:S(2)}) copy-start(bf16[8192,1,256]{2,0,1:T(8,128)(2,1)S(1)} %get-tuple-element.324) | copy-start | bytes 12582916
  211.6 18.6 %all-to-all-start.1 = ((f32[4,1,1,65537]{3,2,1,0:T(1,128)}), f32[4,1,1,65537]{3,2,1,0:T(1,128)S(1)}, u32[]{:S(2)}, u32[]{:S(2)}) async-start(f32[4,1,1,65537]{3,2,1,0:T(1,128)} %broadcast_in_dim.46), calls=%async_computation.1 | async-start | bytes 2101248 | tf_op jit(solution)/shard_map/all_to_all | solution.py:13
  340.6 32.9 %all-to-all-start.3 = ((bf16[32,128,1,1,256]{4,1,3,2,0:T(8,128)(2,1)}), bf16[32,128,1,1,256]{4,1,3,2,0:T(8,128)(2,1)}, u32[]{:S(2)}, u32[]{:S(2)}) async-start(bf16[32,128,1,1,256]{4,1,3,2,0:T(8,128)(2,1)} %get-tuple-element.329), calls=%async_computation.3 | async-start | bytes 4194304 | tf_op jit(solution)/shard_map/all_to_all | solution.py:57
where the time goes:
time: 398 us; the launch traced here: 395 us
  blocking collectives  140 us (35%)
  local copies, waits for them, and re-layouts  90 us (23%)
  other arithmetic  68.5 us (17%)
  matrix products  51.1 us (13%)
  waiting for transfers between devices  34.8 us (9%)
  starting transfers between devices  8.95 us (2%)
    all_to_all x1, blocking collectives, side_by_side(): lax.all_to_all(both, axis, split_axis=split_dim, concat_axis=concat_dim,...  107 us
    all_to_all x1, blocking collectives, exchange_in_pieces(): lax.all_to_all(piece, axis, split_axis=0, concat_axis=0, tiled=True)  33.1 us
    dot_general x16, matrix products, emit_block(): jnp.einsum('nij,jnw->inw', weights, value_block, preferred_element_type=j...  27.2 us
    add x16, other arithmetic, advance(): jnp.exp(rate_row)[:, None, None] * carried_state + addition  26.7 us
    dot_general x16, matrix products, emit_block(): jnp.einsum('ind,ndw->inw', query_block, start_state.astype(jnp.bfloat16),...  19.6 us
    all_to_all x1, waiting for transfers between devices, exchange_in_pieces(): lax.all_to_all(piece, axis, split_axis=0, concat_axis=0, tiled=True)  18.8 us
    all_to_all x1, waiting for transfers between devices, sent_to_all(): lax.all_to_all(jnp.broadcast_to(shard[None], (count, *shard.shape)), axis...  14.4 us
    dynamic_update_slice x32, local copies, waits for them, and re-layouts, retain_items(): lax.map(emit_block, (query_blocks, key_blocks, value_blocks, running, sta...  13.7 us
  transfers between devices with their start and end apart: 3, of which 3 were waited for; matrix products, arithmetic and copies ran while one was open for 4% of the time, Pallas kernels for 0%

commit v1 on v0

v1 whole, which is shorter than its diff:
```python
import functools

import jax
import jax.numpy as jnp
from jax import lax
from jax.experimental import pallas as pl
from jax.experimental.pallas import tpu as pltpu
from jax.sharding import Mesh, PartitionSpec as P

HEADS = 16
DK = 256
DV = 512
ROWS = 256
HALF = HEADS // 2
CHIPS = 64
SLICES = CHIPS // HALF
PIECE = DK // SLICES
TILES = DV // 128
SLICE = PIECE * TILES
SENT = SLICE + 8

f32 = jnp.float32
bf16 = jnp.bfloat16


def triangle():
    rows = lax.broadcasted_iota(jnp.int32, (ROWS, ROWS), 0)
    cols = lax.broadcasted_iota(jnp.int32, (ROWS, ROWS), 1)
    return rows >= cols


def running_of(decay):
    return jnp.dot(triangle().astype(f32).astype(bf16), decay, preferred_element_type=f32)


def running_rows(decay):
    ones = triangle().astype(f32).astype(bf16)
    return lax.dot_general(decay, ones, (((0,), (1,)), ((), ())), preferred_element_type=f32)


def column(table, head):
    lanes = lax.broadcasted_iota(jnp.int32, table.shape, 1)
    return jnp.sum(jnp.where(lanes == head, table, 0.0), axis=1, keepdims=True)


def chunk_state(key, value, run, head):
    fade = column(jnp.exp(run[ROWS - 1 : ROWS, :] - run), head)
    faded = (key.astype(f32) * fade).astype(bf16)
    return lax.dot_general(faded, value, (((0,), (0,)), ((), ())), preferred_element_type=f32)


def put_slices(ref, state):
    for o in range(SLICES):
        for t in range(TILES):
            ref[o, t * PIECE : (t + 1) * PIECE, :] = state[
                o * PIECE : (o + 1) * PIECE, t * 128 : (t + 1) * 128
            ]


def get_slices(ref):
    cols = [
        ref[:, t * PIECE : (t + 1) * PIECE, :].reshape(DK, 128) for t in range(TILES)
    ]
    return jnp.concatenate(cols, axis=1)


def partner_state_kernel(core_ref, key_ref, value_ref, decay_ref, out_ref, run_ref):
    step = pl.program_id(0)

    @pl.when(step == 0)
    def _():
        run_ref[...] = running_of(decay_ref[...])

    head = (1 - core_ref[0]) * HALF + step
    state = chunk_state(key_ref[...], value_ref[...], run_ref[...], head)
    put_slices(out_ref, state.astype(bf16))


def own_state_kernel(
    core_ref, key_ref, value_ref, decay_ref, other_ref, got_ref,
    out_ref, first_ref, damp_ref, run_ref, other_run_ref,
):
    step = pl.program_id(0)

    @pl.when(step == 0)
    def _():
        run_ref[...] = running_of(decay_ref[...])
        other_run_ref[...] = running_of(other_ref[...])

    core = core_ref[0]
    head = core * HALF + step
    run = run_ref[...]
    own = chunk_state(key_ref[...], value_ref[...], run, head)
    got = get_slices(got_ref).astype(f32)
    total = column(run[ROWS - 8 :, :], head)[7:8, :]
    other_total = column(other_run_ref[ROWS - 8 :, :], head)[7:8, :]
    is_first = core == 0
    own_rate = jnp.exp(jnp.where(is_first, other_total, 0.0))
    got_rate = jnp.exp(jnp.where(is_first, 0.0, total))
    both = own * own_rate + got * got_rate
    put_slices(out_ref, both.astype(bf16))
    put_slices(first_ref, jnp.where(is_first, own, got).astype(bf16))
    damping = jnp.broadcast_to(jnp.exp(total + other_total), (8, 128))
    high = damping.astype(bf16).astype(f32)
    rest = damping - high
    middle = rest.astype(bf16).astype(f32)
    low = rest - middle
    rows = lax.broadcasted_iota(jnp.int32, (8, 128), 0)
    parts = jnp.where(rows == 0, high, jnp.where(rows == 1, middle, low)).astype(bf16)
    for o in range(SLICES):
        out_ref[o, SLICE:SENT, :] = parts
    first_total = jnp.where(is_first, total, other_total)
    damp_ref[0] = jnp.broadcast_to(jnp.exp(first_total), (8, 128))


def within_kernel(query_ref, key_ref, value_ref, decay_ref, out_ref, run_ref, rows_ref):
    head = pl.program_id(0)

    @pl.when(head == 0)
    def _():
        run_ref[...] = running_of(decay_ref[...])
        rows_ref[...] = running_rows(decay_ref[...])

    scores = lax.dot_general(
        query_ref[...], key_ref[...], (((1,), (1,)), ((), ())), preferred_element_type=f32
    )
    spread = column(run_ref[...], head) - rows_ref[pl.ds(head, 1), :]
    factor = jnp.exp(jnp.where(triangle(), spread, -jnp.inf))
    weights = (scores * factor).astype(bf16)
    out_ref[...] = jnp.dot(weights, value_ref[...], preferred_element_type=f32)


STEP = 8


def prefix_kernel(in_ref, out_ref, state_ref):
    @pl.when(pl.program_id(0) == 0)
    def _():
        state_ref[...] = jnp.zeros_like(state_ref)

    state = state_ref[...]
    for b in range(STEP):
        parts = in_ref[b, SLICE:SENT, :].astype(f32)
        damping = parts[0:1] + parts[1:2] + parts[2:3]
        out_ref[b] = state.astype(bf16)
        state = damping * state + in_ref[b, :SLICE, :].astype(f32)
    state_ref[...] = state


def middle_kernel(core_ref, start_ref, first_ref, damp_ref, send_ref, use_ref):
    is_first = core_ref[0] == 0
    start = start_ref[...].astype(f32)
    middle = start * damp_ref[0, 0:1, :][None] + first_ref[...].astype(f32)
    send_ref[...] = jnp.where(is_first, middle, start).astype(bf16)
    use_ref[...] = jnp.where(is_first, start, middle).astype(bf16)


def finish_kernel(group_ref, query_ref, start_ref, within_ref, gate_ref, decay_ref, *rest):
    out_ref, run_ref = rest[-2:]
    step = pl.program_id(0)

    @pl.when(step == 0)
    def _():
        run_ref[...] = running_of(decay_ref[...])

    head = group_ref[0] * HALF + step
    across = jnp.dot(query_ref[...], get_slices(start_ref), preferred_element_type=f32)
    retained = within_ref[...] + across * jnp.exp(column(run_ref[...], head))
    average = jnp.mean(retained, axis=1, keepdims=True)
    centered = retained - average
    variance = jnp.mean(centered * centered, axis=1, keepdims=True)
    normed = centered * lax.rsqrt(variance + 1e-06)
    gate = gate_ref[...].astype(f32)
    out_ref[...] = (gate / (1.0 + jnp.exp(-gate)) * normed).astype(bf16)


def call(kernel, name, grid, in_specs, out_specs, out_shape, scratch, flops, aliases=None):
    return pl.pallas_call(
        kernel,
        out_shape=out_shape,
        grid_spec=pltpu.PrefetchScalarGridSpec(
            num_scalar_prefetch=1,
            grid=(grid,),
            in_specs=in_specs,
            out_specs=out_specs,
            scratch_shapes=scratch,
        ),
        compiler_params=pltpu.CompilerParams(dimension_semantics=("arbitrary",)),
        cost_estimate=pl.CostEstimate(flops=flops, transcendentals=0, bytes_accessed=0),
        input_output_aliases=aliases or {},
        name=name,
    )


def shape(*dims, dtype=bf16):
    return jax.ShapeDtypeStruct(dims, dtype)


def shards(queries, key_vectors, values, decay_log, gate_input):
    core = lax.axis_index("core").astype(jnp.int32).reshape(1)
    swap = [(0, 1), (1, 0)]
    other_decay = lax.ppermute(decay_log, "core", swap)

    whole = pl.BlockSpec((ROWS, HEADS), lambda i, c: (0, 0))
    own = lambda width: pl.BlockSpec((ROWS, width), lambda i, c: (0, c[0] * HALF + i))
    theirs = lambda width: pl.BlockSpec((ROWS, width), lambda i, c: (0, (1 - c[0]) * HALF + i))
    slices = pl.BlockSpec((SLICES, SLICE, 128), lambda i, c: (i, 0, 0))
    sent = pl.BlockSpec((SLICES, SENT, 128), lambda i, c: (i, 0, 0))
    damp = pl.BlockSpec((1, 8, 128), lambda i, c: (i, 0, 0))
    table = pltpu.VMEM((ROWS, HEADS), f32)

    theirs_state = call(
        partner_state_kernel, "partner_state", HALF, [theirs(DK), theirs(DV), whole], slices,
        shape(CHIPS, SLICE, 128), [table], 2 * HALF * ROWS * DK * DV,
    )(core, key_vectors, values, decay_log)
    got = lax.ppermute(theirs_state, "core", swap)
    block_state, first_state, damping = call(
        own_state_kernel, "own_state", HALF,
        [own(DK), own(DV), whole, whole, slices], [sent, slices, damp],
        [shape(CHIPS, SENT, 128), shape(CHIPS, SLICE, 128), shape(HALF, 8, 128, dtype=f32)],
        [table, table], 2 * HALF * ROWS * DK * DV,
    )(core, key_vectors, values, decay_log, other_decay, got)
    everyone = ("seq", "chip")
    collected = lax.all_to_all(block_state, everyone, 0, 0, tiled=True)

    head_block = lambda width: pl.BlockSpec((ROWS, width), lambda i: (0, i))
    within = pl.pallas_call(
        within_kernel,
        out_shape=shape(ROWS, HEADS * DV, dtype=f32),
        grid=(HEADS,),
        in_specs=[head_block(DK), head_block(DK), head_block(DV), pl.BlockSpec((ROWS, HEADS), lambda i: (0, 0))],
        out_specs=head_block(DV),
        scratch_shapes=[table, pltpu.VMEM((HEADS, ROWS), f32)],
        compiler_params=pltpu.CompilerParams(dimension_semantics=("arbitrary",)),
        cost_estimate=pl.CostEstimate(flops=2 * HEADS * ROWS * ROWS * (DK + DV), transcendentals=0, bytes_accessed=0),
        name="within",
    )(queries, key_vectors, values, decay_log)

    starts = pl.pallas_call(
        prefix_kernel,
        out_shape=shape(CHIPS, SLICE, 128),
        grid=(CHIPS // STEP,),
        in_specs=[pl.BlockSpec((STEP, SENT, 128), lambda i: (i, 0, 0))],
        out_specs=pl.BlockSpec((STEP, SLICE, 128), lambda i: (i, 0, 0)),
        scratch_shapes=[pltpu.VMEM((SLICE, 128), f32)],
        compiler_params=pltpu.CompilerParams(dimension_semantics=("arbitrary",)),
        name="prefix",
    )(collected)
    start = lax.all_to_all(starts, everyone, 0, 0, tiled=True)
    send, use = call(
        middle_kernel, "middle", HALF, [slices, slices, damp], [slices, slices],
        [shape(CHIPS, SLICE, 128)] * 2, [], 4 * CHIPS * SLICE * 128,
    )(core, start, first_state, damping)
    their_use = lax.ppermute(send, "core", swap)

    specs = [own(DK), slices, own(DV), own(DV), whole]
    flops = 2 * HALF * ROWS * DK * DV
    half = call(
        finish_kernel, "finish_own", HALF, specs, own(DV), shape(ROWS, HEADS * DV), [table], flops,
    )(core, queries, use, within, gate_input, decay_log)
    return call(
        finish_kernel, "finish_theirs", HALF, specs + [pl.BlockSpec(memory_space=pl.ANY)], own(DV),
        shape(ROWS, HEADS * DV), [table], flops, {6: 0},
    )(1 - core, queries, their_use, within, gate_input, decay_log, half)


def solution(mesh):
    mesh = Mesh(mesh.devices.reshape(4, 16, 2), ("seq", "chip", "core"))
    spec = P(("seq", "chip", "core"), None)
    return jax.shard_map(
        shards, mesh=mesh, in_specs=(spec,) * 5, out_specs=spec, check_vma=False
    )
```

time: 398 us -> 152 us (0.38)
  local copies, waits for them, and re-layouts: 90 us -> 4.75 us
  other arithmetic: 68.5 us -> 0 us
  blocking collectives: 140 us -> 73.9 us
  Pallas kernels: 0 us -> 61.6 us
  matrix products: 51.1 us -> 0 us
  waiting for transfers between devices: 34.8 us -> 4.01 us
    all_to_all x2, blocking collectives: 140 us -> 73.9 us  [the longest x1 42.1 us: shards(): collected = lax.all_to_all(block_state, everyone, 0, 0, tiled=True)]
    pallas_call x0 -> x7, Pallas kernels: none -> 61.6 us  [the longest x1 15.1 us: shards(): pl.pallas_call(within_kernel, out_shape=shape(ROWS, HEADS * DV, dtype=f32...]
    dot_general x33 -> x0, matrix products: 51.1 us -> none  [the longest x16 27.2 us: emit_block(): jnp.einsum('nij,jnw->inw', weights, value_block, preferred_element_type=j...]
    all_to_all x2 -> x0, waiting for transfers between devices: 33.2 us -> none  [the longest x1 18.8 us: exchange_in_pieces(): lax.all_to_all(piece, axis, split_axis=0, concat_axis=0, tiled=True)]
    add x17 -> x0, other arithmetic: 29.4 us -> none  [the longest x16 26.7 us: advance(): jnp.exp(rate_row)[:, None, None] * carried_state + addition]
    all_to_all x3 -> x0, local copies, waits for them, and re-layouts: 20.8 us -> none  [the longest x1 13.5 us: side_by_side(): lax.all_to_all(both, axis, split_axis=split_dim, concat_axis=concat_dim,...]
    dynamic_update_slice x32 -> x0, local copies, waits for them, and re-layouts: 13.7 us -> none  [retain_items(): lax.map(emit_block, (query_blocks, key_blocks, value_blocks, running, sta...]
    dynamic_update_slice x16 -> x0, other arithmetic: 11.7 us -> none  [retain_items(): closing, local_starts = lax.scan(advance, initial, (block_decay, additions))]
  transfers between devices with their start and end apart: 3 -> 3, of which waited for: 3 -> 1; matrix products, arithmetic and copies ran while one was open for 4% -> 0% of each run, Pallas kernels for 0% -> 16%
where the time goes in v1:
time: 152 us; the launch traced here: 150 us
  blocking collectives  73.9 us (49%)
  Pallas kernels  61.6 us (41%)
  starting transfers between devices  6 us (4%)
  local copies, waits for them, and re-layouts  4.75 us (3%)
  waiting for transfers between devices  4.01 us (3%)
    all_to_all x1, blocking collectives, shards(): collected = lax.all_to_all(block_state, everyone, 0, 0, tiled=True)  42.1 us
    all_to_all x1, blocking collectives, shards(): start = lax.all_to_all(starts, everyone, 0, 0, tiled=True)  31.8 us
    pallas_call x1, Pallas kernels, shards(): pl.pallas_call(within_kernel, out_shape=shape(ROWS, HEADS * DV, dtype=f32...  15.1 us
    pallas_call x1, Pallas kernels, shards(): call(finish_kernel, 'finish_own', HALF, specs, own(DV), shape(ROWS, HEADS...  9.05 us
    pallas_call x1, Pallas kernels, shards(): call(finish_kernel, 'finish_theirs', HALF, specs + [pl.BlockSpec(memory_s...  9.04 us
    pallas_call x1, Pallas kernels, shards(): call(own_state_kernel, 'own_state', HALF, [own(DK), own(DV), whole, whole...  8.3 us
    pallas_call x1, Pallas kernels, shards(): call(partner_state_kernel, 'partner_state', HALF, [theirs(DK), theirs(DV)...  7.42 us
    pallas_call x1, Pallas kernels, shards(): call(middle_kernel, 'middle', HALF, [slices, slices, damp], [slices, slic...  6.82 us
  transfers between devices with their start and end apart: 3, of which 1 were waited for; matrix products, arithmetic and copies ran while one was open for 0% of the time, Pallas kernels for 16%

profile of v1, /device:TPU:1, one launch (start us, length us, event | category | flops | bytes accessed | tf_op | source)
XLA Modules:
  0.0 150.2 jit_solution(3609345496636583238)
XLA Ops:
  0.0 1.4 copy.9.decay_ref
  1.4 0.0 copy-start
  1.4 7.4 %partner_state.1 = bf16[64,128,128]{2,1,0:T(8,128)(2,1)} custom-call(s32[1]{0:T(128)} %bitcast.core_ref.group_ref, bf16[256,4096]{1,0:T(8,128)(2,1)} %key_ref.5, bf16[256,8192]{1,0:T(8,128)(2,1)} %value_ref.5, bf16[256,16]{1,0:T(8,128)(2,1)} %copy.9.decay_ref), custom_call_target="tpu_custom_call" | custom-call | flops 536870912 | tf_op jit(solution)/shard_map/partner_state/pallas_call | solution.py:212
  8.8 1.4 collective-permute-start.1
  10.2 0.0 copy-done
  10.2 0.1 collective-permute-start
  10.3 4.0 %collective-permute-done.other_ref = bf16[256,16]{1,0:T(8,128)(2,1)S(1)} collective-permute-done((bf16[256,16]{1,0:T(8,128)(2,1)S(1)}, bf16[256,16]{1,0:T(8,128)(2,1)S(1)}, u32[]{:S(2)}, u32[]{:S(2)}) %collective-permute-start) | collective-permute-done | bytes 8224 | tf_op jit(solution)/shard_map/ppermute | solution.py:202
  14.3 0.0 copy-start.3
  14.3 0.0 collective-permute-done.1.got_ref
  14.3 0.6 copy-done.3
  14.9 0.0 copy-start.1
  14.9 1.3 copy-done.1
  16.3 8.3 %own_state.1 = (bf16[64,136,128]{2,1,0:T(8,128)(2,1)}, bf16[64,128,128]{2,1,0:T(8,128)(2,1)}, f32[8,8,128]{2,1,0:T(8,128)}) custom-call(s32[1]{0:T(128)} %bitcast.core_ref.group_ref, bf16[256,4096]{1,0:T(8,128)(2,1)} %key_ref.5, bf16[256,8192]{1,0:T(8,128)(2,1)} %value_ref.5, bf16[256,16]{1,0:T(8,128)(2,1)} %copy.9.decay_ref, bf16[256,16]{1,0:T(8,128)(2,1)} %copy-done.3, ...), custom_call_target="tpu_custom_call" | custom-call | flops 536870912 | tf_op jit(solution)/shard_map/own_state/pallas_call | solution.py:217
  24.6 42.1 %all_to_all.10.in_ref = bf16[64,136,128]{2,1,0:T(8,128)(2,1)} all-to-all(bf16[64,136,128]{2,1,0:T(8,128)(2,1)} %get-tuple-element.10), channel_id=1, replica_groups=mesh['seq'=4,'chip'=16,'core'=2] {'seq','chip'}, dimensions={0} | all-to-all | bytes 4456448 | tf_op jit(solution)/shard_map/all_to_all | solution.py:224
  66.7 5.8 %prefix.1 = bf16[64,128,128]{2,1,0:T(8,128)(2,1)} custom-call(bf16[64,136,128]{2,1,0:T(8,128)(2,1)} %all_to_all.10.in_ref), custom_call_target="tpu_custom_call" | custom-call | tf_op jit(solution)/shard_map/prefix/pallas_call | solution.py:239
  72.5 31.8 %all_to_all.11.start_ref = bf16[64,128,128]{2,1,0:T(8,128)(2,1)} all-to-all(bf16[64,128,128]{2,1,0:T(8,128)(2,1)} %prefix.1), channel_id=1, replica_groups=mesh['seq'=4,'chip'=16,'core'=2] {'seq','chip'}, dimensions={0} | all-to-all | bytes 4194304 | tf_op jit(solution)/shard_map/all_to_all | solution.py:249
  104.3 6.8 %middle.1 = (bf16[64,128,128]{2,1,0:T(8,128)(2,1)}, bf16[64,128,128]{2,1,0:T(8,128)(2,1)}) custom-call(s32[1]{0:T(128)} %bitcast.core_ref.group_ref, bf16[64,128,128]{2,1,0:T(8,128)(2,1)} %all_to_all.11.start_ref, bf16[64,128,128]{2,1,0:T(8,128)(2,1)} %get-tuple-element.11.first_ref, f32[8,8,128]{2,1,0:T(8,128)} %get-tuple-element.12.damp_ref), custom_call_target="tpu_custom_call" | custom-call | flops 4194304 | tf_op jit(solution)/shard_map/middle/pallas_call | solution.py:250
  111.1 4.5 %collective-permute-start.2 = (bf16[64,128,128]{2,1,0:T(8,128)(2,1)}, bf16[64,128,128]{2,1,0:T(8,128)(2,1)S(1)}, u32[]{:S(2)}, u32[]{:S(2)}) collective-permute-start(bf16[64,128,128]{2,1,0:T(8,128)(2,1)} %get-tuple-element.13), channel_id=1, source_target_pairs={{0,1},{1,0},{2,3},{3,2},{4,5},{5,4},{6,7},{7,6},{8,9},{9,8},{10,11... | collective-permute-start | bytes 6291464 | tf_op jit(solution)/shard_map/ppermute | solution.py:254
  115.7 15.1 %within.1.within_ref = f32[256,8192]{1,0:T(8,128)} custom-call(bf16[256,4096]{1,0:T(8,128)(2,1)} %query_ref.5, bf16[256,4096]{1,0:T(8,128)(2,1)} %key_ref.5, bf16[256,8192]{1,0:T(8,128)(2,1)} %value_ref.5, bf16[256,16]{1,0:T(8,128)(2,1)} %copy.9.decay_ref), custom_call_target="tpu_custom_call" | custom-call | flops 1610612736 | tf_op jit(solution)/shard_map/within/pallas_call | solution.py:227
  130.8 9.0 %finish_own.1.rest_0_ = bf16[256,8192]{1,0:T(8,128)(2,1)} custom-call(s32[1]{0:T(128)} %bitcast.core_ref.group_ref, bf16[256,4096]{1,0:T(8,128)(2,1)} %query_ref.5, bf16[64,128,128]{2,1,0:T(8,128)(2,1)} %get-tuple-element.14.start_ref, f32[256,8192]{1,0:T(8,128)} %within.1.within_ref, bf16[256,8192]{1,0:T(8,128)(2,1)} %gate_ref.3, bf16[256,16]{1,0:T(8,128)(2,1)} %copy.9.decay_ref), custom_call_target="tpu_custom_call" | custom-call | flops 536870912 | tf_op jit(solution)/shard_map/finish_own/pallas_call | solution.py:258
  139.8 0.0 collective-permute-done.2.start_ref
  139.8 0.0 copy-start.2
  139.8 1.4 copy-done.2
  141.2 9.0 %finish_theirs.1 = bf16[256,8192]{1,0:T(8,128)(2,1)} custom-call(s32[1]{0:T(128)S(6)} %sub.3.group_ref, bf16[256,4096]{1,0:T(8,128)(2,1)} %query_ref.5, bf16[64,128,128]{2,1,0:T(8,128)(2,1)} %copy-done.2, f32[256,8192]{1,0:T(8,128)} %within.1.within_ref, bf16[256,8192]{1,0:T(8,128)(2,1)} %gate_ref.3, ...), custom_call_target="tpu_custom_call", output_to_operand_aliasing={{}: (6, {})} | custom-call | flops 536870912 | tf_op jit(solution)/shard_map/finish_theirs/pallas_call | solution.py:261
Async XLA Ops:
  1.4 8.8 %copy-start = (bf16[256,16]{1,0:T(8,128)(2,1)S(1)}, bf16[256,16]{1,0:T(8,128)(2,1)}, u32[]{:S(2)}) copy-start(bf16[256,16]{1,0:T(8,128)(2,1)} %copy.9.decay_ref) | copy-start | bytes 24580
  8.8 5.5 %collective-permute-start.1 = (bf16[64,128,128]{2,1,0:T(8,128)(2,1)}, bf16[64,128,128]{2,1,0:T(8,128)(2,1)S(1)}, u32[]{:S(2)}, u32[]{:S(2)}) collective-permute-start(bf16[64,128,128]{2,1,0:T(8,128)(2,1)} %partner_state.1), channel_id=1, source_target_pairs={{0,1},{1,0},{2,3},{3,2},{4,5},{5,4},{6,7},{7,6},{8,9},{9,8},{10,11... | collective-permute-start | bytes 6291464 | tf_op jit(solution)/shard_map/ppermute | solution.py:216
  10.2 4.1 %collective-permute-start = (bf16[256,16]{1,0:T(8,128)(2,1)S(1)}, bf16[256,16]{1,0:T(8,128)(2,1)S(1)}, u32[]{:S(2)}, u32[]{:S(2)}) collective-permute-start(bf16[256,16]{1,0:T(8,128)(2,1)S(1)} %copy-done), channel_id=1, source_target_pairs={{0,1},{1,0},{2,3},{3,2},{4,5},{5,4},{6,7},{7,6},{8,9},{9,8},{10,11... | collective-permute-start | bytes 24584 | tf_op jit(solution)/shard_map/ppermute | solution.py:202
  14.3 0.6 copy-start.3
  14.9 1.3 copy-start.1
  111.1 28.7 %collective-permute-start.2 = (bf16[64,128,128]{2,1,0:T(8,128)(2,1)}, bf16[64,128,128]{2,1,0:T(8,128)(2,1)S(1)}, u32[]{:S(2)}, u32[]{:S(2)}) collective-permute-start(bf16[64,128,128]{2,1,0:T(8,128)(2,1)} %get-tuple-element.13), channel_id=1, source_target_pairs={{0,1},{1,0},{2,3},{3,2},{4,5},{5,4},{6,7},{7,6},{8,9},{9,8},{10,11... | collective-permute-start | bytes 6291464 | tf_op jit(solution)/shard_map/ppermute | solution.py:254
  139.8 1.4 copy-start.2

commit v2 on v1

v2 whole, which is shorter than its diff:
```python
import jax
import jax.numpy as jnp
from jax import lax
from jax.experimental import pallas as pl
from jax.experimental.pallas import tpu as pltpu
from jax.sharding import Mesh, PartitionSpec as P

HEADS = 16
DK = 256
DV = 512
ROWS = 256
HALF = HEADS // 2
CHIPS = 64
SLICES = CHIPS // HALF
PIECE = DK // SLICES
TILES = DV // 128
SLICE = PIECE * TILES
SENT = SLICE + 8
PER_STEP = 4
BLOCKS_PER_STEP = 32

f32 = jnp.float32
bf16 = jnp.bfloat16


def triangle():
    rows = lax.broadcasted_iota(jnp.int32, (ROWS, ROWS), 0)
    cols = lax.broadcasted_iota(jnp.int32, (ROWS, ROWS), 1)
    return rows >= cols


def running_of(decay):
    ones = triangle().astype(f32).astype(bf16)
    return lax.dot_general(ones, decay, (((1,), (1,)), ((), ())), preferred_element_type=f32)


def running_rows(decay):
    ones = triangle().astype(f32).astype(bf16)
    return lax.dot_general(decay, ones, (((1,), (1,)), ((), ())), preferred_element_type=f32)


def column(table, head):
    lanes = lax.broadcasted_iota(jnp.int32, table.shape, 1)
    return jnp.sum(jnp.where(lanes == head, table, 0.0), axis=1, keepdims=True)


def put_slices(ref, at, state):
    for o in range(SLICES):
        for t in range(TILES):
            ref[at * SLICES + o, t * PIECE : (t + 1) * PIECE, :] = state[
                o * PIECE : (o + 1) * PIECE, t * 128 : (t + 1) * 128
            ]


def get_slices(ref, at):
    cols = [
        ref[at * SLICES : (at + 1) * SLICES, t * PIECE : (t + 1) * PIECE, :].reshape(DK, 128)
        for t in range(TILES)
    ]
    return jnp.concatenate(cols, axis=1)


def state_kernel(group_ref, key_ref, value_ref, decay_ref, out_ref, fade_ref):
    step = pl.program_id(0)

    @pl.when(step == 0)
    def _():
        run = running_of(decay_ref[...])
        fade_ref[...] = jnp.exp(run[ROWS - 1 : ROWS, :] - run)

    for n in range(PER_STEP):
        fade = column(fade_ref[...], group_ref[0] * HALF + step * PER_STEP + n)
        faded = (key_ref[:, n * DK : (n + 1) * DK].astype(f32) * fade).astype(bf16)
        state = lax.dot_general(
            faded, value_ref[:, n * DV : (n + 1) * DV], (((0,), (0,)), ((), ())),
            preferred_element_type=f32,
        )
        put_slices(out_ref, n, state.astype(bf16))


def combine_kernel(core_ref, own_ref, got_ref, decay_ref, other_ref, out_ref, rate_ref):
    step = pl.program_id(0)
    is_first = core_ref[0] == 0

    @pl.when(step == 0)
    def _():
        ones = jnp.ones((128, ROWS), f32).astype(bf16)
        total = lax.dot_general(
            decay_ref[...], ones, (((1,), (1,)), ((), ())), preferred_element_type=f32
        )
        other = lax.dot_general(
            other_ref[...], ones, (((1,), (1,)), ((), ())), preferred_element_type=f32
        )
        rate_ref[0] = jnp.exp(jnp.where(is_first, other, 0.0))
        rate_ref[1] = jnp.exp(jnp.where(is_first, 0.0, total))
        rate_ref[2] = jnp.exp(total + other)

    rows = lax.broadcasted_iota(jnp.int32, (8, 128), 0)
    for n in range(PER_STEP):
        head = pl.ds(core_ref[0] * HALF + step * PER_STEP + n, 1)
        own_rate = rate_ref[0, head, :]
        got_rate = rate_ref[1, head, :]
        damping = rate_ref[2, head, :]
        high = damping.astype(bf16).astype(f32)
        rest = damping - high
        middle = rest.astype(bf16).astype(f32)
        parts = jnp.where(rows == 0, high, jnp.where(rows == 1, middle, rest - middle))
        parts = parts.astype(bf16)
        for o in range(n * SLICES, (n + 1) * SLICES):
            both = own_ref[o].astype(f32) * own_rate + got_ref[o].astype(f32) * got_rate
            out_ref[o, :SLICE, :] = both.astype(bf16)
            out_ref[o, SLICE:SENT, :] = parts


def within_kernel(
    core_ref, *refs,
):
    own, theirs = refs[0:4], refs[4:8]
    decay_ref, other_ref, own_out, theirs_out, reach_out, run_ref, rows_ref, reach_ref = refs[8:]
    step = pl.program_id(0)
    core = core_ref[0]

    @pl.when(step == 0)
    def _():
        run = running_of(decay_ref[...])
        run_ref[...] = run
        rows_ref[...] = running_rows(decay_ref[...])
        other = running_of(other_ref[...])[ROWS - 1 : ROWS, :]
        reach_out[...] = jnp.exp(run + jnp.where(core == 0, 0.0, other))
        reach_ref[...] = jnp.where(core == 0, 0.0, jnp.exp(run))

    for group, ins, out_ref in ((core, own, own_out), (1 - core, theirs, theirs_out)):
        query_ref, key_ref, value_ref, state_ref = ins
        head = group * HALF + step
        query = query_ref[...]
        scores = lax.dot_general(
            query, key_ref[...], (((1,), (1,)), ((), ())), preferred_element_type=f32
        )
        spread = column(run_ref[...], head) - rows_ref[pl.ds(head, 1), :]
        factor = jnp.exp(jnp.where(triangle(), spread, -jnp.inf))
        weights = (scores * factor).astype(bf16)
        local = jnp.dot(weights, value_ref[...], preferred_element_type=f32)
        before = jnp.dot(query, get_slices(state_ref, 0), preferred_element_type=f32)
        out_ref[...] = local + before * column(reach_ref[...], head)


def prefix_kernel(in_ref, out_ref, state_ref):
    @pl.when(pl.program_id(0) == 0)
    def _():
        state_ref[...] = jnp.zeros_like(state_ref)

    state = state_ref[...]
    for b in range(BLOCKS_PER_STEP):
        parts = in_ref[b, SLICE:SENT, :].astype(f32)
        damping = parts[0:1] + parts[1:2] + parts[2:3]
        out_ref[b] = state.astype(bf16)
        state = damping * state + in_ref[b, :SLICE, :].astype(f32)
    state_ref[...] = state


def finish_kernel(group_ref, query_ref, start_ref, within_ref, gate_ref, reach_ref, *rest):
    out_ref = rest[-1]
    for n in range(PER_STEP):
        head = group_ref[0] * HALF + pl.program_id(0) * PER_STEP + n
        wide = slice(n * DV, (n + 1) * DV)
        across = jnp.dot(
            query_ref[:, n * DK : (n + 1) * DK], get_slices(start_ref, n),
            preferred_element_type=f32,
        )
        retained = within_ref[:, wide] + across * column(reach_ref[...], head)
        average = jnp.mean(retained, axis=1, keepdims=True)
        centered = retained - average
        variance = jnp.mean(centered * centered, axis=1, keepdims=True)
        normed = centered * lax.rsqrt(variance + 1e-06)
        gate = gate_ref[:, wide].astype(f32)
        out_ref[:, wide] = (gate / (1.0 + jnp.exp(-gate)) * normed).astype(bf16)


def call(kernel, name, grid, in_specs, out_specs, out_shape, scratch, flops, aliases=None):
    return pl.pallas_call(
        kernel,
        out_shape=out_shape,
        grid_spec=pltpu.PrefetchScalarGridSpec(
            num_scalar_prefetch=1,
            grid=(grid,),
            in_specs=in_specs,
            out_specs=out_specs,
            scratch_shapes=scratch,
        ),
        compiler_params=pltpu.CompilerParams(dimension_semantics=("arbitrary",)),
        cost_estimate=pl.CostEstimate(flops=flops, transcendentals=0, bytes_accessed=0),
        input_output_aliases=aliases or {},
        name=name,
    )


def shape(*dims, dtype=bf16):
    return jax.ShapeDtypeStruct(dims, dtype)


def shards(queries, key_vectors, values, decay_log, gate_input):
    core = lax.axis_index("core").astype(jnp.int32).reshape(1)
    other = 1 - core
    swap = [(0, 1), (1, 0)]
    everyone = ("seq", "chip")
    decay = decay_log.T
    other_decay = lax.ppermute(decay, "core", swap)

    steps = HALF // PER_STEP
    whole = lambda *dims: pl.BlockSpec(dims, lambda i, c: (0,) * len(dims))
    heads = lambda width, n=PER_STEP: pl.BlockSpec(
        (ROWS, width * n), lambda i, c: (0, c[0] * (HALF // n) + i)
    )
    theirs = lambda width: pl.BlockSpec((ROWS, width), lambda i, c: (0, (1 - c[0]) * HALF + i))
    half = lambda width, n=PER_STEP: pl.BlockSpec((ROWS, width * n), lambda i, c: (0, i))
    pieces = lambda n=PER_STEP: pl.BlockSpec((SLICES * n, SLICE, 128), lambda i, c: (i, 0, 0))
    sent = pl.BlockSpec((SLICES * PER_STEP, SENT, 128), lambda i, c: (i, 0, 0))
    decays = whole(HEADS, ROWS)
    table = pltpu.VMEM((ROWS, HEADS), f32)
    flops = 2 * HALF * ROWS * DK * DV

    def chunk_states(group, name):
        return call(
            state_kernel, name, steps, [heads(DK), heads(DV), decays], pieces(),
            shape(CHIPS, SLICE, 128), [table], flops,
        )(group, key_vectors, values, decay)

    theirs_state = chunk_states(other, "theirs_state")
    got = lax.ppermute(theirs_state, "core", swap)
    own_state = chunk_states(core, "own_state")
    block_state = call(
        combine_kernel, "combine", steps, [pieces(), pieces(), decays, decays], sent,
        shape(CHIPS, SENT, 128), [pltpu.VMEM((3, HEADS, 128), f32)], flops // 8,
    )(core, own_state, got, decay, other_decay)
    block_state, late_decay, late_state = lax.optimization_barrier((block_state, decay, own_state))
    collected = lax.all_to_all(block_state, everyone, 0, 0, tiled=True)
    their_first = lax.ppermute(late_state, "core", swap)

    own_within, their_within, reach = call(
        within_kernel, "within", HALF,
        [heads(DK, 1), heads(DK, 1), heads(DV, 1), pieces(1),
         theirs(DK), theirs(DK), theirs(DV), pieces(1), decays, decays],
        [half(DV, 1), half(DV, 1), whole(ROWS, HEADS)],
        [shape(ROWS, HALF * DV, dtype=f32)] * 2 + [shape(ROWS, HEADS, dtype=f32)],
        [table, pltpu.VMEM((HEADS, ROWS), f32), table], 4 * flops,
    )(core, queries, key_vectors, values, got, queries, key_vectors, values, their_first,
      late_decay, other_decay)
    collected, own_within = lax.optimization_barrier((collected, own_within))

    starts = pl.pallas_call(
        prefix_kernel,
        out_shape=shape(CHIPS, SLICE, 128),
        grid=(CHIPS // BLOCKS_PER_STEP,),
        in_specs=[pl.BlockSpec((BLOCKS_PER_STEP, SENT, 128), lambda i: (i, 0, 0))],
        out_specs=pl.BlockSpec((BLOCKS_PER_STEP, SLICE, 128), lambda i: (i, 0, 0)),
        scratch_shapes=[pltpu.VMEM((SLICE, 128), f32)],
        compiler_params=pltpu.CompilerParams(dimension_semantics=("arbitrary",)),
        name="prefix",
    )(collected)
    start = lax.all_to_all(starts, everyone, 0, 0, tiled=True)
    their_start = lax.ppermute(start, "core", swap)

    specs = [heads(DK), pieces(), half(DV), heads(DV), whole(ROWS, HEADS)]
    result = shape(ROWS, HEADS * DV)
    done = call(finish_kernel, "finish_own", steps, specs, heads(DV), result, [], flops)(
        core, queries, start, own_within, gate_input, reach
    )
    return call(
        finish_kernel, "finish_theirs", steps, specs + [pl.BlockSpec(memory_space=pl.ANY)],
        heads(DV), result, [], flops, {6: 0},
    )(other, queries, their_start, their_within, gate_input, reach, done)


def solution(mesh):
    mesh = Mesh(mesh.devices.reshape(4, 16, 2), ("seq", "chip", "core"))
    spec = P(("seq", "chip", "core"), None)
    return jax.shard_map(
        shards, mesh=mesh, in_specs=(spec,) * 5, out_specs=spec, check_vma=False
    )
```

time: 152 us -> 112 us (0.74)
  blocking collectives: 73.9 us -> 34.1 us
  Pallas kernels: 61.6 us -> 39.4 us
  waiting for transfers between devices: 4.01 us -> 17.9 us
  starting transfers between devices: 6 us -> 16.5 us
    all_to_all x1 -> x0, blocking collectives: 42.1 us -> none  [shards(): collected = lax.all_to_all(block_state, everyone, 0, 0, tiled=True)]
    pallas_call x6, Pallas kernels: 55.8 us -> 36.5 us  [the longest x1 11.7 us: shards(): call(within_kernel, 'within', HALF, [heads(DK, 1), heads(DK, 1), heads(DV...]
    all_to_all x0 -> x1, waiting for transfers between devices: none -> 17.9 us  [shards(): collected = lax.all_to_all(block_state, everyone, 0, 0, tiled=True)]
    all_to_all x0 -> x1, starting transfers between devices: none -> 11.3 us  [shards(): collected = lax.all_to_all(block_state, everyone, 0, 0, tiled=True)]
    ppermute x2 -> x3, waiting for transfers between devices: 4.01 us -> 0.01 us  [the longest x1 0.01 us: shards(): other_decay = lax.ppermute(decay, 'core', swap)]
    pallas_call x1, Pallas kernels: 5.84 us -> 2.88 us  [shards(): pl.pallas_call(prefix_kernel, out_shape=shape(CHIPS, SLICE, 128), grid=(C...]
    all_to_all x1, blocking collectives: 31.8 us -> 34.1 us  [shards(): start = lax.all_to_all(starts, everyone, 0, 0, tiled=True)]
    unnamed x9 -> x10, local copies, waits for them, and re-layouts: 4.75 us -> 3.32 us
  transfers between devices with their start and end apart: 3 -> 5, of which waited for: 1 -> 1; matrix products, arithmetic and copies ran while one was open for 0% -> 0% of each run, Pallas kernels for 16% -> 20%
where the time goes in v2:
time: 112 us; the launch traced here: 111 us
  Pallas kernels  39.4 us (35%)
  blocking collectives  34.1 us (30%)
  waiting for transfers between devices  17.9 us (16%)
  starting transfers between devices  16.5 us (15%)
  local copies, waits for them, and re-layouts  3.32 us (3%)
    all_to_all x1, blocking collectives, shards(): start = lax.all_to_all(starts, everyone, 0, 0, tiled=True)  34.1 us
    all_to_all x1, waiting for transfers between devices, shards(): collected = lax.all_to_all(block_state, everyone, 0, 0, tiled=True)  17.9 us
    pallas_call x1, Pallas kernels, shards(): call(within_kernel, 'within', HALF, [heads(DK, 1), heads(DK, 1), heads(DV...  11.7 us
    all_to_all x1, starting transfers between devices, shards(): collected = lax.all_to_all(block_state, everyone, 0, 0, tiled=True)  11.3 us
    pallas_call x2, Pallas kernels, chunk_states(): call(state_kernel, name, steps, [heads(DK), heads(DV), decays], pieces(),...  8.18 us
    pallas_call x1, Pallas kernels, shards(): call(finish_kernel, 'finish_theirs', steps, specs + [pl.BlockSpec(memory_...  6.49 us
    pallas_call x1, Pallas kernels, shards(): call(finish_kernel, 'finish_own', steps, specs, heads(DV), result, [], fl...  6.48 us
    pallas_call x1, Pallas kernels, shards(): call(combine_kernel, 'combine', steps, [pieces(), pieces(), decays, decay...  3.59 us
  transfers between devices with their start and end apart: 5, of which 1 were waited for; matrix products, arithmetic and copies ran while one was open for 0% of the time, Pallas kernels for 20%

profile of v2, /device:TPU:1, one launch (start us, length us, event | category | flops | bytes accessed | tf_op | source)
XLA Modules:
  0.0 111.3 jit_solution(18058954713247781456)
XLA Ops:
  0.0 0.0 copy-start.3
  0.0 4.2 %theirs_state.1 = bf16[64,128,128]{2,1,0:T(8,128)(2,1)} custom-call(s32[1]{0:T(128)S(6)} %sub.3.group_ref, bf16[256,4096]{1,0:T(8,128)(2,1)} %refs_5_.1, bf16[256,8192]{1,0:T(8,128)(2,1)} %refs_6_.1, bf16[16,256]{1,0:T(8,128)(2,1)} %bitcast.2), custom_call_target="tpu_custom_call" | custom-call | flops 536870912 | tf_op jit(solution)/shard_map/theirs_state/pallas_call | solution.py:223
  4.2 1.3 %collective-permute-start = (bf16[64,128,128]{2,1,0:T(8,128)(2,1)}, bf16[64,128,128]{2,1,0:T(8,128)(2,1)S(1)}, u32[]{:S(2)}, u32[]{:S(2)}) collective-permute-start(bf16[64,128,128]{2,1,0:T(8,128)(2,1)} %theirs_state.1), channel_id=1, source_target_pairs={{0,1},{1,0},{2,3},{3,2},{4,5},{5,4},{6,7},{7,6},{8,9},{9,8},{10,11... | collective-permute-start | bytes 6291464 | tf_op jit(solution)/shard_map/ppermute | solution.py:229
  5.6 0.0 copy-done.3
  5.6 0.1 collective-permute-start.1
  5.6 4.0 %own_state.1.own_ref = bf16[64,128,128]{2,1,0:T(8,128)(2,1)} custom-call(s32[1]{0:T(128)} %bitcast.group_ref.core_ref, bf16[256,4096]{1,0:T(8,128)(2,1)} %refs_5_.1, bf16[256,8192]{1,0:T(8,128)(2,1)} %refs_6_.1, bf16[16,256]{1,0:T(8,128)(2,1)} %bitcast.3), custom_call_target="tpu_custom_call" | custom-call | flops 536870912 | tf_op jit(solution)/shard_map/own_state/pallas_call | solution.py:223
  9.6 0.0 collective-permute-done.1.other_ref.refs_9_
  9.6 0.0 copy-start.4
  9.6 0.0 collective-permute-done.got_ref.refs_3_
  9.6 0.6 copy-done.4
  10.2 0.0 copy-start.2
  10.2 1.4 %copy-done.2 = bf16[64,128,128]{2,1,0:T(8,128)(2,1)} copy-done((bf16[64,128,128]{2,1,0:T(8,128)(2,1)}, bf16[64,128,128]{2,1,0:T(8,128)(2,1)S(1)}, u32[]{:S(2)}) %copy-start.2) | copy-done | bytes 2097176
  11.6 3.6 %combine.1 = bf16[64,136,128]{2,1,0:T(8,128)(2,1)} custom-call(s32[1]{0:T(128)} %bitcast.group_ref.core_ref, bf16[64,128,128]{2,1,0:T(8,128)(2,1)} %own_state.1.own_ref, bf16[64,128,128]{2,1,0:T(8,128)(2,1)} %copy-done.2, bf16[16,256]{1,0:T(8,128)(2,1)} %bitcast.4, bf16[16,256]{1,0:T(8,128)(2,1)} %copy-done.4), custom_call_target="tpu_custom_call" | custom-call | flops 67108864 | tf_op jit(solution)/shard_map/combine/pallas_call | solution.py:231
  15.2 0.4 collective-permute-start.2
  15.6 11.3 %all-to-all-start = ((bf16[64,136,128]{2,1,0:T(8,128)(2,1)}), bf16[64,136,128]{2,1,0:T(8,128)(2,1)S(1)}, u32[]{:S(2)}, u32[]{:S(2)}) async-start(bf16[64,136,128]{2,1,0:T(8,128)(2,1)} %combine.1), calls=%async_computation | async-start | bytes 4456448 | tf_op jit(solution)/shard_map/all_to_all | solution.py:236
  26.9 0.0 collective-permute-done.2.refs_7_
  26.9 11.7 %within.1 = (f32[256,4096]{1,0:T(8,128)}, f32[256,4096]{1,0:T(8,128)}, f32[256,16]{1,0:T(8,128)}) custom-call(s32[1]{0:T(128)} %bitcast.group_ref.core_ref, bf16[256,4096]{1,0:T(8,128)(2,1)} %query_ref.3, bf16[256,4096]{1,0:T(8,128)(2,1)} %refs_5_.1, bf16[256,8192]{1,0:T(8,128)(2,1)} %refs_6_.1, bf16[64,128,128]{2,1,0:T(8,128)(2,1)} %copy-done.2, ...), custom_call_target="tpu_custom_call" | custom-call | flops 2147483648 | tf_op jit(solution)/shard_map/within/pallas_call | solution.py:239
  38.6 17.9 %all-to-all-done.in_ref = bf16[64,136,128]{2,1,0:T(8,128)(2,1)S(1)} async-done(((bf16[64,136,128]{2,1,0:T(8,128)(2,1)}), bf16[64,136,128]{2,1,0:T(8,128)(2,1)S(1)}, u32[]{:S(2)}, u32[]{:S(2)}) %all-to-all-start) | async-done | bytes 2228256 | tf_op jit(solution)/shard_map/all_to_all | solution.py:236
  56.5 0.0 copy-start
  56.5 1.4 %copy-done = bf16[64,136,128]{2,1,0:T(8,128)(2,1)} copy-done((bf16[64,136,128]{2,1,0:T(8,128)(2,1)}, bf16[64,136,128]{2,1,0:T(8,128)(2,1)S(1)}, u32[]{:S(2)}) %copy-start) | copy-done | bytes 2228248
  57.9 2.9 %prefix.1 = bf16[64,128,128]{2,1,0:T(8,128)(2,1)} custom-call(bf16[64,136,128]{2,1,0:T(8,128)(2,1)} %copy-done), custom_call_target="tpu_custom_call" | custom-call | tf_op jit(solution)/shard_map/prefix/pallas_call | solution.py:250
  60.8 34.1 %all_to_all.10.start_ref = bf16[64,128,128]{2,1,0:T(8,128)(2,1)S(1)} all-to-all(bf16[64,128,128]{2,1,0:T(8,128)(2,1)} %prefix.1), channel_id=1, replica_groups=mesh['seq'=4,'chip'=16,'core'=2] {'seq','chip'}, dimensions={0} | all-to-all | bytes 4194304 | tf_op jit(solution)/shard_map/all_to_all | solution.py:260
  94.9 0.0 copy-start.1
  94.9 3.4 %collective-permute-start.3 = (bf16[64,128,128]{2,1,0:T(8,128)(2,1)S(1)}, bf16[64,128,128]{2,1,0:T(8,128)(2,1)}, u32[]{:S(2)}, u32[]{:S(2)}) collective-permute-start(bf16[64,128,128]{2,1,0:T(8,128)(2,1)S(1)} %all_to_all.10.start_ref), channel_id=1, source_target_pairs={{0,1},{1,0},{2,3},{3,2},{4,5},{5,4},{6,7},{7,6},{8,9},{9,8},{10,11... | collective-permute-start | bytes 6291464 | tf_op jit(solution)/shard_map/ppermute | solution.py:261
  98.3 0.0 copy-done.1
  98.3 6.5 %finish_own.1.rest_0_ = bf16[256,8192]{1,0:T(8,128)(2,1)} custom-call(s32[1]{0:T(128)} %bitcast.group_ref.core_ref, bf16[256,4096]{1,0:T(8,128)(2,1)} %query_ref.3, bf16[64,128,128]{2,1,0:T(8,128)(2,1)} %copy-done.1, f32[256,4096]{1,0:T(8,128)} %get-tuple-element.20.within_ref, bf16[256,8192]{1,0:T(8,128)(2,1)} %gate_ref.3, ...), custom_call_target="tpu_custom_call" | custom-call | flops 536870912 | tf_op jit(solution)/shard_map/finish_own/pallas_call | solution.py:265
  104.8 0.0 collective-permute-done.3.start_ref
  104.8 6.5 %finish_theirs.1 = bf16[256,8192]{1,0:T(8,128)(2,1)} custom-call(s32[1]{0:T(128)S(6)} %sub.3.group_ref, bf16[256,4096]{1,0:T(8,128)(2,1)} %query_ref.3, bf16[64,128,128]{2,1,0:T(8,128)(2,1)} %collective-permute-done.3.start_ref, f32[256,4096]{1,0:T(8,128)} %get-tuple-element.18.within_ref, ...), custom_call_target="tpu_custom_call", output_to_operand_aliasing={{}: (6, {})} | custom-call | flops 536870912 | tf_op jit(solution)/shard_map/finish_theirs/pallas_call | solution.py:268
Async XLA Ops:
  0.0 5.6 %copy-start.3 = (bf16[256,16]{0,1:T(8,128)(2,1)S(1)}, bf16[256,16]{0,1:T(8,128)(2,1)}, u32[]{:S(2)}) copy-start(bf16[256,16]{0,1:T(8,128)(2,1)} %param.8) | copy-start | bytes 24580
  4.2 5.4 %collective-permute-start = (bf16[64,128,128]{2,1,0:T(8,128)(2,1)}, bf16[64,128,128]{2,1,0:T(8,128)(2,1)S(1)}, u32[]{:S(2)}, u32[]{:S(2)}) collective-permute-start(bf16[64,128,128]{2,1,0:T(8,128)(2,1)} %theirs_state.1), channel_id=1, source_target_pairs={{0,1},{1,0},{2,3},{3,2},{4,5},{5,4},{6,7},{7,6},{8,9},{9,8},{10,11... | collective-permute-start | bytes 6291464 | tf_op jit(solution)/shard_map/ppermute | solution.py:229
  5.6 4.1 %collective-permute-start.1 = (bf16[16,256]{1,0:T(8,128)(2,1)S(1)}, bf16[16,256]{1,0:T(8,128)(2,1)S(1)}, u32[]{:S(2)}, u32[]{:S(2)}) collective-permute-start(bf16[16,256]{1,0:T(8,128)(2,1)S(1)} %bitcast.6), channel_id=1, source_target_pairs={{0,1},{1,0},{2,3},{3,2},{4,5},{5,4},{6,7},{7,6},{8,9},{9,8},{10,11... | collective-permute-start | bytes 24584 | tf_op jit(solution)/shard_map/ppermute | solution.py:207
  9.6 0.6 copy-start.4
  10.2 1.4 %copy-start.2 = (bf16[64,128,128]{2,1,0:T(8,128)(2,1)}, bf16[64,128,128]{2,1,0:T(8,128)(2,1)S(1)}, u32[]{:S(2)}) copy-start(bf16[64,128,128]{2,1,0:T(8,128)(2,1)S(1)} %collective-permute-done.got_ref.refs_3_) | copy-start | bytes 6291460
  15.2 11.7 %collective-permute-start.2 = (bf16[64,128,128]{2,1,0:T(8,128)(2,1)}, bf16[64,128,128]{2,1,0:T(8,128)(2,1)}, u32[]{:S(2)}, u32[]{:S(2)}) collective-permute-start(bf16[64,128,128]{2,1,0:T(8,128)(2,1)} %own_state.1.own_ref), channel_id=1, source_target_pairs={{0,1},{1,0},{2,3},{3,2},{4,5},{5,4},{6,7},{7,6},{8,9},{9,8},{10,11... | collective-permute-start | bytes 6291464 | tf_op jit(solution)/shard_map/ppermute | solution.py:237
  15.6 40.9 %all-to-all-start = ((bf16[64,136,128]{2,1,0:T(8,128)(2,1)}), bf16[64,136,128]{2,1,0:T(8,128)(2,1)S(1)}, u32[]{:S(2)}, u32[]{:S(2)}) async-start(bf16[64,136,128]{2,1,0:T(8,128)(2,1)} %combine.1), calls=%async_computation | async-start | bytes 4456448 | tf_op jit(solution)/shard_map/all_to_all | solution.py:236
  56.5 1.4 %copy-start = (bf16[64,136,128]{2,1,0:T(8,128)(2,1)}, bf16[64,136,128]{2,1,0:T(8,128)(2,1)S(1)}, u32[]{:S(2)}) copy-start(bf16[64,136,128]{2,1,0:T(8,128)(2,1)S(1)} %all-to-all-done.in_ref) | copy-start | bytes 6684676
  94.9 3.4 %copy-start.1 = (bf16[64,128,128]{2,1,0:T(8,128)(2,1)}, bf16[64,128,128]{2,1,0:T(8,128)(2,1)S(1)}, u32[]{:S(2)}) copy-start(bf16[64,128,128]{2,1,0:T(8,128)(2,1)S(1)} %all_to_all.10.start_ref) | copy-start | bytes 6291460
  94.9 9.9 %collective-permute-start.3 = (bf16[64,128,128]{2,1,0:T(8,128)(2,1)S(1)}, bf16[64,128,128]{2,1,0:T(8,128)(2,1)}, u32[]{:S(2)}, u32[]{:S(2)}) collective-permute-start(bf16[64,128,128]{2,1,0:T(8,128)(2,1)S(1)} %all_to_all.10.start_ref), channel_id=1, source_target_pairs={{0,1},{1,0},{2,3},{3,2},{4,5},{5,4},{6,7},{7,6},{8,9},{9,8},{10,11... | collective-permute-start | bytes 6291464 | tf_op jit(solution)/shard_map/ppermute | solution.py:261

commit v3 on v2

v3 whole, which is shorter than its diff:
```python
import jax
import jax.numpy as jnp
from jax import lax
from jax.experimental import pallas as pl
from jax.experimental.pallas import tpu as pltpu
from jax.sharding import Mesh, PartitionSpec as P

HEADS = 16
DK = 256
DV = 512
ROWS = 256
HALF = HEADS // 2
LINE = 4
GROUPS = 2
GROUP = HALF // GROUPS
PIECE = DK // LINE
TILES = DV // 128
SLICE = PIECE * TILES
SENT = SLICE + 8
STATE = LINE * SLICE
PER_STEP = 2

f32 = jnp.float32
bf16 = jnp.bfloat16


def triangle():
    rows = lax.broadcasted_iota(jnp.int32, (ROWS, ROWS), 0)
    cols = lax.broadcasted_iota(jnp.int32, (ROWS, ROWS), 1)
    return rows >= cols


def running_of(decay):
    ones = triangle().astype(f32).astype(bf16)
    return lax.dot_general(ones, decay, (((1,), (1,)), ((), ())), preferred_element_type=f32)


def running_rows(decay):
    ones = triangle().astype(f32).astype(bf16)
    return lax.dot_general(decay, ones, (((1,), (1,)), ((), ())), preferred_element_type=f32)


def column(table, head):
    lanes = lax.broadcasted_iota(jnp.int32, table.shape, 1)
    return jnp.sum(jnp.where(lanes == head, table, 0.0), axis=1, keepdims=True)


def put_slices(ref, at, state):
    for o in range(LINE):
        for t in range(TILES):
            ref[at * LINE + o, t * PIECE : (t + 1) * PIECE, :] = state[
                o * PIECE : (o + 1) * PIECE, t * 128 : (t + 1) * 128
            ]


def get_slices(ref, at):
    cols = [
        ref[at * LINE : (at + 1) * LINE, t * PIECE : (t + 1) * PIECE, :].reshape(DK, 128)
        for t in range(TILES)
    ]
    return jnp.concatenate(cols, axis=1)


def state_kernel(group_ref, key_ref, value_ref, decay_ref, out_ref, fade_ref):
    step = pl.program_id(0)

    @pl.when(step == 0)
    def _():
        run = running_of(decay_ref[...])
        fade_ref[...] = jnp.exp(run[ROWS - 1 : ROWS, :] - run)

    for n in range(PER_STEP):
        fade = column(fade_ref[...], group_ref[0] + step * PER_STEP + n)
        faded = (key_ref[:, n * DK : (n + 1) * DK].astype(f32) * fade).astype(bf16)
        state = lax.dot_general(
            faded, value_ref[:, n * DV : (n + 1) * DV], (((0,), (0,)), ((), ())),
            preferred_element_type=f32,
        )
        put_slices(out_ref, n, state.astype(bf16))


def split_rows(damping):
    rows = lax.broadcasted_iota(jnp.int32, (8, 128), 0)
    high = damping.astype(bf16).astype(f32)
    rest = damping - high
    middle = rest.astype(bf16).astype(f32)
    parts = jnp.where(rows == 0, high, jnp.where(rows == 1, middle, rest - middle))
    return parts.astype(bf16)


def joined_row(rows):
    parts = rows.astype(f32)
    return parts[0:1] + parts[1:2] + parts[2:3]


def combine_kernel(group_ref, own_ref, got_ref, decay_ref, other_ref, out_ref, rate_ref):
    step = pl.program_id(0)
    is_first = group_ref[0] < HALF

    @pl.when(step == 0)
    def _():
        ones = jnp.ones((128, ROWS), f32).astype(bf16)
        total = lax.dot_general(
            decay_ref[...], ones, (((1,), (1,)), ((), ())), preferred_element_type=f32
        )
        other = lax.dot_general(
            other_ref[...], ones, (((1,), (1,)), ((), ())), preferred_element_type=f32
        )
        rate_ref[0] = jnp.exp(jnp.where(is_first, other, 0.0))
        rate_ref[1] = jnp.exp(jnp.where(is_first, 0.0, total))
        rate_ref[2] = jnp.exp(total + other)

    for n in range(PER_STEP):
        head = pl.ds(group_ref[0] + step * PER_STEP + n, 1)
        own_rate = rate_ref[0, head, :]
        got_rate = rate_ref[1, head, :]
        for s in range(LINE):
            at = n * LINE + s
            both = own_ref[at].astype(f32) * own_rate + got_ref[at].astype(f32) * got_rate
            out_ref[n, s * SLICE : (s + 1) * SLICE, :] = both.astype(bf16)
        out_ref[n, STATE:, :] = split_rows(rate_ref[2, head, :])


def line_kernel(y_ref, in_ref, *refs):
    outs, total_ref = refs[:LINE], refs[LINE]
    damping = [joined_row(in_ref[z, STATE:, :]) for z in range(LINE)]
    for s in range(LINE):
        rows = slice(s * SLICE, (s + 1) * SLICE)
        state = in_ref[0, rows, :].astype(f32)
        for z in range(1, LINE):
            state = damping[z] * state + in_ref[z, rows, :].astype(f32)
        total_ref[s] = state
    parts = split_rows(damping[0] * damping[1] * damping[2] * damping[3])
    for d in range(LINE):
        outs[d][:SLICE, :] = total_ref[(y_ref[0] + d) % LINE].astype(bf16)
        outs[d][SLICE:, :] = parts


def plane_kernel(y_ref, *refs):
    ins, out_ref, lines_ref = refs[:LINE], refs[LINE], refs[LINE + 1]
    for d in range(LINE):
        lines_ref[(y_ref[0] - d) % LINE] = ins[d][...].astype(f32)
    state = jnp.zeros((SLICE, 128), f32)
    damping = jnp.ones((1, 128), f32)
    for y in range(LINE):
        rate = joined_row(lines_ref[y, SLICE:, :])
        state = rate * state + lines_ref[y, :SLICE, :]
        damping = damping * rate
    out_ref[:SLICE, :] = state.astype(bf16)
    out_ref[SLICE:, :] = split_rows(damping)


def carry_kernel(y_ref, *refs):
    ins, planes, outs = refs[:LINE], refs[LINE : 2 * LINE - 1], refs[2 * LINE - 1 : 3 * LINE - 1]
    lines_ref, carry_ref = refs[3 * LINE - 1 :]
    for d in range(LINE):
        lines_ref[(y_ref[0] - d) % LINE] = ins[d][...].astype(f32)
    state = jnp.zeros((SLICE, 128), f32)
    for plane in reversed(planes):
        state = joined_row(plane[SLICE:, :]) * state + plane[:SLICE, :].astype(f32)
    for y in range(LINE):
        carry_ref[y] = state
        state = joined_row(lines_ref[y, SLICE:, :]) * state + lines_ref[y, :SLICE, :]
    for d in range(LINE):
        outs[d][...] = carry_ref[(y_ref[0] + d) % LINE].astype(bf16)


def start_kernel(y_ref, in_ref, *refs):
    carries, out_ref, carry_ref = refs[:LINE], refs[LINE], refs[LINE + 1]
    for d in range(LINE):
        carry_ref[(y_ref[0] - d) % LINE] = carries[d][...].astype(f32)
    for s in range(LINE):
        rows = slice(s * SLICE, (s + 1) * SLICE)
        state = carry_ref[s]
        for z in range(LINE):
            out_ref[z, rows, :] = state.astype(bf16)
            if z + 1 < LINE:
                state = joined_row(in_ref[z, STATE:, :]) * state + in_ref[z, rows, :].astype(f32)


def within_kernel(group_ref, *refs):
    own, theirs = refs[0:4], refs[4:8]
    decay_ref, other_ref, own_out, theirs_out, reach_out, run_ref, rows_ref, reach_ref = refs[8:]
    step = pl.program_id(0)
    first = group_ref[0]

    @pl.when(step == 0)
    def _():
        run = running_of(decay_ref[...])
        run_ref[...] = run
        rows_ref[...] = running_rows(decay_ref[...])
        other = running_of(other_ref[...])[ROWS - 1 : ROWS, :]
        reach_out[...] = jnp.exp(run + jnp.where(first < HALF, 0.0, other))
        reach_ref[...] = jnp.where(first < HALF, 0.0, jnp.exp(run))

    far = jnp.where(first < HALF, first + HALF, first - HALF)
    for base, ins, out_ref in ((first, own, own_out), (far, theirs, theirs_out)):
        query_ref, key_ref, value_ref, state_ref = ins
        head = base + step
        query = query_ref[...]
        scores = lax.dot_general(
            query, key_ref[...], (((1,), (1,)), ((), ())), preferred_element_type=f32
        )
        spread = column(run_ref[...], head) - rows_ref[pl.ds(head, 1), :]
        factor = jnp.exp(jnp.where(triangle(), spread, -jnp.inf))
        weights = (scores * factor).astype(bf16)
        local = jnp.dot(weights, value_ref[...], preferred_element_type=f32)
        before = jnp.dot(query, get_slices(state_ref, 0), preferred_element_type=f32)
        out_ref[...] = local + before * column(reach_ref[...], head)


def finish_kernel(group_ref, query_ref, start_ref, within_ref, gate_ref, reach_ref, *rest):
    out_ref = rest[-1]
    for n in range(PER_STEP):
        head = group_ref[0] + pl.program_id(0) * PER_STEP + n
        wide = slice(n * DV, (n + 1) * DV)
        across = jnp.dot(
            query_ref[:, n * DK : (n + 1) * DK], get_slices(start_ref, n),
            preferred_element_type=f32,
        )
        retained = within_ref[:, wide] + across * column(reach_ref[...], head)
        average = jnp.mean(retained, axis=1, keepdims=True)
        centered = retained - average
        variance = jnp.mean(centered * centered, axis=1, keepdims=True)
        normed = centered * lax.rsqrt(variance + 1e-06)
        gate = gate_ref[:, wide].astype(f32)
        out_ref[:, wide] = (gate / (1.0 + jnp.exp(-gate)) * normed).astype(bf16)


def call(kernel, name, grid, in_specs, out_specs, out_shape, scratch, flops, aliases=None):
    return pl.pallas_call(
        kernel,
        out_shape=out_shape,
        grid_spec=pltpu.PrefetchScalarGridSpec(
            num_scalar_prefetch=1,
            grid=(grid,),
            in_specs=in_specs,
            out_specs=out_specs,
            scratch_shapes=scratch,
        ),
        compiler_params=pltpu.CompilerParams(dimension_semantics=("arbitrary",)),
        cost_estimate=pl.CostEstimate(flops=flops, transcendentals=0, bytes_accessed=0),
        input_output_aliases=aliases or {},
        name=name,
    )


def shape(*dims, dtype=bf16):
    return jax.ShapeDtypeStruct(dims, dtype)


def exchange(arrays, axis, ring=True):
    done = []
    for d, array in enumerate(arrays, 1):
        pairs = [(i, (i + d) % LINE) for i in range(LINE) if ring or i + d < LINE]
        done.append(lax.ppermute(array, axis, pairs))
    return done


def shards(queries, key_vectors, values, decay_log, gate_input):
    core = lax.axis_index("core").astype(jnp.int32).reshape(1)
    place = lax.axis_index("y").astype(jnp.int32).reshape(1)
    swap = [(0, 1), (1, 0)]
    decay = decay_log.T
    other_decay = lax.ppermute(decay, "core", swap)

    steps = GROUP // PER_STEP
    whole = lambda *dims: pl.BlockSpec(dims, lambda i, c: (0,) * len(dims))
    heads = lambda width, n=PER_STEP: pl.BlockSpec(
        (ROWS, width * n), lambda i, c: (0, c[0] // n + i)
    )
    theirs = lambda width: pl.BlockSpec((ROWS, width), lambda i, c: (0, (c[0] + HALF) % HEADS + i))
    half = lambda width, n=PER_STEP: pl.BlockSpec((ROWS, width * n), lambda i, c: (0, i))
    pieces = lambda n=PER_STEP: pl.BlockSpec((LINE * n, SLICE, 128), lambda i, c: (i, 0, 0))
    decays = whole(HEADS, ROWS)
    table = pltpu.VMEM((ROWS, HEADS), f32)
    flops = 2 * GROUP * ROWS * DK * DV
    slices_shape = shape(GROUP * LINE, SLICE, 128)
    local = pl.BlockSpec(memory_space=pltpu.VMEM)

    def chunk_states(group, name):
        return call(
            state_kernel, name, steps, [heads(DK), heads(DV), decays], pieces(),
            slices_shape, [table], flops,
        )(group, key_vectors, values, decay)

    def within_of(g, their_first, late_decay):
        return call(
            within_kernel, f"within_{g}", GROUP,
            [heads(DK, 1), heads(DK, 1), heads(DV, 1), pieces(1),
             theirs(DK), theirs(DK), theirs(DV), pieces(1), decays, decays],
            [half(DV, 1), half(DV, 1), whole(ROWS, HEADS)],
            [shape(ROWS, GROUP * DV, dtype=f32)] * 2 + [shape(ROWS, HEADS, dtype=f32)],
            [table, pltpu.VMEM((HEADS, ROWS), f32), table], 4 * flops,
        )(own_heads[g], queries, key_vectors, values, got[g], queries, key_vectors, values,
          their_first, late_decay, other_decay)

    def starts_of(g):
        lines = call(
            line_kernel, f"line_{g}", 1, [whole(LINE, STATE + 8, 128)], [local] * LINE,
            [shape(SENT, 128)] * LINE, [pltpu.VMEM((LINE, SLICE, 128), f32)], flops // 16,
        )(place, collected[g])
        lines = [lines[0]] + exchange(lines[1:], "y")
        plane = call(
            plane_kernel, f"plane_{g}", 1, [local] * LINE, local,
            shape(SENT, 128), [pltpu.VMEM((LINE, SENT, 128), f32)], flops // 64,
        )(place, *lines)
        planes = exchange([plane] * (LINE - 1), "x", ring=False)
        carries = call(
            carry_kernel, f"carry_{g}", 1, [local] * (2 * LINE - 1), [local] * LINE,
            [shape(SLICE, 128)] * LINE,
            [pltpu.VMEM((LINE, SENT, 128), f32), pltpu.VMEM((LINE, SLICE, 128), f32)], flops // 64,
        )(place, *lines, *planes)
        carries = [carries[0]] + exchange(carries[1:], "y")
        return call(
            start_kernel, f"starts_{g}", 1, [whole(LINE, STATE + 8, 128)] + [local] * LINE,
            whole(LINE, STATE, 128), shape(LINE, STATE, 128),
            [pltpu.VMEM((LINE, SLICE, 128), f32)], flops // 16,
        )(place, collected[g], *carries)

    own_heads = [core * HALF + g * GROUP for g in range(GROUPS)]
    their_heads = [(1 - core) * HALF + g * GROUP for g in range(GROUPS)]
    collected, got, own_states = [], [], []
    for g in range(GROUPS):
        theirs_state = chunk_states(their_heads[g], f"theirs_state_{g}")
        got.append(lax.ppermute(theirs_state, "core", swap))
        own_states.append(chunk_states(own_heads[g], f"own_state_{g}"))
        block_state = call(
            combine_kernel, f"combine_{g}", steps, [pieces(), pieces(), decays, decays],
            pl.BlockSpec((PER_STEP, STATE + 8, 128), lambda i, c: (i, 0, 0)),
            shape(LINE, STATE + 8, 128), [pltpu.VMEM((3, HEADS, 128), f32)], flops // 8,
        )(own_heads[g], own_states[g], got[g], decay, other_decay)
        collected.append(lax.all_to_all(block_state, "z", 0, 0, tiled=True))

    within = [within_of(g, lax.ppermute(own_states[g], "core", swap), decay) for g in range(GROUPS)]
    start = [
        lax.all_to_all(starts_of(g), "z", 0, 0, tiled=True).reshape(GROUP * LINE, SLICE, 128)
        for g in range(GROUPS)
    ]
    specs = [heads(DK), pieces(), half(DV), heads(DV), whole(ROWS, HEADS)]
    result = shape(ROWS, HEADS * DV)
    done = None
    for g in range(GROUPS):
        their_start = lax.ppermute(start[g], "core", swap)
        for n, (group, states) in enumerate(((own_heads[g], start[g]), (their_heads[g], their_start))):
            more = [] if done is None else [done]
            done = call(
                finish_kernel, f"finish_{g}_{n}", steps,
                specs + [pl.BlockSpec(memory_space=pl.ANY)] * len(more),
                heads(DV), result, [], flops, {6: 0} if more else None,
            )(group, queries, states, within[g][n], gate_input, within[g][2], *more)
    return done


def solution(mesh):
    mesh = Mesh(mesh.devices.reshape(4, 4, 4, 2), ("x", "y", "z", "core"))
    spec = P(("x", "y", "z", "core"), None)
    return jax.shard_map(
        shards, mesh=mesh, in_specs=(spec,) * 5, out_specs=spec, check_vma=False
    )
```

time: 112 us -> 170 us (1.52)
  starting transfers between devices: 16.5 us -> 73.4 us
  blocking collectives: 34.1 us -> 0 us
  Pallas kernels: 39.4 us -> 64.3 us
  waiting for transfers between devices: 17.9 us -> 24.8 us
  local copies, waits for them, and re-layouts: 3.32 us -> 6.4 us
    ppermute x3 -> x24, starting transfers between devices: 5.18 us -> 55.6 us  [the longest x18 34.6 us: exchange(): done.append(lax.ppermute(array, axis, pairs))]
    all_to_all x1 -> x0, blocking collectives: 34.1 us -> none  [shards(): start = lax.all_to_all(starts, everyone, 0, 0, tiled=True)]
    pallas_call x5 -> x16, Pallas kernels: 31.2 us -> 51.9 us  [the longest x4 17 us: shards(): call(finish_kernel, f'finish_{g}_{n}', steps, specs + [pl.BlockSpec(memor...]
    ppermute x3 -> x24, waiting for transfers between devices: 0.01 us -> 16.1 us  [the longest x18 16.1 us: exchange(): done.append(lax.ppermute(array, axis, pairs))]
    all_to_all x1 -> x4, waiting for transfers between devices: 17.9 us -> 8.65 us  [the longest x2 8.28 us: shards(): collected.append(lax.all_to_all(block_state, 'z', 0, 0, tiled=True))]
    all_to_all x1 -> x4, starting transfers between devices: 11.3 us -> 17.3 us  [the longest x2 8.66 us: shards(): collected.append(lax.all_to_all(block_state, 'z', 0, 0, tiled=True))]
    pallas_call x2 -> x4, Pallas kernels: 8.18 us -> 12.4 us  [chunk_states(): call(state_kernel, name, steps, [heads(DK), heads(DV), decays], pieces(),...]
    unnamed x10 -> x54, local copies, waits for them, and re-layouts: 3.32 us -> 6.4 us
  transfers between devices with their start and end apart: 5 -> 29, of which waited for: 1 -> 16; matrix products, arithmetic and copies ran while one was open for 0% -> 0% of each run, Pallas kernels for 20% -> 34%
where the time goes in v3:
time: 170 us; the launch traced here: 169 us
  starting transfers between devices  73.4 us (43%)
  Pallas kernels  64.3 us (38%)
  waiting for transfers between devices  24.8 us (15%)
  local copies, waits for them, and re-layouts  6.4 us (4%)
    ppermute x18, starting transfers between devices, exchange(): done.append(lax.ppermute(array, axis, pairs))  34.6 us
    pallas_call x4, Pallas kernels, shards(): call(finish_kernel, f'finish_{g}_{n}', steps, specs + [pl.BlockSpec(memor...  17 us
    ppermute x18, waiting for transfers between devices, exchange(): done.append(lax.ppermute(array, axis, pairs))  16.1 us
    pallas_call x2, Pallas kernels, within_of(): call(within_kernel, f'within_{g}', GROUP, [heads(DK, 1), heads(DK, 1), he...  13 us
    pallas_call x4, Pallas kernels, chunk_states(): call(state_kernel, name, steps, [heads(DK), heads(DV), decays], pieces(),...  12.4 us
    ppermute x2, starting transfers between devices, shards(): their_start = lax.ppermute(start[g], 'core', swap)  10.5 us
    ppermute x2, starting transfers between devices, shards(): lax.ppermute(own_states[g], 'core', swap)  9 us
    all_to_all x2, starting transfers between devices, shards(): collected.append(lax.all_to_all(block_state, 'z', 0, 0, tiled=True))  8.66 us
  transfers between devices with their start and end apart: 29, of which 16 were waited for; matrix products, arithmetic and copies ran while one was open for 0% of the time, Pallas kernels for 34%

profile of v3, /device:TPU:1, one launch (start us, length us, event | category | flops | bytes accessed | tf_op | source)
XLA Modules:
  0.0 169.1 jit_solution(12266028595482187744)
XLA Ops:
  0.0 3.1 %theirs_state_0.1 = bf16[16,256,128]{2,1,0:T(8,128)(2,1)} custom-call(s32[1]{0:T(128)} %bitcast.group_ref, bf16[256,4096]{1,0:T(8,128)(2,1)} %refs_5_.3, bf16[256,8192]{1,0:T(8,128)(2,1)} %refs_6_.3, bf16[16,256]{1,0:T(8,128)(2,1)} %bitcast.8), custom_call_target="tpu_custom_call" | custom-call | flops 268435456 | tf_op jit(solution)/shard_map/theirs_state_0/pallas_call | solution.py:282
  3.1 1.4 collective-permute-start.13
  4.5 3.1 %theirs_state_1.1 = bf16[16,256,128]{2,1,0:T(8,128)(2,1)} custom-call(s32[1]{0:T(128)S(6)} %add.6.group_ref, bf16[256,4096]{1,0:T(8,128)(2,1)} %refs_5_.3, bf16[256,8192]{1,0:T(8,128)(2,1)} %refs_6_.3, bf16[16,256]{1,0:T(8,128)(2,1)} %bitcast.9), custom_call_target="tpu_custom_call" | custom-call | flops 268435456 | tf_op jit(solution)/shard_map/theirs_state_1/pallas_call | solution.py:282
  7.7 0.4 collective-permute-start.1
  8.1 3.1 %own_state_0.1.own_ref = bf16[16,256,128]{2,1,0:T(8,128)(2,1)} custom-call(s32[1]{0:T(128)} %bitcast.2.group_ref, bf16[256,4096]{1,0:T(8,128)(2,1)} %refs_5_.3, bf16[256,8192]{1,0:T(8,128)(2,1)} %refs_6_.3, bf16[16,256]{1,0:T(8,128)(2,1)} %bitcast.10), custom_call_target="tpu_custom_call" | custom-call | flops 268435456 | tf_op jit(solution)/shard_map/own_state_0/pallas_call | solution.py:282
  11.2 0.6 copy-done.14
  11.8 1.0 copy-done.3
  12.8 2.6 %combine_0.1 = bf16[4,1032,128]{2,1,0:T(8,128)(2,1)} custom-call(s32[1]{0:T(128)} %bitcast.2.group_ref, bf16[16,256,128]{2,1,0:T(8,128)(2,1)} %own_state_0.1.own_ref, bf16[16,256,128]{2,1,0:T(8,128)(2,1)} %copy-done.3, bf16[16,256]{1,0:T(8,128)(2,1)} %bitcast.11, bf16[16,256]{1,0:T(8,128)(2,1)} %copy-done.14), custom_call_target="tpu_custom_call" | custom-call | flops 33554432 | tf_op jit(solution)/shard_map/combine_0/pallas_call | solution.py:328
  15.4 5.1 %all-to-all-start.2 = ((bf16[4,1032,128]{2,1,0:T(8,128)(2,1)}), bf16[4,1032,128]{2,1,0:T(8,128)(2,1)S(1)}, u32[]{:S(2)}, u32[]{:S(2)}) async-start(bf16[4,1032,128]{2,1,0:T(8,128)(2,1)} %combine_0.1), calls=%async_computation.2 | async-start | bytes 2113536 | tf_op jit(solution)/shard_map/all_to_all | solution.py:333
  20.5 3.1 %own_state_1.1.own_ref = bf16[16,256,128]{2,1,0:T(8,128)(2,1)} custom-call(s32[1]{0:T(128)S(6)} %add.7.group_ref, bf16[256,4096]{1,0:T(8,128)(2,1)} %refs_5_.3, bf16[256,8192]{1,0:T(8,128)(2,1)} %refs_6_.3, bf16[16,256]{1,0:T(8,128)(2,1)} %bitcast.12), custom_call_target="tpu_custom_call" | custom-call | flops 268435456 | tf_op jit(solution)/shard_map/own_state_1/pallas_call | solution.py:282
  23.6 1.0 copy-done.2
  24.6 2.6 %combine_1.1 = bf16[4,1032,128]{2,1,0:T(8,128)(2,1)} custom-call(s32[1]{0:T(128)S(6)} %add.7.group_ref, bf16[16,256,128]{2,1,0:T(8,128)(2,1)} %own_state_1.1.own_ref, bf16[16,256,128]{2,1,0:T(8,128)(2,1)} %copy-done.2, bf16[16,256]{1,0:T(8,128)(2,1)} %bitcast.13, bf16[16,256]{1,0:T(8,128)(2,1)} %copy-done.14), custom_call_target="tpu_custom_call" | custom-call | flops 33554432 | tf_op jit(solution)/shard_map/combine_1/pallas_call | solution.py:328
  27.2 8.3 %all-to-all-done.2.in_ref = bf16[4,1032,128]{2,1,0:T(8,128)(2,1)S(1)} async-done(((bf16[4,1032,128]{2,1,0:T(8,128)(2,1)}), bf16[4,1032,128]{2,1,0:T(8,128)(2,1)S(1)}, u32[]{:S(2)}, u32[]{:S(2)}) %all-to-all-start.2) | async-done | bytes 1056800 | tf_op jit(solution)/shard_map/all_to_all | solution.py:333
  35.4 3.5 %all-to-all-start = ((bf16[4,1032,128]{2,1,0:T(8,128)(2,1)}), bf16[4,1032,128]{2,1,0:T(8,128)(2,1)S(1)}, u32[]{:S(2)}, u32[]{:S(2)}) async-start(bf16[4,1032,128]{2,1,0:T(8,128)(2,1)} %combine_1.1), calls=%async_computation | async-start | bytes 2113536 | tf_op jit(solution)/shard_map/all_to_all | solution.py:333
  39.0 2.1 %line_0.1 = (bf16[264,128]{1,0:T(8,128)(2,1)}, bf16[264,128]{1,0:T(8,128)(2,1)}, bf16[264,128]{1,0:T(8,128)(2,1)}, bf16[264,128]{1,0:T(8,128)(2,1)}) custom-call(s32[1]{0:T(128)} %bitcast.1.y_ref, bf16[4,1032,128]{2,1,0:T(8,128)(2,1)} %copy-done.1), custom_call_target="tpu_custom_call" | custom-call | flops 16777216 | tf_op jit(solution)/shard_map/line_0/pallas_call | solution.py:299
  41.1 1.3 collective-permute-start.14
  42.4 2.6 %collective-permute-start.15 = (bf16[264,128]{1,0:T(8,128)(2,1)}, bf16[264,128]{1,0:T(8,128)(2,1)S(1)}, u32[]{:S(2)}, u32[]{:S(2)}) collective-permute-start(bf16[264,128]{1,0:T(8,128)(2,1)} %get-tuple-element.40), channel_id=1, source_target_pairs={{0,16},{8,24},{16,0},{24,8},{1,17},{9,25},{17,1},{25,9},{2,18},{10... | collective-permute-start | bytes 202760 | tf_op jit(solution)/shard_map/ppermute | solution.py:256
  45.0 1.1 collective-permute-start.16
  46.1 1.6 collective-permute-done.15.refs_2_
  47.8 1.5 collective-permute-done.16.refs_3_
  49.2 0.6 copy-done.12
  49.9 1.7 %plane_0.1 = bf16[264,128]{1,0:T(8,128)(2,1)} custom-call(s32[1]{0:T(128)} %bitcast.1.y_ref, bf16[264,128]{1,0:T(8,128)(2,1)} %get-tuple-element.38.refs_0_, bf16[264,128]{1,0:T(8,128)(2,1)} %copy-done.8, bf16[264,128]{1,0:T(8,128)(2,1)} %copy-done.10, bf16[264,128]{1,0:T(8,128)(2,1)} %copy-done.12), custom_call_target="tpu_custom_call" | custom-call | flops 4194304 | tf_op jit(solution)/shard_map/plane_0/pallas_call | solution.py:304
  51.6 3.1 %collective-permute-start.17 = (bf16[264,128]{1,0:T(8,128)(2,1)}, bf16[264,128]{1,0:T(8,128)(2,1)S(1)}, u32[]{:S(2)}, u32[]{:S(2)}) collective-permute-start(bf16[264,128]{1,0:T(8,128)(2,1)} %plane_0.1), channel_id=1, source_target_pairs={{0,32},{32,64},{64,96},{1,33},{33,65},{65,97},{2,34},{34,66},{66,9... | collective-permute-start | bytes 202760 | tf_op jit(solution)/shard_map/ppermute | solution.py:256
  54.7 4.4 %collective-permute-start.18 = (bf16[264,128]{1,0:T(8,128)(2,1)}, bf16[264,128]{1,0:T(8,128)(2,1)S(1)}, u32[]{:S(2)}, u32[]{:S(2)}) collective-permute-start(bf16[264,128]{1,0:T(8,128)(2,1)} %plane_0.1), channel_id=1, source_target_pairs={{0,64},{32,96},{1,65},{33,97},{2,66},{34,98},{3,67},{35,99},{4,68}... | collective-permute-start | bytes 202760 | tf_op jit(solution)/shard_map/ppermute | solution.py:256
  59.1 1.3 collective-permute-start.19
  60.7 1.7 collective-permute-done.19.refs_6_
  62.4 0.6 copy-done.19
  63.0 1.9 %carry_0.1 = (bf16[256,128]{1,0:T(8,128)(2,1)}, bf16[256,128]{1,0:T(8,128)(2,1)}, bf16[256,128]{1,0:T(8,128)(2,1)}, bf16[256,128]{1,0:T(8,128)(2,1)}) custom-call(s32[1]{0:T(128)} %bitcast.1.y_ref, bf16[264,128]{1,0:T(8,128)(2,1)} %get-tuple-element.38.refs_0_, bf16[264,128]{1,0:T(8,128)(2,1)} %copy-done.8, bf16[264,128]{1,0:T(8,128)(2,1)} %copy-done.10, ...), custom_call_target="tpu_custom_call" | custom-call | flops 4194304 | tf_op jit(solution)/shard_map/carry_0/pallas_call | solution.py:309
  64.9 3.5 %collective-permute-start.21 = (bf16[256,128]{1,0:T(8,128)(2,1)}, bf16[256,128]{1,0:T(8,128)(2,1)S(1)}, u32[]{:S(2)}, u32[]{:S(2)}) collective-permute-start(bf16[256,128]{1,0:T(8,128)(2,1)} %get-tuple-element.44), channel_id=1, source_target_pairs={{0,16},{8,24},{16,0},{24,8},{1,17},{9,25},{17,1},{25,9},{2,18},{10... | collective-permute-start | bytes 196616 | tf_op jit(solution)/shard_map/ppermute | solution.py:256
  68.4 1.1 collective-permute-done.20.refs_1_
  69.5 1.5 collective-permute-done.21.refs_2_
  71.0 0.8 collective-permute-done.22.refs_3_
  71.7 0.6 copy-done.26
  72.3 2.6 %starts_0.1 = bf16[4,1024,128]{2,1,0:T(8,128)(2,1)} custom-call(s32[1]{0:T(128)} %bitcast.1.y_ref, bf16[4,1032,128]{2,1,0:T(8,128)(2,1)} %copy-done.1, bf16[256,128]{1,0:T(8,128)(2,1)} %get-tuple-element.42.refs_0_, bf16[256,128]{1,0:T(8,128)(2,1)} %copy-done.22, bf16[256,128]{1,0:T(8,128)(2,1)} %copy-done.24, bf16[256,128]{1,0:T(8,128)(2,1)} %copy-done.26), custom_call_target="tpu_custom_call" | custom-call | flops 16777216 | tf_op jit(solution)/shard_map/starts_0/pallas_call | solution.py:315
  74.9 4.4 %all-to-all-start.3 = ((bf16[4,1024,128]{2,1,0:T(8,128)(2,1)}), bf16[4,1024,128]{2,1,0:T(8,128)(2,1)S(1)}, u32[]{:S(2)}, u32[]{:S(2)}) async-start(bf16[4,1024,128]{2,1,0:T(8,128)(2,1)} %starts_0.1), calls=%async_computation.3 | async-start | bytes 2097152 | tf_op jit(solution)/shard_map/all_to_all | solution.py:337
  79.3 2.1 %line_1.1 = (bf16[264,128]{1,0:T(8,128)(2,1)}, bf16[264,128]{1,0:T(8,128)(2,1)}, bf16[264,128]{1,0:T(8,128)(2,1)}, bf16[264,128]{1,0:T(8,128)(2,1)}) custom-call(s32[1]{0:T(128)} %bitcast.1.y_ref, bf16[4,1032,128]{2,1,0:T(8,128)(2,1)} %copy-done), custom_call_target="tpu_custom_call" | custom-call | flops 16777216 | tf_op jit(solution)/shard_map/line_1/pallas_call | solution.py:299
  81.6 2.5 %collective-permute-start.3 = (bf16[264,128]{1,0:T(8,128)(2,1)}, bf16[264,128]{1,0:T(8,128)(2,1)S(1)}, u32[]{:S(2)}, u32[]{:S(2)}) collective-permute-start(bf16[264,128]{1,0:T(8,128)(2,1)} %get-tuple-element.29), channel_id=1, source_target_pairs={{0,16},{8,24},{16,0},{24,8},{1,17},{9,25},{17,1},{25,9},{2,18},{10... | collective-permute-start | bytes 202760 | tf_op jit(solution)/shard_map/ppermute | solution.py:256
  84.1 1.6 collective-permute-start.4
  86.0 0.7 collective-permute-done.3.refs_2_
  86.8 1.0 collective-permute-done.4.refs_3_
  87.8 0.6 copy-done.13
  88.4 1.7 %plane_1.1 = bf16[264,128]{1,0:T(8,128)(2,1)} custom-call(s32[1]{0:T(128)} %bitcast.1.y_ref, bf16[264,128]{1,0:T(8,128)(2,1)} %get-tuple-element.27.refs_0_, bf16[264,128]{1,0:T(8,128)(2,1)} %copy-done.9, bf16[264,128]{1,0:T(8,128)(2,1)} %copy-done.11, bf16[264,128]{1,0:T(8,128)(2,1)} %copy-done.13), custom_call_target="tpu_custom_call" | custom-call | flops 4194304 | tf_op jit(solution)/shard_map/plane_1/pallas_call | solution.py:304
  90.1 1.3 collective-permute-start.5
  91.4 6.4 %collective-permute-start.6 = (bf16[264,128]{1,0:T(8,128)(2,1)}, bf16[264,128]{1,0:T(8,128)(2,1)S(1)}, u32[]{:S(2)}, u32[]{:S(2)}) collective-permute-start(bf16[264,128]{1,0:T(8,128)(2,1)} %plane_1.1), channel_id=1, source_target_pairs={{0,64},{32,96},{1,65},{33,97},{2,66},{34,98},{3,67},{35,99},{4,68}... | collective-permute-start | bytes 202760 | tf_op jit(solution)/shard_map/ppermute | solution.py:256
  97.8 1.3 collective-permute-start.7
  99.1 0.7 collective-permute-done.6.refs_5_
  99.8 0.9 collective-permute-done.7.refs_6_
  100.8 0.6 copy-done.20
  101.4 1.9 %carry_1.1 = (bf16[256,128]{1,0:T(8,128)(2,1)}, bf16[256,128]{1,0:T(8,128)(2,1)}, bf16[256,128]{1,0:T(8,128)(2,1)}, bf16[256,128]{1,0:T(8,128)(2,1)}) custom-call(s32[1]{0:T(128)} %bitcast.1.y_ref, bf16[264,128]{1,0:T(8,128)(2,1)} %get-tuple-element.27.refs_0_, bf16[264,128]{1,0:T(8,128)(2,1)} %copy-done.9, bf16[264,128]{1,0:T(8,128)(2,1)} %copy-done.11, ...), custom_call_target="tpu_custom_call" | custom-call | flops 4194304 | tf_op jit(solution)/shard_map/carry_1/pallas_call | solution.py:309
  103.3 2.9 %collective-permute-start.10 = (bf16[256,128]{1,0:T(8,128)(2,1)}, bf16[256,128]{1,0:T(8,128)(2,1)S(1)}, u32[]{:S(2)}, u32[]{:S(2)}) collective-permute-start(bf16[256,128]{1,0:T(8,128)(2,1)} %get-tuple-element.34), channel_id=1, source_target_pairs={{0,24},{8,0},{16,8},{24,16},{1,25},{9,1},{17,9},{25,17},{2,26},{10... | collective-permute-start | bytes 196616 | tf_op jit(solution)/shard_map/ppermute | solution.py:256
  106.3 1.2 collective-permute-start.9
  107.5 0.4 collective-permute-done.10.refs_3_
  107.9 3.6 %collective-permute-done.8.refs_1_ = bf16[256,128]{1,0:T(8,128)(2,1)S(1)} collective-permute-done((bf16[256,128]{1,0:T(8,128)(2,1)}, bf16[256,128]{1,0:T(8,128)(2,1)S(1)}, u32[]{:S(2)}, u32[]{:S(2)}) %collective-permute-start.8) | collective-permute-done | bytes 65568 | tf_op jit(solution)/shard_map/ppermute | solution.py:256
  111.5 0.6 copy-done.23
  112.2 2.7 %starts_1.1 = bf16[4,1024,128]{2,1,0:T(8,128)(2,1)} custom-call(s32[1]{0:T(128)} %bitcast.1.y_ref, bf16[4,1032,128]{2,1,0:T(8,128)(2,1)} %copy-done, bf16[256,128]{1,0:T(8,128)(2,1)} %get-tuple-element.31.refs_0_, bf16[256,128]{1,0:T(8,128)(2,1)} %copy-done.23, bf16[256,128]{1,0:T(8,128)(2,1)} %copy-done.25, bf16[256,128]{1,0:T(8,128)(2,1)} %copy-done.21), custom_call_target="tpu_custom_call" | custom-call | flops 16777216 | tf_op jit(solution)/shard_map/starts_1/pallas_call | solution.py:315
  114.9 4.3 %all-to-all-start.1 = ((bf16[4,1024,128]{2,1,0:T(8,128)(2,1)}), bf16[4,1024,128]{2,1,0:T(8,128)(2,1)}, u32[]{:S(2)}, u32[]{:S(2)}) async-start(bf16[4,1024,128]{2,1,0:T(8,128)(2,1)} %starts_1.1), calls=%async_computation.1 | async-start | bytes 2097152 | tf_op jit(solution)/shard_map/all_to_all | solution.py:337
  119.1 8.9 %collective-permute-start.24 = (bf16[16,256,128]{2,1,0:T(8,128)(2,1)S(1)}, bf16[16,256,128]{2,1,0:T(8,128)(2,1)}, u32[]{:S(2)}, u32[]{:S(2)}) collective-permute-start(bf16[16,256,128]{2,1,0:T(8,128)(2,1)S(1)} %copy-done.4), channel_id=1, source_target_pairs={{0,1},{1,0},{2,3},{3,2},{4,5},{5,4},{6,7},{7,6},{8,9},{9,8},{10,11... | collective-permute-start | bytes 3145736 | tf_op jit(solution)/shard_map/ppermute | solution.py:335
  128.9 10.1 %collective-permute-start.11 = (bf16[16,256,128]{2,1,0:T(8,128)(2,1)}, bf16[16,256,128]{2,1,0:T(8,128)(2,1)}, u32[]{:S(2)}, u32[]{:S(2)}) collective-permute-start(bf16[16,256,128]{2,1,0:T(8,128)(2,1)} %bitcast.4.start_ref), channel_id=1, source_target_pairs={{0,1},{1,0},{2,3},{3,2},{4,5},{5,4},{6,7},{7,6},{8,9},{9,8},{10,11... | collective-permute-start | bytes 3145736 | tf_op jit(solution)/shard_map/ppermute | solution.py:344
  139.1 6.5 %within_0.1 = (f32[256,2048]{1,0:T(8,128)}, f32[256,2048]{1,0:T(8,128)}, f32[256,16]{1,0:T(8,128)}) custom-call(s32[1]{0:T(128)} %bitcast.2.group_ref, bf16[256,4096]{1,0:T(8,128)(2,1)} %query_ref.7, bf16[256,4096]{1,0:T(8,128)(2,1)} %refs_5_.3, bf16[256,8192]{1,0:T(8,128)(2,1)} %refs_6_.3, bf16[16,256,128]{2,1,0:T(8,128)(2,1)} %copy-done.3, ...), custom_call_target="tpu_custom_call" | custom-call | flops 1073741824 | tf_op jit(solution)/shard_map/within_0/pallas_call | solution.py:288
  145.6 6.5 %within_1.1 = (f32[256,2048]{1,0:T(8,128)}, f32[256,2048]{1,0:T(8,128)}, f32[256,16]{1,0:T(8,128)}) custom-call(s32[1]{0:T(128)S(6)} %add.7.group_ref, bf16[256,4096]{1,0:T(8,128)(2,1)} %query_ref.7, bf16[256,4096]{1,0:T(8,128)(2,1)} %refs_5_.3, bf16[256,8192]{1,0:T(8,128)(2,1)} %refs_6_.3, bf16[16,256,128]{2,1,0:T(8,128)(2,1)} %copy-done.2, ...), custom_call_target="tpu_custom_call" | custom-call | flops 1073741824 | tf_op jit(solution)/shard_map/within_1/pallas_call | solution.py:288
  152.1 4.3 %finish_0_0.1.rest_0_ = bf16[256,8192]{1,0:T(8,128)(2,1)} custom-call(s32[1]{0:T(128)} %bitcast.2.group_ref, bf16[256,4096]{1,0:T(8,128)(2,1)} %query_ref.7, bf16[16,256,128]{2,1,0:T(8,128)(2,1)} %bitcast.7, f32[256,2048]{1,0:T(8,128)} %get-tuple-element.48.within_ref, bf16[256,8192]{1,0:T(8,128)(2,1)} %gate_ref.7, f32[256,16]{1,0:T(8,128)} %get-tuple-element.47.reach_ref), custom_call_target="tpu_custom_call" | custom-call | flops 268435456 | tf_op jit(solution)/shard_map/finish_0_0/pallas_call | solution.py:347
  156.3 4.2 %finish_0_1.1.rest_0_ = bf16[256,8192]{1,0:T(8,128)(2,1)} custom-call(s32[1]{0:T(128)} %bitcast.group_ref, bf16[256,4096]{1,0:T(8,128)(2,1)} %query_ref.7, bf16[16,256,128]{2,1,0:T(8,128)(2,1)} %collective-permute-done.23.start_ref, f32[256,2048]{1,0:T(8,128)} %get-tuple-element.46.within_ref, ...), custom_call_target="tpu_custom_call", output_to_operand_aliasing={{}: (6, {})} | custom-call | flops 268435456 | tf_op jit(solution)/shard_map/finish_0_1/pallas_call | solution.py:347
  160.6 4.3 %finish_1_0.1.rest_0_ = bf16[256,8192]{1,0:T(8,128)(2,1)} custom-call(s32[1]{0:T(128)S(6)} %add.7.group_ref, bf16[256,4096]{1,0:T(8,128)(2,1)} %query_ref.7, bf16[16,256,128]{2,1,0:T(8,128)(2,1)} %bitcast.4.start_ref, f32[256,2048]{1,0:T(8,128)} %get-tuple-element.37.within_ref, bf16[256,8192]{1,0:T(8,128)(2,1)} %gate_ref.7, ...), custom_call_target="tpu_custom_call", output_to_operand_aliasing={{}: (6, {})} | custom-call | flops 268435456 | tf_op jit(solution)/shard_map/finish_1_0/pallas_call | solution.py:347
  164.8 4.2 %finish_1_1.1 = bf16[256,8192]{1,0:T(8,128)(2,1)} custom-call(s32[1]{0:T(128)S(6)} %add.6.group_ref, bf16[256,4096]{1,0:T(8,128)(2,1)} %query_ref.7, bf16[16,256,128]{2,1,0:T(8,128)(2,1)} %collective-permute-done.11.start_ref, f32[256,2048]{1,0:T(8,128)} %get-tuple-element.35.within_ref, bf16[256,8192]{1,0:T(8,128)(2,1)} %gate_ref.7, ...), custom_call_target="tpu_custom_call", output_to_operand_aliasing={{}: (6, {})} | custom-call | flops 268435456 | tf_op jit(solution)/shard_map/finish_1_1/pallas_call | solution.py:347
  (68 shorter events, 1.9 us)
Async XLA Ops:
  3.1 8.1 %collective-permute-start.13 = (bf16[16,256,128]{2,1,0:T(8,128)(2,1)}, bf16[16,256,128]{2,1,0:T(8,128)(2,1)S(1)}, u32[]{:S(2)}, u32[]{:S(2)}) collective-permute-start(bf16[16,256,128]{2,1,0:T(8,128)(2,1)} %theirs_state_0.1), channel_id=1, source_target_pairs={{0,1},{1,0},{2,3},{3,2},{4,5},{5,4},{6,7},{7,6},{8,9},{9,8},{10,11... | collective-permute-start | bytes 3145736 | tf_op jit(solution)/shard_map/ppermute | solution.py:326
  4.5 3.2 %copy-start.7 = (bf16[256,16]{0,1:T(8,128)(2,1)S(1)}, bf16[256,16]{0,1:T(8,128)(2,1)}, u32[]{:S(2)}) copy-start(bf16[256,16]{0,1:T(8,128)(2,1)} %param.8) | copy-start | bytes 24580
  7.6 16.0 %collective-permute-start = (bf16[16,256,128]{2,1,0:T(8,128)(2,1)}, bf16[16,256,128]{2,1,0:T(8,128)(2,1)S(1)}, u32[]{:S(2)}, u32[]{:S(2)}) collective-permute-start(bf16[16,256,128]{2,1,0:T(8,128)(2,1)} %theirs_state_1.1), channel_id=1, source_target_pairs={{0,1},{1,0},{2,3},{3,2},{4,5},{5,4},{6,7},{7,6},{8,9},{9,8},{10,11... | collective-permute-start | bytes 3145736 | tf_op jit(solution)/shard_map/ppermute | solution.py:326
  7.7 3.5 %collective-permute-start.1 = (bf16[16,256]{1,0:T(8,128)(2,1)S(1)}, bf16[16,256]{1,0:T(8,128)(2,1)S(1)}, u32[]{:S(2)}, u32[]{:S(2)}) collective-permute-start(bf16[16,256]{1,0:T(8,128)(2,1)S(1)} %bitcast.16), channel_id=1, source_target_pairs={{0,1},{1,0},{2,3},{3,2},{4,5},{5,4},{6,7},{7,6},{8,9},{9,8},{10,11... | collective-permute-start | bytes 24584 | tf_op jit(solution)/shard_map/ppermute | solution.py:265
  11.2 0.6 copy-start.14
  11.8 1.0 copy-start.3
  15.4 20.1 %all-to-all-start.2 = ((bf16[4,1032,128]{2,1,0:T(8,128)(2,1)}), bf16[4,1032,128]{2,1,0:T(8,128)(2,1)S(1)}, u32[]{:S(2)}, u32[]{:S(2)}) async-start(bf16[4,1032,128]{2,1,0:T(8,128)(2,1)} %combine_0.1), calls=%async_computation.2 | async-start | bytes 2113536 | tf_op jit(solution)/shard_map/all_to_all | solution.py:333
  23.6 1.0 copy-start.2
  35.4 3.5 %copy-start.1 = (bf16[4,1032,128]{2,1,0:T(8,128)(2,1)}, bf16[4,1032,128]{2,1,0:T(8,128)(2,1)S(1)}, u32[]{:S(2)}) copy-start(bf16[4,1032,128]{2,1,0:T(8,128)(2,1)S(1)} %all-to-all-done.2.in_ref) | copy-start | bytes 3170308
  35.4 39.5 %all-to-all-start = ((bf16[4,1032,128]{2,1,0:T(8,128)(2,1)}), bf16[4,1032,128]{2,1,0:T(8,128)(2,1)S(1)}, u32[]{:S(2)}, u32[]{:S(2)}) async-start(bf16[4,1032,128]{2,1,0:T(8,128)(2,1)} %combine_1.1), calls=%async_computation | async-start | bytes 2113536 | tf_op jit(solution)/shard_map/all_to_all | solution.py:333
  41.1 5.0 %collective-permute-start.14 = (bf16[264,128]{1,0:T(8,128)(2,1)}, bf16[264,128]{1,0:T(8,128)(2,1)S(1)}, u32[]{:S(2)}, u32[]{:S(2)}) collective-permute-start(bf16[264,128]{1,0:T(8,128)(2,1)} %get-tuple-element.39), channel_id=1, source_target_pairs={{0,8},{8,16},{16,24},{24,0},{1,9},{9,17},{17,25},{25,1},{2,10},{10... | collective-permute-start | bytes 202760 | tf_op jit(solution)/shard_map/ppermute | solution.py:256
  42.4 5.3 %collective-permute-start.15 = (bf16[264,128]{1,0:T(8,128)(2,1)}, bf16[264,128]{1,0:T(8,128)(2,1)S(1)}, u32[]{:S(2)}, u32[]{:S(2)}) collective-permute-start(bf16[264,128]{1,0:T(8,128)(2,1)} %get-tuple-element.40), channel_id=1, source_target_pairs={{0,16},{8,24},{16,0},{24,8},{1,17},{9,25},{17,1},{25,9},{2,18},{10... | collective-permute-start | bytes 202760 | tf_op jit(solution)/shard_map/ppermute | solution.py:256
  45.0 4.2 %collective-permute-start.16 = (bf16[264,128]{1,0:T(8,128)(2,1)}, bf16[264,128]{1,0:T(8,128)(2,1)S(1)}, u32[]{:S(2)}, u32[]{:S(2)}) collective-permute-start(bf16[264,128]{1,0:T(8,128)(2,1)} %get-tuple-element.41), channel_id=1, source_target_pairs={{0,24},{8,0},{16,8},{24,16},{1,25},{9,1},{17,9},{25,17},{2,26},{10... | collective-permute-start | bytes 202760 | tf_op jit(solution)/shard_map/ppermute | solution.py:256
  46.1 3.1 %copy-start.8 = (bf16[264,128]{1,0:T(8,128)(2,1)}, bf16[264,128]{1,0:T(8,128)(2,1)S(1)}, u32[]{:S(2)}) copy-start(bf16[264,128]{1,0:T(8,128)(2,1)S(1)} %collective-permute-done.14.refs_1_) | copy-start | bytes 202756
  47.7 1.5 copy-start.10
  49.2 0.6 copy-start.12
  51.6 8.8 %collective-permute-start.17 = (bf16[264,128]{1,0:T(8,128)(2,1)}, bf16[264,128]{1,0:T(8,128)(2,1)S(1)}, u32[]{:S(2)}, u32[]{:S(2)}) collective-permute-start(bf16[264,128]{1,0:T(8,128)(2,1)} %plane_0.1), channel_id=1, source_target_pairs={{0,32},{32,64},{64,96},{1,33},{33,65},{65,97},{2,34},{34,66},{66,9... | collective-permute-start | bytes 202760 | tf_op jit(solution)/shard_map/ppermute | solution.py:256
  54.7 6.0 %collective-permute-start.18 = (bf16[264,128]{1,0:T(8,128)(2,1)}, bf16[264,128]{1,0:T(8,128)(2,1)S(1)}, u32[]{:S(2)}, u32[]{:S(2)}) collective-permute-start(bf16[264,128]{1,0:T(8,128)(2,1)} %plane_0.1), channel_id=1, source_target_pairs={{0,64},{32,96},{1,65},{33,97},{2,66},{34,98},{3,67},{35,99},{4,68}... | collective-permute-start | bytes 202760 | tf_op jit(solution)/shard_map/ppermute | solution.py:256
  59.1 3.3 %collective-permute-start.19 = (bf16[264,128]{1,0:T(8,128)(2,1)}, bf16[264,128]{1,0:T(8,128)(2,1)S(1)}, u32[]{:S(2)}, u32[]{:S(2)}) collective-permute-start(bf16[264,128]{1,0:T(8,128)(2,1)} %plane_0.1), channel_id=1, source_target_pairs={{0,96},{1,97},{2,98},{3,99},{4,100},{5,101},{6,102},{7,103},{8,104... | collective-permute-start | bytes 202760 | tf_op jit(solution)/shard_map/ppermute | solution.py:256
  60.4 2.0 %copy-start.15 = (bf16[264,128]{1,0:T(8,128)(2,1)}, bf16[264,128]{1,0:T(8,128)(2,1)S(1)}, u32[]{:S(2)}) copy-start(bf16[264,128]{1,0:T(8,128)(2,1)S(1)} %collective-permute-done.17.refs_4_) | copy-start | bytes 202756
  60.7 1.7 copy-start.17
  62.4 0.6 copy-start.19
  64.9 4.5 %collective-permute-start.20 = (bf16[256,128]{1,0:T(8,128)(2,1)}, bf16[256,128]{1,0:T(8,128)(2,1)S(1)}, u32[]{:S(2)}, u32[]{:S(2)}) collective-permute-start(bf16[256,128]{1,0:T(8,128)(2,1)} %get-tuple-element.43), channel_id=1, source_target_pairs={{0,8},{8,16},{16,24},{24,0},{1,9},{9,17},{17,25},{25,1},{2,10},{10... | collective-permute-start | bytes 196616 | tf_op jit(solution)/shard_map/ppermute | solution.py:256
  64.9 6.0 %collective-permute-start.21 = (bf16[256,128]{1,0:T(8,128)(2,1)}, bf16[256,128]{1,0:T(8,128)(2,1)S(1)}, u32[]{:S(2)}, u32[]{:S(2)}) collective-permute-start(bf16[256,128]{1,0:T(8,128)(2,1)} %get-tuple-element.44), channel_id=1, source_target_pairs={{0,16},{8,24},{16,0},{24,8},{1,17},{9,25},{17,1},{25,9},{2,18},{10... | collective-permute-start | bytes 196616 | tf_op jit(solution)/shard_map/ppermute | solution.py:256
  68.4 3.3 %collective-permute-start.22 = (bf16[256,128]{1,0:T(8,128)(2,1)}, bf16[256,128]{1,0:T(8,128)(2,1)S(1)}, u32[]{:S(2)}, u32[]{:S(2)}) collective-permute-start(bf16[256,128]{1,0:T(8,128)(2,1)} %get-tuple-element.45), channel_id=1, source_target_pairs={{0,24},{8,0},{16,8},{24,16},{1,25},{9,1},{17,9},{25,17},{2,26},{10... | collective-permute-start | bytes 196616 | tf_op jit(solution)/shard_map/ppermute | solution.py:256
  69.5 2.3 %copy-start.22 = (bf16[256,128]{1,0:T(8,128)(2,1)}, bf16[256,128]{1,0:T(8,128)(2,1)S(1)}, u32[]{:S(2)}) copy-start(bf16[256,128]{1,0:T(8,128)(2,1)S(1)} %collective-permute-done.20.refs_1_) | copy-start | bytes 196612
  71.0 0.8 copy-start.24
  71.7 0.6 copy-start.26
  74.9 4.4 %copy-start = (bf16[4,1032,128]{2,1,0:T(8,128)(2,1)}, bf16[4,1032,128]{2,1,0:T(8,128)(2,1)S(1)}, u32[]{:S(2)}) copy-start(bf16[4,1032,128]{2,1,0:T(8,128)(2,1)S(1)} %all-to-all-done.in_ref) | copy-start | bytes 3170308
  74.9 39.9 %all-to-all-start.3 = ((bf16[4,1024,128]{2,1,0:T(8,128)(2,1)}), bf16[4,1024,128]{2,1,0:T(8,128)(2,1)S(1)}, u32[]{:S(2)}, u32[]{:S(2)}) async-start(bf16[4,1024,128]{2,1,0:T(8,128)(2,1)} %starts_0.1), calls=%async_computation.3 | async-start | bytes 2097152 | tf_op jit(solution)/shard_map/all_to_all | solution.py:337
  81.5 4.6 %collective-permute-start.2 = (bf16[264,128]{1,0:T(8,128)(2,1)}, bf16[264,128]{1,0:T(8,128)(2,1)S(1)}, u32[]{:S(2)}, u32[]{:S(2)}) collective-permute-start(bf16[264,128]{1,0:T(8,128)(2,1)} %get-tuple-element.28), channel_id=1, source_target_pairs={{0,8},{8,16},{16,24},{24,0},{1,9},{9,17},{17,25},{25,1},{2,10},{10... | collective-permute-start | bytes 202760 | tf_op jit(solution)/shard_map/ppermute | solution.py:256
  81.6 5.1 %collective-permute-start.3 = (bf16[264,128]{1,0:T(8,128)(2,1)}, bf16[264,128]{1,0:T(8,128)(2,1)S(1)}, u32[]{:S(2)}, u32[]{:S(2)}) collective-permute-start(bf16[264,128]{1,0:T(8,128)(2,1)} %get-tuple-element.29), channel_id=1, source_target_pairs={{0,16},{8,24},{16,0},{24,8},{1,17},{9,25},{17,1},{25,9},{2,18},{10... | collective-permute-start | bytes 202760 | tf_op jit(solution)/shard_map/ppermute | solution.py:256
  84.1 3.6 %collective-permute-start.4 = (bf16[264,128]{1,0:T(8,128)(2,1)}, bf16[264,128]{1,0:T(8,128)(2,1)S(1)}, u32[]{:S(2)}, u32[]{:S(2)}) collective-permute-start(bf16[264,128]{1,0:T(8,128)(2,1)} %get-tuple-element.30), channel_id=1, source_target_pairs={{0,24},{8,0},{16,8},{24,16},{1,25},{9,1},{17,9},{25,17},{2,26},{10... | collective-permute-start | bytes 202760 | tf_op jit(solution)/shard_map/ppermute | solution.py:256
  86.0 1.8 %copy-start.9 = (bf16[264,128]{1,0:T(8,128)(2,1)}, bf16[264,128]{1,0:T(8,128)(2,1)S(1)}, u32[]{:S(2)}) copy-start(bf16[264,128]{1,0:T(8,128)(2,1)S(1)} %collective-permute-done.2.refs_1_) | copy-start | bytes 202756
  86.8 1.0 copy-start.11
  87.8 0.6 copy-start.13
  90.1 9.0 %collective-permute-start.5 = (bf16[264,128]{1,0:T(8,128)(2,1)}, bf16[264,128]{1,0:T(8,128)(2,1)S(1)}, u32[]{:S(2)}, u32[]{:S(2)}) collective-permute-start(bf16[264,128]{1,0:T(8,128)(2,1)} %plane_1.1), channel_id=1, source_target_pairs={{0,32},{32,64},{64,96},{1,33},{33,65},{65,97},{2,34},{34,66},{66,9... | collective-permute-start | bytes 202760 | tf_op jit(solution)/shard_map/ppermute | solution.py:256
  91.4 8.4 %collective-permute-start.6 = (bf16[264,128]{1,0:T(8,128)(2,1)}, bf16[264,128]{1,0:T(8,128)(2,1)S(1)}, u32[]{:S(2)}, u32[]{:S(2)}) collective-permute-start(bf16[264,128]{1,0:T(8,128)(2,1)} %plane_1.1), channel_id=1, source_target_pairs={{0,64},{32,96},{1,65},{33,97},{2,66},{34,98},{3,67},{35,99},{4,68}... | collective-permute-start | bytes 202760 | tf_op jit(solution)/shard_map/ppermute | solution.py:256
  97.8 2.9 %collective-permute-start.7 = (bf16[264,128]{1,0:T(8,128)(2,1)}, bf16[264,128]{1,0:T(8,128)(2,1)S(1)}, u32[]{:S(2)}, u32[]{:S(2)}) collective-permute-start(bf16[264,128]{1,0:T(8,128)(2,1)} %plane_1.1), channel_id=1, source_target_pairs={{0,96},{1,97},{2,98},{3,99},{4,100},{5,101},{6,102},{7,103},{8,104... | collective-permute-start | bytes 202760 | tf_op jit(solution)/shard_map/ppermute | solution.py:256
  99.1 1.6 copy-start.16
  99.8 1.0 copy-start.18
  100.8 0.6 copy-start.20
  103.3 4.6 %collective-permute-start.10 = (bf16[256,128]{1,0:T(8,128)(2,1)}, bf16[256,128]{1,0:T(8,128)(2,1)S(1)}, u32[]{:S(2)}, u32[]{:S(2)}) collective-permute-start(bf16[256,128]{1,0:T(8,128)(2,1)} %get-tuple-element.34), channel_id=1, source_target_pairs={{0,24},{8,0},{16,8},{24,16},{1,25},{9,1},{17,9},{25,17},{2,26},{10... | collective-permute-start | bytes 196616 | tf_op jit(solution)/shard_map/ppermute | solution.py:256
  106.3 5.2 %collective-permute-start.8 = (bf16[256,128]{1,0:T(8,128)(2,1)}, bf16[256,128]{1,0:T(8,128)(2,1)S(1)}, u32[]{:S(2)}, u32[]{:S(2)}) collective-permute-start(bf16[256,128]{1,0:T(8,128)(2,1)} %get-tuple-element.32), channel_id=1, source_target_pairs={{0,8},{8,16},{16,24},{24,0},{1,9},{9,17},{17,25},{25,1},{2,10},{10... | collective-permute-start | bytes 196616 | tf_op jit(solution)/shard_map/ppermute | solution.py:256
  106.3 5.2 %collective-permute-start.9 = (bf16[256,128]{1,0:T(8,128)(2,1)}, bf16[256,128]{1,0:T(8,128)(2,1)S(1)}, u32[]{:S(2)}, u32[]{:S(2)}) collective-permute-start(bf16[256,128]{1,0:T(8,128)(2,1)} %get-tuple-element.33), channel_id=1, source_target_pairs={{0,16},{8,24},{16,0},{24,8},{1,17},{9,25},{17,1},{25,9},{2,18},{10... | collective-permute-start | bytes 196616 | tf_op jit(solution)/shard_map/ppermute | solution.py:256
  107.9 3.6 %copy-start.21 = (bf16[256,128]{1,0:T(8,128)(2,1)}, bf16[256,128]{1,0:T(8,128)(2,1)S(1)}, u32[]{:S(2)}) copy-start(bf16[256,128]{1,0:T(8,128)(2,1)S(1)} %collective-permute-done.10.refs_3_) | copy-start | bytes 196612
  111.5 0.6 copy-start.23
  111.5 0.7 copy-start.25
  112.2 7.0 %copy-start.4 = (bf16[16,256,128]{2,1,0:T(8,128)(2,1)S(1)}, bf16[16,256,128]{2,1,0:T(8,128)(2,1)}, u32[]{:S(2)}) copy-start(bf16[16,256,128]{2,1,0:T(8,128)(2,1)} %own_state_0.1.own_ref) | copy-start | bytes 3145732
  112.2 15.9 %copy-start.5 = (bf16[16,256,128]{2,1,0:T(8,128)(2,1)S(1)}, bf16[16,256,128]{2,1,0:T(8,128)(2,1)}, u32[]{:S(2)}) copy-start(bf16[16,256,128]{2,1,0:T(8,128)(2,1)} %own_state_1.1.own_ref) | copy-start | bytes 3145732
  114.9 30.7 %copy-start.6 = (bf16[4,1024,128]{2,1,0:T(8,128)(2,1)}, bf16[4,1024,128]{2,1,0:T(8,128)(2,1)S(1)}, u32[]{:S(2)}) copy-start(bf16[4,1024,128]{2,1,0:T(8,128)(2,1)S(1)} %all-to-all-done.3) | copy-start | bytes 3145732
  114.9 14.1 %all-to-all-start.1 = ((bf16[4,1024,128]{2,1,0:T(8,128)(2,1)}), bf16[4,1024,128]{2,1,0:T(8,128)(2,1)}, u32[]{:S(2)}, u32[]{:S(2)}) async-start(bf16[4,1024,128]{2,1,0:T(8,128)(2,1)} %starts_1.1), calls=%async_computation.1 | async-start | bytes 2097152 | tf_op jit(solution)/shard_map/all_to_all | solution.py:337
  119.1 19.9 %collective-permute-start.24 = (bf16[16,256,128]{2,1,0:T(8,128)(2,1)S(1)}, bf16[16,256,128]{2,1,0:T(8,128)(2,1)}, u32[]{:S(2)}, u32[]{:S(2)}) collective-permute-start(bf16[16,256,128]{2,1,0:T(8,128)(2,1)S(1)} %copy-done.4), channel_id=1, source_target_pairs={{0,1},{1,0},{2,3},{3,2},{4,5},{5,4},{6,7},{7,6},{8,9},{9,8},{10,11... | collective-permute-start | bytes 3145736 | tf_op jit(solution)/shard_map/ppermute | solution.py:335
  128.1 17.5 %collective-permute-start.12 = (bf16[16,256,128]{2,1,0:T(8,128)(2,1)S(1)}, bf16[16,256,128]{2,1,0:T(8,128)(2,1)}, u32[]{:S(2)}, u32[]{:S(2)}) collective-permute-start(bf16[16,256,128]{2,1,0:T(8,128)(2,1)S(1)} %copy-done.5), channel_id=1, source_target_pairs={{0,1},{1,0},{2,3},{3,2},{4,5},{5,4},{6,7},{7,6},{8,9},{9,8},{10,11... | collective-permute-start | bytes 3145736 | tf_op jit(solution)/shard_map/ppermute | solution.py:335
  128.2 28.2 %collective-permute-start.23 = (bf16[16,256,128]{2,1,0:T(8,128)(2,1)S(1)}, bf16[16,256,128]{2,1,0:T(8,128)(2,1)}, u32[]{:S(2)}, u32[]{:S(2)}) collective-permute-start(bf16[16,256,128]{2,1,0:T(8,128)(2,1)S(1)} %bitcast.6), channel_id=1, source_target_pairs={{0,1},{1,0},{2,3},{3,2},{4,5},{5,4},{6,7},{7,6},{8,9},{9,8},{10,11... | collective-permute-start | bytes 3145736 | tf_op jit(solution)/shard_map/ppermute | solution.py:344
  128.9 35.9 %collective-permute-start.11 = (bf16[16,256,128]{2,1,0:T(8,128)(2,1)}, bf16[16,256,128]{2,1,0:T(8,128)(2,1)}, u32[]{:S(2)}, u32[]{:S(2)}) collective-permute-start(bf16[16,256,128]{2,1,0:T(8,128)(2,1)} %bitcast.4.start_ref), channel_id=1, source_target_pairs={{0,1},{1,0},{2,3},{3,2},{4,5},{5,4},{6,7},{7,6},{8,9},{9,8},{10,11... | collective-permute-start | bytes 3145736 | tf_op jit(solution)/shard_map/ppermute | solution.py:344

commit v4 on v2

v4 whole, which is shorter than its diff:
```python
import jax
import jax.numpy as jnp
from jax import lax
from jax.experimental import pallas as pl
from jax.experimental.pallas import tpu as pltpu
from jax.sharding import Mesh, PartitionSpec as P


HEADS = 16
DK = 256
DV = 512
ROWS = 256
HALF = HEADS // 2
CHIPS = 64
SLICES = CHIPS // HALF
PIECE = DK // SLICES
TILES = DV // 128
SLICE = PIECE * TILES
SENT = SLICE + 8
PER_STEP = 4
MIB = 2**20
LIMIT = 20

f32 = jnp.float32
bf16 = jnp.bfloat16


def triangle():
    rows = lax.broadcasted_iota(jnp.int32, (ROWS, ROWS), 0)
    cols = lax.broadcasted_iota(jnp.int32, (ROWS, ROWS), 1)
    return rows >= cols


def running_of(decay):
    ones = triangle().astype(f32).astype(bf16)
    return lax.dot_general(ones, decay, (((1,), (1,)), ((), ())), preferred_element_type=f32)


def running_rows(decay):
    ones = triangle().astype(f32).astype(bf16)
    return lax.dot_general(decay, ones, (((1,), (1,)), ((), ())), preferred_element_type=f32)


def column(table, head):
    lanes = lax.broadcasted_iota(jnp.int32, table.shape, 1)
    return jnp.sum(jnp.where(lanes == head, table, 0.0), axis=1, keepdims=True)


def put_slices(ref, at, state):
    for o in range(SLICES):
        for t in range(TILES):
            ref[at * SLICES + o, t * PIECE : (t + 1) * PIECE, :] = state[
                o * PIECE : (o + 1) * PIECE, t * 128 : (t + 1) * 128
            ]


def get_slices(ref, at):
    cols = [
        ref[pl.ds(at * SLICES, SLICES), t * PIECE : (t + 1) * PIECE, :].reshape(DK, 128)
        for t in range(TILES)
    ]
    return jnp.concatenate(cols, axis=1)


def state_kernel(group_ref, key_ref, value_ref, decay_ref, *refs):
    if len(refs) == 2:
        (out_ref, fade_ref), copies = refs, ()
    else:
        done_ref, out_ref, copy_ref, done_copy_ref, fade_ref = refs
        copies = (copy_ref,)
        size = PER_STEP * SLICES
        done_copy_ref[...] = done_ref[pl.ds(pl.program_id(0) * size, size)]
    step = pl.program_id(0)

    @pl.when(step == 0)
    def _():
        run = running_of(decay_ref[...])
        fade_ref[...] = jnp.exp(run[ROWS - 1 : ROWS, :] - run)

    for n in range(PER_STEP):
        at = step * PER_STEP + n
        fade = column(fade_ref[...], group_ref[0] * HALF + at)
        faded = (key_ref[:, n * DK : (n + 1) * DK].astype(f32) * fade).astype(bf16)
        state = lax.dot_general(
            faded, value_ref[:, n * DV : (n + 1) * DV], (((0,), (0,)), ((), ())),
            preferred_element_type=f32,
        )
        put_slices(out_ref, at, state.astype(bf16))
        for copy_ref in copies:
            put_slices(copy_ref, n, state.astype(bf16))


def combine_kernel(core_ref, own_ref, got_ref, decay_ref, other_ref, out_ref, rate_ref):
    step = pl.program_id(0)
    is_first = core_ref[0] == 0
    ones = jnp.ones((128, ROWS), f32).astype(bf16)
    total = lax.dot_general(
        decay_ref[...], ones, (((1,), (1,)), ((), ())), preferred_element_type=f32
    )
    other = lax.dot_general(
        other_ref[...], ones, (((1,), (1,)), ((), ())), preferred_element_type=f32
    )
    rate_ref[0] = jnp.exp(jnp.where(is_first, other, 0.0))
    rate_ref[1] = jnp.exp(jnp.where(is_first, 0.0, total))
    rate_ref[2] = jnp.exp(total + other)
    rows = lax.broadcasted_iota(jnp.int32, (8, 128), 0)
    for n in range(PER_STEP):
        head = pl.ds(core_ref[0] * HALF + step * PER_STEP + n, 1)
        own_rate = rate_ref[0, head, :]
        got_rate = rate_ref[1, head, :]
        damping = rate_ref[2, head, :]
        high = damping.astype(bf16).astype(f32)
        rest = damping - high
        middle = rest.astype(bf16).astype(f32)
        parts = jnp.where(rows == 0, high, jnp.where(rows == 1, middle, rest - middle))
        parts = parts.astype(bf16)
        for o in range(n * SLICES, (n + 1) * SLICES):
            at = step * PER_STEP * SLICES + o
            both = own_ref[at].astype(f32) * own_rate + got_ref[at].astype(f32) * got_rate
            out_ref[o, :SLICE, :] = both.astype(bf16)
            out_ref[o, SLICE:SENT, :] = parts


def within_kernel(core_ref, *refs):
    own, theirs, (got_ref, first_ref, decay_ref, other_ref) = refs[0:4], refs[4:8], refs[8:12]
    outs, (reach_out, run_ref, rows_ref, reach_ref) = refs[12:16], refs[16:]
    step = pl.program_id(0)
    core = core_ref[0]

    @pl.when(step == 0)
    def _():
        run = running_of(decay_ref[...])
        run_ref[...] = run
        rows_ref[...] = running_rows(decay_ref[...])
        other = running_of(other_ref[...])[ROWS - 1 : ROWS, :]
        reach = jnp.exp(run + jnp.where(core == 0, 0.0, other))
        for h in range(HEADS):
            reach_out[h] = jnp.broadcast_to(reach[:, h : h + 1], (ROWS, 128))
        reach_ref[...] = jnp.where(core == 0, 0.0, jnp.exp(run))

    for group, ins, state_ref, out_ref, gated_ref in (
        (core, own, got_ref, outs[0], outs[1]),
        (1 - core, theirs, first_ref, outs[2], outs[3]),
    ):
        query_ref, key_ref, value_ref, gate_ref = ins
        head = group * HALF + step
        query = query_ref[...]
        scores = lax.dot_general(
            query, key_ref[...], (((1,), (1,)), ((), ())), preferred_element_type=f32
        )
        spread = column(run_ref[...], head) - rows_ref[pl.ds(head, 1), :]
        factor = jnp.exp(jnp.where(triangle(), spread, -jnp.inf))
        weights = (scores * factor).astype(bf16)
        local = jnp.dot(weights, value_ref[...], preferred_element_type=f32)
        before = jnp.dot(query, get_slices(state_ref, 0), preferred_element_type=f32)
        out_ref[0] = local + before * column(reach_ref[...], head)
        gate = gate_ref[...].astype(f32)
        gated_ref[0] = gate / (1.0 + jnp.exp(-gate))


def prefix_kernel(in_ref, out_ref):
    state = jnp.zeros((SLICE, 128), f32)
    for b in range(CHIPS):
        parts = in_ref[b, SLICE:SENT, :].astype(f32)
        damping = parts[0:1] + parts[1:2] + parts[2:3]
        out_ref[b] = state.astype(bf16)
        state = damping * state + in_ref[b, :SLICE, :].astype(f32)


def finish_kernel(group_ref, query_ref, start_ref, within_ref, gated_ref, reach_ref, *rest):
    out_ref = rest[-1]
    for n in range(PER_STEP):
        at = pl.program_id(0) * PER_STEP + n
        across = jnp.dot(
            query_ref[:, n * DK : (n + 1) * DK], get_slices(start_ref, at),
            preferred_element_type=f32,
        )
        reach = reach_ref[n]
        retained = within_ref[n] + across * jnp.concatenate([reach] * TILES, axis=1)
        average = jnp.mean(retained, axis=1, keepdims=True)
        centered = retained - average
        variance = jnp.mean(centered * centered, axis=1, keepdims=True)
        normed = centered * lax.rsqrt(variance + 1e-06)
        out_ref[:, n * DV : (n + 1) * DV] = (gated_ref[n] * normed).astype(bf16)


def call(kernel, grid, in_specs, out_specs, out_shape, scratch, flops, aliases=None):
    return pl.pallas_call(
        kernel,
        out_shape=out_shape,
        grid_spec=pltpu.PrefetchScalarGridSpec(
            num_scalar_prefetch=1,
            grid=(grid,),
            in_specs=in_specs,
            out_specs=out_specs,
            scratch_shapes=scratch,
        ),
        compiler_params=pltpu.CompilerParams(
            dimension_semantics=("arbitrary",), vmem_limit_bytes=LIMIT * MIB
        ),
        cost_estimate=pl.CostEstimate(flops=flops, transcendentals=0, bytes_accessed=0),
        input_output_aliases=aliases or {},
    )


def far(value):
    return pltpu.with_memory_space_constraint(value, pltpu.HBM)


def near(value):
    return pltpu.with_memory_space_constraint(value, pltpu.VMEM)


def shape(*dims, dtype=bf16):
    return jax.ShapeDtypeStruct(dims, dtype)


def shards(queries, key_vectors, values, decay_log, gate_input):
    core = lax.axis_index("core").astype(jnp.int32).reshape(1)
    other = 1 - core
    swap = [(0, 1), (1, 0)]
    everyone = ("seq", "chip")
    decay = decay_log.T
    other_decay = lax.ppermute(decay, "core", swap)

    steps = HALF // PER_STEP
    here = pl.BlockSpec(memory_space=pltpu.VMEM)
    decays = pl.BlockSpec((HEADS, ROWS), lambda i, c: (0, 0))
    heads = lambda width, n=PER_STEP: pl.BlockSpec(
        (ROWS, width * n), lambda i, c: (0, c[0] * (HALF // n) + i)
    )
    theirs = lambda width: pl.BlockSpec((ROWS, width), lambda i, c: (0, (1 - c[0]) * HALF + i))
    table = pltpu.VMEM((ROWS, HEADS), f32)
    flops = 2 * HALF * ROWS * DK * DV
    slices = pltpu.VMEM((CHIPS, SLICE, 128), bf16)

    pieces = pl.BlockSpec((SLICES * PER_STEP, SLICE, 128), lambda i, c: (i, 0, 0))
    sent = pl.BlockSpec((SLICES * PER_STEP, SENT, 128), lambda i, c: (i, 0, 0))
    key_far, value_far, decay_far = far(key_vectors), far(values), far(decay)

    def chunk_states(group, out_specs, out_shape, *done):
        return call(
            state_kernel, steps, [heads(DK), heads(DV), decays] + [here] * len(done),
            out_specs, out_shape, [table], flops,
        )(group, key_far, value_far, decay_far, *done)

    theirs_state = chunk_states(other, here, slices)
    got = lax.ppermute(theirs_state, "core", swap)
    stored = pltpu.HBM((CHIPS, SLICE, 128), bf16)
    own_state, late_own, late_theirs = chunk_states(
        core, [here, pieces, pieces], [slices, stored, stored], near(theirs_state)
    )
    block_state = call(
        combine_kernel, steps, [here, here, decays, decays], sent,
        pltpu.HBM((CHIPS, SENT, 128), bf16), [pltpu.VMEM((3, HEADS, 128), f32)], flops // 8,
    )(core, near(own_state), near(got), decay_far, other_decay)
    collected = lax.all_to_all(block_state, everyone, 0, 0, tiled=True)
    their_first = lax.ppermute(late_own, "core", swap)
    own_first = lax.ppermute(late_theirs, "core", swap)

    block = lambda: pl.BlockSpec((1, ROWS, DV), lambda i, c: (i, 0, 0))
    own_within, own_gated, their_within, their_gated, reach = call(
        within_kernel, HALF,
        [heads(DK, 1), heads(DK, 1), heads(DV, 1), heads(DV, 1),
         theirs(DK), theirs(DK), theirs(DV), theirs(DV),
         pl.BlockSpec((SLICES, SLICE, 128), lambda i, c: (i, 0, 0)),
         pl.BlockSpec((SLICES, SLICE, 128), lambda i, c: (i, 0, 0)), decays, decays],
        [block() for _ in range(4)] + [pl.BlockSpec((HEADS, ROWS, 128), lambda i, c: (0, 0, 0))],
        [pltpu.HBM((HALF, ROWS, DV), f32)] * 4 + [pltpu.HBM((HEADS, ROWS, 128), f32)],
        [table, pltpu.VMEM((HEADS, ROWS), f32), table], 4 * flops,
    )(core, far(queries), key_far, value_far, far(gate_input), far(queries), key_far, value_far,
      far(gate_input), far(own_first), far(their_first), decay_far, other_decay)

    starts = pl.pallas_call(
        prefix_kernel,
        out_shape=slices,
        in_specs=[here],
        out_specs=here,
        compiler_params=pltpu.CompilerParams(vmem_limit_bytes=LIMIT * MIB),
        name="prefix",
    )(near(collected))
    start = lax.all_to_all(starts, everyone, 0, 0, tiled=True)
    their_start = lax.ppermute(start, "core", swap)

    blocks = pl.BlockSpec((PER_STEP, ROWS, DV), lambda i, c: (i, 0, 0))
    reaches = pl.BlockSpec((PER_STEP, ROWS, 128), lambda i, c: (c[0] * steps + i, 0, 0))
    specs = [heads(DK), here, blocks, blocks, reaches]
    result = shape(ROWS, HEADS * DV)
    done = call(finish_kernel, steps, specs, heads(DV), result, [], flops)(
        core, far(queries), near(start), far(own_within), far(own_gated), far(reach)
    )
    return call(
        finish_kernel, steps, specs + [pl.BlockSpec(memory_space=pl.ANY)],
        heads(DV), result, [], flops, {6: 0},
    )(other, far(queries), near(their_start), far(their_within), far(their_gated), far(reach), done)


def solution(mesh):
    mesh = Mesh(mesh.devices.reshape(4, 16, 2), ("seq", "chip", "core"))
    spec = P(("seq", "chip", "core"), None)

    return jax.shard_map(shards, mesh=mesh, in_specs=(spec,) * 5, out_specs=spec, check_vma=False)
```

time: 112 us -> 121 us (1.080)
  blocking collectives: 34.1 us -> 42 us
  waiting for transfers between devices: 17.9 us -> 23.9 us
  local copies, waits for them, and re-layouts: 3.32 us -> 0.01 us
  starting transfers between devices: 16.5 us -> 13.8 us
  Pallas kernels: 39.4 us -> 40.9 us
    all_to_all x1, blocking collectives: 34.1 us -> 42 us  [shards(): collected = lax.all_to_all(block_state, everyone, 0, 0, tiled=True)]
    all_to_all x1, waiting for transfers between devices: 17.9 us -> 23.9 us  [shards(): start = lax.all_to_all(starts, everyone, 0, 0, tiled=True)]
    all_to_all x1, starting transfers between devices: 11.3 us -> 5.53 us  [shards(): start = lax.all_to_all(starts, everyone, 0, 0, tiled=True)]
    unnamed x10 -> x2, local copies, waits for them, and re-layouts: 3.32 us -> 0.01 us
    ppermute x1 -> x2, starting transfers between devices: 0.43 us -> 2.24 us  [the longest x1 2.14 us: shards(): own_first = lax.ppermute(late_theirs, 'core', swap)]
    pallas_call x7, Pallas kernels: 39.4 us -> 40.9 us  [the longest x1 17 us: shards(): call(within_kernel, HALF, [heads(DK, 1), heads(DK, 1), heads(DV, 1), head...]
  transfers between devices with their start and end apart: 5 -> 6, of which waited for: 1 -> 1; matrix products, arithmetic and copies ran while one was open for 0% -> 0% of each run, Pallas kernels for 20% -> 22%
where the time goes in v4:
time: 121 us
  blocking collectives  42 us (35%)
  Pallas kernels  40.9 us (34%)
  waiting for transfers between devices  23.9 us (20%)
  starting transfers between devices  13.8 us (11%)
    all_to_all x1, blocking collectives, shards(): collected = lax.all_to_all(block_state, everyone, 0, 0, tiled=True)  42 us
    all_to_all x1, waiting for transfers between devices, shards(): start = lax.all_to_all(starts, everyone, 0, 0, tiled=True)  23.9 us
    pallas_call x1, Pallas kernels, shards(): call(within_kernel, HALF, [heads(DK, 1), heads(DK, 1), heads(DV, 1), head...  17 us
    pallas_call x2, Pallas kernels, chunk_states(): call(state_kernel, steps, [heads(DK), heads(DV), decays] + [here] * len(d...  7.46 us
    pallas_call x1, Pallas kernels, shards(): call(finish_kernel, steps, specs, heads(DV), result, [], flops)  5.88 us
    pallas_call x1, Pallas kernels, shards(): call(finish_kernel, steps, specs + [pl.BlockSpec(memory_space=pl.ANY)], h...  5.86 us
    all_to_all x1, starting transfers between devices, shards(): start = lax.all_to_all(starts, everyone, 0, 0, tiled=True)  5.53 us
    ppermute x1, starting transfers between devices, shards(): their_start = lax.ppermute(start, 'core', swap)  4.52 us
  transfers between devices with their start and end apart: 6, of which 1 were waited for; matrix products, arithmetic and copies ran while one was open for 0% of the time, Pallas kernels for 22%

profile of v4, /device:TPU:1, one launch (start us, length us, event | category | flops | bytes accessed | tf_op | source)
XLA Modules:
  0.0 120.6 jit_solution(1616703897302284013)
XLA Ops:
  0.0 0.0 copy-start
  0.0 3.2 %shard_map.55.refs_0_ = bf16[64,128,128]{2,1,0:T(8,128)(2,1)S(1)} custom-call(s32[1]{0:T(128)S(6)} %sub.3.group_ref, bf16[256,4096]{1,0:T(8,128)(2,1)} %refs_5_.1, bf16[256,8192]{1,0:T(8,128)(2,1)} %refs_6_.1, bf16[16,256]{1,0:T(8,128)(2,1)} %bitcast.2), custom_call_target="tpu_custom_call" | custom-call | flops 536870912 | tf_op jit(solution)/shard_map/pallas_call | solution.py:242
  3.2 1.4 %collective-permute-start = (bf16[64,128,128]{2,1,0:T(8,128)(2,1)S(1)}, bf16[64,128,128]{2,1,0:T(8,128)(2,1)S(1)}, u32[]{:S(2)}, u32[]{:S(2)}) collective-permute-start(bf16[64,128,128]{2,1,0:T(8,128)(2,1)S(1)} %shard_map.55.refs_0_), channel_id=1, source_target_pairs={{0,1},{1,0},{2,3},{3,2},{4,5},{5,4},{6,7},{7,6},{8,9},{9,8},{10,11... | collective-permute-start | bytes 6291464 | tf_op jit(solution)/shard_map/ppermute | solution.py:248
  4.7 0.0 copy-done
  4.7 0.1 collective-permute-start.1
  4.8 4.2 %shard_map.56 = (bf16[64,128,128]{2,1,0:T(8,128)(2,1)S(1)}, bf16[64,128,128]{2,1,0:T(8,128)(2,1)}, bf16[64,128,128]{2,1,0:T(8,128)(2,1)}) custom-call(s32[1]{0:T(128)} %bitcast.group_ref.core_ref, bf16[256,4096]{1,0:T(8,128)(2,1)} %refs_5_.1, bf16[256,8192]{1,0:T(8,128)(2,1)} %refs_6_.1, bf16[16,256]{1,0:T(8,128)(2,1)} %bitcast.3, ...), custom_call_target="tpu_custom_call" | custom-call | flops 536870912 | tf_op jit(solution)/shard_map/pallas_call | solution.py:242
  9.0 0.0 collective-permute-done.1.other_ref.refs_11_
  9.0 0.0 collective-permute-done.got_ref
  9.0 2.8 %shard_map.57 = bf16[64,136,128]{2,1,0:T(8,128)(2,1)} custom-call(s32[1]{0:T(128)} %bitcast.group_ref.core_ref, bf16[64,128,128]{2,1,0:T(8,128)(2,1)S(1)} %get-tuple-element.13.own_ref, bf16[64,128,128]{2,1,0:T(8,128)(2,1)S(1)} %collective-permute-done.got_ref, bf16[16,256]{1,0:T(8,128)(2,1)} %bitcast.4, ...), custom_call_target="tpu_custom_call" | custom-call | flops 67108864 | tf_op jit(solution)/shard_map/pallas_call | solution.py:253
  11.9 42.0 %all_to_all.10.in_ref = bf16[64,136,128]{2,1,0:T(8,128)(2,1)S(1)} all-to-all(bf16[64,136,128]{2,1,0:T(8,128)(2,1)} %shard_map.57), channel_id=1, replica_groups=mesh['seq'=4,'chip'=16,'core'=2] {'seq','chip'}, dimensions={0} | all-to-all | bytes 4456448 | tf_op jit(solution)/shard_map/all_to_all | solution.py:257
  53.8 1.8 %prefix.1 = bf16[64,128,128]{2,1,0:T(8,128)(2,1)} custom-call(bf16[64,136,128]{2,1,0:T(8,128)(2,1)S(1)} %all_to_all.10.in_ref), custom_call_target="tpu_custom_call" | custom-call | tf_op jit(solution)/shard_map/prefix/pallas_call | solution.py:274
  55.7 5.5 %all-to-all-start.1 = ((bf16[64,128,128]{2,1,0:T(8,128)(2,1)}), bf16[64,128,128]{2,1,0:T(8,128)(2,1)S(1)}, u32[]{:S(2)}, u32[]{:S(2)}) async-start(bf16[64,128,128]{2,1,0:T(8,128)(2,1)} %prefix.1), calls=%async_computation.1 | async-start | bytes 4194304 | tf_op jit(solution)/shard_map/all_to_all | solution.py:282
  61.2 2.1 %collective-permute-start.3 = (bf16[64,128,128]{2,1,0:T(8,128)(2,1)}, bf16[64,128,128]{2,1,0:T(8,128)(2,1)}, u32[]{:S(2)}, u32[]{:S(2)}) collective-permute-start(bf16[64,128,128]{2,1,0:T(8,128)(2,1)} %get-tuple-element.14), channel_id=1, source_target_pairs={{0,1},{1,0},{2,3},{3,2},{4,5},{5,4},{6,7},{7,6},{8,9},{9,8},{10,11... | collective-permute-start | bytes 6291464 | tf_op jit(solution)/shard_map/ppermute | solution.py:259
  63.3 0.1 collective-permute-start.4
  63.4 23.9 %all-to-all-done.1.start_ref = bf16[64,128,128]{2,1,0:T(8,128)(2,1)S(1)} async-done(((bf16[64,128,128]{2,1,0:T(8,128)(2,1)}), bf16[64,128,128]{2,1,0:T(8,128)(2,1)S(1)}, u32[]{:S(2)}, u32[]{:S(2)}) %all-to-all-start.1) | async-done | bytes 2097184 | tf_op jit(solution)/shard_map/all_to_all | solution.py:282
  87.3 4.5 %collective-permute-start.2 = (bf16[64,128,128]{2,1,0:T(8,128)(2,1)S(1)}, bf16[64,128,128]{2,1,0:T(8,128)(2,1)S(1)}, u32[]{:S(2)}, u32[]{:S(2)}) collective-permute-start(bf16[64,128,128]{2,1,0:T(8,128)(2,1)S(1)} %all-to-all-done.1.start_ref), channel_id=1, source_target_pairs={{0,1},{1,0},{2,3},{3,2},{4,5},{5,4},{6,7},{7,6},{8,9},{9,8},{10,11... | collective-permute-start | bytes 6291464 | tf_op jit(solution)/shard_map/ppermute | solution.py:283
  91.8 0.0 collective-permute-done.3.refs_8_
  91.8 0.0 collective-permute-done.4.refs_9_
  91.8 17.0 %shard_map.58 = (f32[8,256,512]{2,1,0:T(8,128)}, f32[8,256,512]{2,1,0:T(8,128)}, f32[8,256,512]{2,1,0:T(8,128)}, f32[8,256,512]{2,1,0:T(8,128)}, f32[16,256,128]{2,1,0:T(8,128)}) custom-call(s32[1]{0:T(128)} %bitcast.group_ref.core_ref, bf16[256,4096]{1,0:T(8,128)(2,1)} %query_ref.3, bf16[256,4096]{1,0:T(8,128)(2,1)} %refs_5_.1, bf16[256,8192]{1,0:T(8,128)(2,1)} %refs_6_.1, ...), custom_call_target="tpu_custom_call" | custom-call | flops 2147483648 | tf_op jit(solution)/shard_map/pallas_call | solution.py:262
  108.8 5.9 %shard_map.59.rest_0_ = bf16[256,8192]{1,0:T(8,128)(2,1)} custom-call(s32[1]{0:T(128)} %bitcast.group_ref.core_ref, bf16[256,4096]{1,0:T(8,128)(2,1)} %query_ref.3, bf16[64,128,128]{2,1,0:T(8,128)(2,1)S(1)} %all-to-all-done.1.start_ref, f32[8,256,512]{2,1,0:T(8,128)} %get-tuple-element.19.within_ref, f32[8,256,512]{2,1,0:T(8,128)} %get-tuple-element.20.gated_ref, ...), custom_call_target="tpu_custom_call" | custom-call | flops 536870912 | tf_op jit(solution)/shard_map/pallas_call | solution.py:289
  114.7 0.0 collective-permute-done.2.start_ref
  114.7 5.9 %shard_map.60 = bf16[256,8192]{1,0:T(8,128)(2,1)} custom-call(s32[1]{0:T(128)S(6)} %sub.3.group_ref, bf16[256,4096]{1,0:T(8,128)(2,1)} %query_ref.3, bf16[64,128,128]{2,1,0:T(8,128)(2,1)S(1)} %collective-permute-done.2.start_ref, f32[8,256,512]{2,1,0:T(8,128)} %get-tuple-element.16.within_ref, ...), custom_call_target="tpu_custom_call", output_to_operand_aliasing={{}: (6, {})} | custom-call | flops 536870912 | tf_op jit(solution)/shard_map/pallas_call | solution.py:292
Async XLA Ops:
  0.0 4.7 %copy-start = (bf16[256,16]{0,1:T(8,128)(2,1)S(1)}, bf16[256,16]{0,1:T(8,128)(2,1)}, u32[]{:S(2)}) copy-start(bf16[256,16]{0,1:T(8,128)(2,1)} %param.8) | copy-start | bytes 24580
  3.2 5.8 %collective-permute-start = (bf16[64,128,128]{2,1,0:T(8,128)(2,1)S(1)}, bf16[64,128,128]{2,1,0:T(8,128)(2,1)S(1)}, u32[]{:S(2)}, u32[]{:S(2)}) collective-permute-start(bf16[64,128,128]{2,1,0:T(8,128)(2,1)S(1)} %shard_map.55.refs_0_), channel_id=1, source_target_pairs={{0,1},{1,0},{2,3},{3,2},{4,5},{5,4},{6,7},{7,6},{8,9},{9,8},{10,11... | collective-permute-start | bytes 6291464 | tf_op jit(solution)/shard_map/ppermute | solution.py:248
  4.7 4.3 %collective-permute-start.1 = (bf16[16,256]{1,0:T(8,128)(2,1)S(1)}, bf16[16,256]{1,0:T(8,128)(2,1)S(1)}, u32[]{:S(2)}, u32[]{:S(2)}) collective-permute-start(bf16[16,256]{1,0:T(8,128)(2,1)S(1)} %bitcast.6), channel_id=1, source_target_pairs={{0,1},{1,0},{2,3},{3,2},{4,5},{5,4},{6,7},{7,6},{8,9},{9,8},{10,11... | collective-permute-start | bytes 24584 | tf_op jit(solution)/shard_map/ppermute | solution.py:224
  55.7 31.6 %all-to-all-start.1 = ((bf16[64,128,128]{2,1,0:T(8,128)(2,1)}), bf16[64,128,128]{2,1,0:T(8,128)(2,1)S(1)}, u32[]{:S(2)}, u32[]{:S(2)}) async-start(bf16[64,128,128]{2,1,0:T(8,128)(2,1)} %prefix.1), calls=%async_computation.1 | async-start | bytes 4194304 | tf_op jit(solution)/shard_map/all_to_all | solution.py:282
  61.2 30.6 %collective-permute-start.3 = (bf16[64,128,128]{2,1,0:T(8,128)(2,1)}, bf16[64,128,128]{2,1,0:T(8,128)(2,1)}, u32[]{:S(2)}, u32[]{:S(2)}) collective-permute-start(bf16[64,128,128]{2,1,0:T(8,128)(2,1)} %get-tuple-element.14), channel_id=1, source_target_pairs={{0,1},{1,0},{2,3},{3,2},{4,5},{5,4},{6,7},{7,6},{8,9},{9,8},{10,11... | collective-permute-start | bytes 6291464 | tf_op jit(solution)/shard_map/ppermute | solution.py:259
  63.3 28.5 %collective-permute-start.4 = (bf16[64,128,128]{2,1,0:T(8,128)(2,1)}, bf16[64,128,128]{2,1,0:T(8,128)(2,1)}, u32[]{:S(2)}, u32[]{:S(2)}) collective-permute-start(bf16[64,128,128]{2,1,0:T(8,128)(2,1)} %get-tuple-element.15), channel_id=1, source_target_pairs={{0,1},{1,0},{2,3},{3,2},{4,5},{5,4},{6,7},{7,6},{8,9},{9,8},{10,11... | collective-permute-start | bytes 6291464 | tf_op jit(solution)/shard_map/ppermute | solution.py:258
  87.3 27.4 %collective-permute-start.2 = (bf16[64,128,128]{2,1,0:T(8,128)(2,1)S(1)}, bf16[64,128,128]{2,1,0:T(8,128)(2,1)S(1)}, u32[]{:S(2)}, u32[]{:S(2)}) collective-permute-start(bf16[64,128,128]{2,1,0:T(8,128)(2,1)S(1)} %all-to-all-done.1.start_ref), channel_id=1, source_target_pairs={{0,1},{1,0},{2,3},{3,2},{4,5},{5,4},{6,7},{7,6},{8,9},{9,8},{10,11... | collective-permute-start | bytes 6291464 | tf_op jit(solution)/shard_map/ppermute | solution.py:283

commit v5 on v4

v5 whole, which is shorter than its diff:
```python
import jax
import jax.numpy as jnp
from jax import lax
from jax.experimental import pallas as pl
from jax.experimental.pallas import tpu as pltpu
from jax.sharding import Mesh, PartitionSpec as P


HEADS = 16
DK = 256
DV = 512
ROWS = 256
HALF = HEADS // 2
CHIPS = 64
SLICES = CHIPS // HALF
PIECE = DK // SLICES
TILES = DV // 128
SLICE = PIECE * TILES
SENT = SLICE + 8
MIB = 2**20
LIMIT = 20

f32 = jnp.float32
bf16 = jnp.bfloat16


def triangle():
    rows = lax.broadcasted_iota(jnp.int32, (ROWS, ROWS), 0)
    cols = lax.broadcasted_iota(jnp.int32, (ROWS, ROWS), 1)
    return rows >= cols


def running_of(decay):
    ones = triangle().astype(f32).astype(bf16)
    return lax.dot_general(ones, decay, (((1,), (1,)), ((), ())), preferred_element_type=f32)


def running_rows(decay):
    ones = triangle().astype(f32).astype(bf16)
    return lax.dot_general(decay, ones, (((1,), (1,)), ((), ())), preferred_element_type=f32)


def column(table, head):
    lanes = lax.broadcasted_iota(jnp.int32, table.shape, 1)
    return jnp.sum(jnp.where(lanes == head, table, 0.0), axis=1, keepdims=True)


def put_slices(ref, at, state):
    for o in range(SLICES):
        for t in range(TILES):
            ref[at * SLICES + o, t * PIECE : (t + 1) * PIECE, :] = state[
                o * PIECE : (o + 1) * PIECE, t * 128 : (t + 1) * 128
            ]


def get_slices(ref, at):
    cols = [
        ref[pl.ds(at * SLICES, SLICES), t * PIECE : (t + 1) * PIECE, :].reshape(DK, 128)
        for t in range(TILES)
    ]
    return jnp.concatenate(cols, axis=1)


def columns_of(ref, head, width):
    return ref.at[:, pl.ds(pl.multiple_of(head * width, width), width)]


def start_all(copies):
    for copy in copies:
        copy.start()
    return copies


def states_into(out_ref, group, key_ref, value_ref, run, key_buf, value_buf, sems, done=None):
    copies = []
    for n in range(HALF):
        head = group * HALF + n
        copies.append(start_all((
            pltpu.make_async_copy(columns_of(key_ref, head, DK), key_buf.at[n], sems.at[0, n]),
            pltpu.make_async_copy(columns_of(value_ref, head, DV), value_buf.at[n], sems.at[1, n]),
        )))
    fades = jnp.exp(run[ROWS - 1 : ROWS, :] - run)
    for n in range(HALF):
        fade = column(fades, group * HALF + n)
        for copy in copies[n]:
            copy.wait()
        faded = (key_buf[n].astype(f32) * fade).astype(bf16)
        state = lax.dot_general(
            faded, value_buf[n], (((0,), (0,)), ((), ())), preferred_element_type=f32
        )
        put_slices(out_ref, n, state.astype(bf16))
        if done is not None:
            done(n)


def totals_of(decay):
    ones = jnp.ones((128, ROWS), f32).astype(bf16)
    return lax.dot_general(decay, ones, (((1,), (1,)), ((), ())), preferred_element_type=f32)


def thirds_of(value):
    high = value.astype(bf16).astype(f32)
    rest = value - high
    middle = rest.astype(bf16).astype(f32)
    return high, middle, rest - middle


def theirs_kernel(group_ref, key_ref, value_ref, decay_ref, out_ref, key_buf, value_buf, sems):
    run = running_of(decay_ref[...])
    states_into(out_ref, group_ref[0], key_ref, value_ref, run, key_buf, value_buf, sems)
    for k, third in enumerate(thirds_of(totals_of(decay_ref[...]))):
        out_ref[CHIPS, k * HEADS : (k + 1) * HEADS, :] = third.astype(bf16)


def own_kernel(
    group_ref, key_ref, value_ref, decay_ref, theirs_ref,
    out_ref, total_ref, own_copy_ref, theirs_copy_ref, key_buf, value_buf, sems, out_sems,
):
    theirs_copy = pltpu.make_async_copy(
        theirs_ref.at[pl.ds(0, CHIPS)], theirs_copy_ref, out_sems.at[HALF]
    )
    theirs_copy.start()
    decay = decay_ref[...]
    total_ref[...] = totals_of(decay)
    copies = []

    def done(n):
        rows = pl.ds(n * SLICES, SLICES)
        copies.extend(start_all((
            pltpu.make_async_copy(out_ref.at[rows], own_copy_ref.at[rows], out_sems.at[n]),
        )))

    states_into(
        out_ref, group_ref[0], key_ref, value_ref, running_of(decay), key_buf, value_buf, sems, done
    )
    theirs_copy.wait()
    for copy in copies:
        copy.wait()


def combine_kernel(core_ref, own_ref, got_ref, total_ref, out_ref, buf_ref, rate_ref, sems):
    is_first = core_ref[0] == 0
    total = total_ref[...]
    thirds = [got_ref[CHIPS, k * HEADS : (k + 1) * HEADS, :].astype(f32) for k in range(3)]
    other = thirds[0] + thirds[1] + thirds[2]
    rate_ref[0] = jnp.exp(jnp.where(is_first, other, 0.0))
    rate_ref[1] = jnp.exp(jnp.where(is_first, 0.0, total))
    rate_ref[2] = jnp.exp(total + other)
    rows = lax.broadcasted_iota(jnp.int32, (8, 128), 0)
    copies = []
    for n in range(HALF):
        head = pl.ds(core_ref[0] * HALF + n, 1)
        own_rate = rate_ref[0, head, :]
        got_rate = rate_ref[1, head, :]
        high, middle, low = thirds_of(rate_ref[2, head, :])
        parts = jnp.where(rows == 0, high, jnp.where(rows == 1, middle, low))
        parts = parts.astype(bf16)
        for o in range(n * SLICES, (n + 1) * SLICES):
            both = own_ref[o].astype(f32) * own_rate + got_ref[o].astype(f32) * got_rate
            buf_ref[o, :SLICE, :] = both.astype(bf16)
            buf_ref[o, SLICE:SENT, :] = parts
        block = pl.ds(n * SLICES, SLICES)
        copies.extend(start_all((
            pltpu.make_async_copy(buf_ref.at[block], out_ref.at[block], sems.at[n]),
        )))
    for copy in copies:
        copy.wait()


def within_kernel(core_ref, *refs):
    own, theirs, (got_ref, first_ref, decay_ref, other_ref) = refs[0:3], refs[3:6], refs[6:10]
    outs, (reach_out, run_ref, rows_ref, reach_ref) = refs[10:12], refs[12:]
    step = pl.program_id(0)
    core = core_ref[0]

    @pl.when(step == 0)
    def _():
        run = running_of(decay_ref[...])
        run_ref[...] = run
        rows_ref[...] = running_rows(decay_ref[...])
        other = running_of(other_ref[...])[ROWS - 1 : ROWS, :]
        reach = jnp.exp(run + jnp.where(core == 0, 0.0, other))
        reach_out[...] = reach
        reach_ref[...] = jnp.where(core == 0, 0.0, jnp.exp(run))

    for group, ins, state_ref, out_ref in (
        (core, own, got_ref, outs[0]),
        (1 - core, theirs, first_ref, outs[1]),
    ):
        query_ref, key_ref, value_ref = ins
        head = group * HALF + step
        query = query_ref[...]
        scores = lax.dot_general(
            query, key_ref[...], (((1,), (1,)), ((), ())), preferred_element_type=f32
        )
        spread = column(run_ref[...], head) - rows_ref[pl.ds(head, 1), :]
        factor = jnp.exp(jnp.where(triangle(), spread, -jnp.inf))
        weights = (scores * factor).astype(bf16)
        local = jnp.dot(weights, value_ref[...], preferred_element_type=f32)
        before = jnp.dot(query, get_slices(state_ref, 0), preferred_element_type=f32)
        out_ref[0] = local + before * column(reach_ref[...], head)


def prefix_kernel(in_ref, out_ref):
    state = jnp.zeros((SLICE, 128), f32)
    for b in range(CHIPS):
        parts = in_ref[b, SLICE:SENT, :].astype(f32)
        damping = parts[0:1] + parts[1:2] + parts[2:3]
        out_ref[b] = state.astype(bf16)
        state = damping * state + in_ref[b, :SLICE, :].astype(f32)


def finish_kernel(group_ref, start_ref, reach_ref, query_ref, within_ref, gate_ref, *rest):
    out_ref, query_buf, within_buf, gate_buf, out_buf, sems = rest[-6:]
    copies, writes = [], []
    for n in range(HALF):
        head = group_ref[0] * HALF + n
        copies.append(start_all((
            pltpu.make_async_copy(columns_of(query_ref, head, DK), query_buf.at[n], sems.at[0, n]),
            pltpu.make_async_copy(within_ref.at[n], within_buf.at[n], sems.at[1, n]),
            pltpu.make_async_copy(columns_of(gate_ref, head, DV), gate_buf.at[n], sems.at[2, n]),
        )))
    for n in range(HALF):
        head = group_ref[0] * HALF + n
        reach = column(reach_ref[...], head)
        for copy in copies[n]:
            copy.wait()
        across = jnp.dot(query_buf[n], get_slices(start_ref, n), preferred_element_type=f32)
        retained = within_buf[n] + across * reach
        average = jnp.mean(retained, axis=1, keepdims=True)
        centered = retained - average
        variance = jnp.mean(centered * centered, axis=1, keepdims=True)
        normed = centered * lax.rsqrt(variance + 1e-06)
        gate = gate_buf[n].astype(f32)
        out_buf[n] = (gate / (1.0 + jnp.exp(-gate)) * normed).astype(bf16)
        writes.extend(start_all((
            pltpu.make_async_copy(out_buf.at[n], columns_of(out_ref, head, DV), sems.at[3, n]),
        )))
    for copy in writes:
        copy.wait()


def call(kernel, grid, in_specs, out_specs, out_shape, scratch, flops, aliases=None):
    return pl.pallas_call(
        kernel,
        out_shape=out_shape,
        grid_spec=pltpu.PrefetchScalarGridSpec(
            num_scalar_prefetch=1,
            grid=(grid,),
            in_specs=in_specs,
            out_specs=out_specs,
            scratch_shapes=scratch,
        ),
        compiler_params=pltpu.CompilerParams(
            dimension_semantics=("arbitrary",), vmem_limit_bytes=LIMIT * MIB
        ),
        cost_estimate=pl.CostEstimate(flops=flops, transcendentals=0, bytes_accessed=0),
        input_output_aliases=aliases or {},
    )


def far(value):
    return pltpu.with_memory_space_constraint(value, pltpu.HBM)


def near(value):
    return pltpu.with_memory_space_constraint(value, pltpu.VMEM)


def shards(queries, key_vectors, values, decay_log, gate_input):
    core = lax.axis_index("core").astype(jnp.int32).reshape(1)
    other = 1 - core
    swap = [(0, 1), (1, 0)]
    everyone = ("seq", "chip")
    decay = decay_log.T

    here = pl.BlockSpec(memory_space=pltpu.VMEM)
    decays = pl.BlockSpec((HEADS, ROWS), lambda i, c: (0, 0))
    heads = lambda width: pl.BlockSpec((ROWS, width), lambda i, c: (0, c[0] * HALF + i))
    theirs = lambda width: pl.BlockSpec((ROWS, width), lambda i, c: (0, (1 - c[0]) * HALF + i))
    table = pltpu.VMEM((ROWS, HEADS), f32)
    flops = 2 * HALF * ROWS * DK * DV
    slices = pltpu.VMEM((CHIPS, SLICE, 128), bf16)

    away = pl.BlockSpec(memory_space=pl.ANY)
    key_far, value_far, decay_far = far(key_vectors), far(values), far(decay)
    stored = pltpu.HBM((CHIPS, SLICE, 128), bf16)
    buffers = [
        pltpu.VMEM((HALF, ROWS, DK), bf16), pltpu.VMEM((HALF, ROWS, DV), bf16),
        pltpu.SemaphoreType.DMA((2, HALF)),
    ]
    theirs_state = call(
        theirs_kernel, 1, [away, away, decays], here,
        pltpu.VMEM((CHIPS + 1, SLICE, 128), bf16), buffers, flops
    )(other, key_far, value_far, decay_far)
    got = lax.ppermute(theirs_state, "core", swap)
    own_state, totals, late_own, late_theirs = call(
        own_kernel, 1, [away, away, decays, here], [here, here, away, away],
        [slices, pltpu.VMEM((HEADS, 128), f32), stored, stored],
        buffers + [pltpu.SemaphoreType.DMA((HALF + 1,))], flops,
    )(core, key_far, value_far, decay_far, near(theirs_state))
    block_state = call(
        combine_kernel, 1, [here, here, here], away,
        pltpu.HBM((CHIPS, SENT, 128), bf16),
        [
            pltpu.VMEM((CHIPS, SENT, 128), bf16), pltpu.VMEM((3, HEADS, 128), f32),
            pltpu.SemaphoreType.DMA((HALF,)),
        ], flops // 8,
    )(core, near(own_state), near(got), near(totals))
    collected = lax.all_to_all(block_state, everyone, 0, 0, tiled=True)
    their_first = lax.ppermute(late_own, "core", swap)
    own_first = lax.ppermute(late_theirs, "core", swap)
    other_decay = lax.ppermute(decay, "core", swap)

    block = lambda: pl.BlockSpec((1, ROWS, DV), lambda i, c: (i, 0, 0))
    own_within, their_within, reach = call(
        within_kernel, HALF,
        [heads(DK), heads(DK), heads(DV), theirs(DK), theirs(DK), theirs(DV),
         pl.BlockSpec((SLICES, SLICE, 128), lambda i, c: (i, 0, 0)),
         pl.BlockSpec((SLICES, SLICE, 128), lambda i, c: (i, 0, 0)), decays, decays],
        [block(), block(), pl.BlockSpec((ROWS, HEADS), lambda i, c: (0, 0))],
        [pltpu.HBM((HALF, ROWS, DV), f32)] * 2 + [pltpu.HBM((ROWS, HEADS), f32)],
        [table, pltpu.VMEM((HEADS, ROWS), f32), table], 4 * flops,
    )(core, far(queries), key_far, value_far, far(queries), key_far, value_far,
      far(own_first), far(their_first), decay_far, other_decay)

    starts = pl.pallas_call(
        prefix_kernel,
        out_shape=slices,
        in_specs=[here],
        out_specs=here,
        compiler_params=pltpu.CompilerParams(vmem_limit_bytes=LIMIT * MIB),
        name="prefix",
    )(near(collected))
    start = lax.all_to_all(starts, everyone, 0, 0, tiled=True)
    their_start = lax.ppermute(start, "core", swap)

    specs = [here, pl.BlockSpec((ROWS, HEADS), lambda i, c: (0, 0)), away, away, away]
    result = pltpu.HBM((ROWS, HEADS * DV), bf16)
    scratch = [
        pltpu.VMEM((HALF, ROWS, DK), bf16), pltpu.VMEM((HALF, ROWS, DV), f32),
        pltpu.VMEM((HALF, ROWS, DV), bf16), pltpu.VMEM((HALF, ROWS, DV), bf16),
        pltpu.SemaphoreType.DMA((4, HALF)),
    ]
    done = call(finish_kernel, 1, specs, away, result, scratch, flops)(
        core, near(start), far(reach), far(queries), far(own_within), far(gate_input)
    )
    return call(
        finish_kernel, 1, specs + [away], away, result, scratch, flops, {6: 0},
    )(other, near(their_start), far(reach), far(queries), far(their_within), far(gate_input), done)


def solution(mesh):
    mesh = Mesh(mesh.devices.reshape(4, 16, 2), ("seq", "chip", "core"))
    spec = P(("seq", "chip", "core"), None)

    return jax.shard_map(shards, mesh=mesh, in_specs=(spec,) * 5, out_specs=spec, check_vma=False)
```

time: 121 us -> 123 us (1.017)
  waiting for transfers between devices: 23.9 us -> 28.7 us
  Pallas kernels: 40.9 us -> 36.8 us
  local copies, waits for them, and re-layouts: 0.01 us -> 1.32 us
    ppermute x1, waiting for transfers between devices: 0.01 us -> 3.79 us  [shards(): other_decay = lax.ppermute(decay, 'core', swap)]
    pallas_call x6, Pallas kernels: 39 us -> 36.3 us  [the longest x1 11.7 us: shards(): call(within_kernel, HALF, [heads(DK), heads(DK), heads(DV), theirs(DK), t...]
    pallas_call x1, Pallas kernels: 1.84 us -> 0.52 us  [shards(): pl.pallas_call(prefix_kernel, out_shape=slices, in_specs=[here], out_spec...]
    unnamed x2 -> x4, local copies, waits for them, and re-layouts: 0.01 us -> 1.32 us
  transfers between devices with their start and end apart: 6 -> 6, of which waited for: 1 -> 2; matrix products, arithmetic and copies ran while one was open for 0% -> 0% of each run, Pallas kernels for 22% -> 19%
where the time goes in v5:
time: 123 us; the launch traced here: 122 us
  blocking collectives  42.2 us (34%)
  Pallas kernels  36.8 us (30%)
  waiting for transfers between devices  28.7 us (23%)
  starting transfers between devices  13 us (11%)
  local copies, waits for them, and re-layouts  1.32 us (1%)
    all_to_all x1, blocking collectives, shards(): collected = lax.all_to_all(block_state, everyone, 0, 0, tiled=True)  42.2 us
    all_to_all x1, waiting for transfers between devices, shards(): start = lax.all_to_all(starts, everyone, 0, 0, tiled=True)  24.9 us
    pallas_call x1, Pallas kernels, shards(): call(within_kernel, HALF, [heads(DK), heads(DK), heads(DV), theirs(DK), t...  11.7 us
    pallas_call x1, Pallas kernels, shards(): call(finish_kernel, 1, specs + [away], away, result, scratch, flops, {6: 0})  6.98 us
    pallas_call x1, Pallas kernels, shards(): call(finish_kernel, 1, specs, away, result, scratch, flops)  6.98 us
    all_to_all x1, starting transfers between devices, shards(): start = lax.all_to_all(starts, everyone, 0, 0, tiled=True)  5.79 us
    pallas_call x1, Pallas kernels, shards(): call(own_kernel, 1, [away, away, decays, here], [here, here, away, away],...  5.1 us
    ppermute x1, starting transfers between devices, shards(): their_start = lax.ppermute(start, 'core', swap)  3.98 us
  transfers between devices with their start and end apart: 6, of which 2 were waited for; matrix products, arithmetic and copies ran while one was open for 0% of the time, Pallas kernels for 19%

profile of v5, /device:TPU:1, one launch (start us, length us, event | category | flops | bytes accessed | tf_op | source)
XLA Modules:
  0.0 122.3 jit_solution(3479487094657085386)
XLA Ops:
  0.0 4.0 %shard_map.55.theirs_ref = bf16[65,128,128]{2,1,0:T(8,128)(2,1)S(1)} custom-call(s32[1]{0:T(128)S(6)} %sub.3.group_ref, bf16[256,4096]{1,0:T(8,128)(2,1)} %refs_4_.1, bf16[256,8192]{1,0:T(8,128)(2,1)} %refs_5_.1, bf16[16,256]{1,0:T(8,128)(2,1)} %bitcast.2), custom_call_target="tpu_custom_call" | custom-call | flops 536870912 | tf_op jit(solution)/shard_map/pallas_call | solution.py:292
  4.0 1.5 %collective-permute-start = (bf16[65,128,128]{2,1,0:T(8,128)(2,1)S(1)}, bf16[65,128,128]{2,1,0:T(8,128)(2,1)S(1)}, u32[]{:S(2)}, u32[]{:S(2)}) collective-permute-start(bf16[65,128,128]{2,1,0:T(8,128)(2,1)S(1)} %shard_map.55.theirs_ref), channel_id=1, source_target_pairs={{0,1},{1,0},{2,3},{3,2},{4,5},{5,4},{6,7},{7,6},{8,9},{9,8},{10,11... | collective-permute-start | bytes 6389768 | tf_op jit(solution)/shard_map/ppermute | solution.py:296
  5.4 5.1 %shard_map.56 = (bf16[64,128,128]{2,1,0:T(8,128)(2,1)S(1)}, f32[16,128]{1,0:T(8,128)S(1)}, bf16[64,128,128]{2,1,0:T(8,128)(2,1)}, bf16[64,128,128]{2,1,0:T(8,128)(2,1)}) custom-call(s32[1]{0:T(128)} %bitcast.group_ref.core_ref, bf16[256,4096]{1,0:T(8,128)(2,1)} %refs_4_.1, bf16[256,8192]{1,0:T(8,128)(2,1)} %refs_5_.1, bf16[16,256]{1,0:T(8,128)(2,1)} %bitcast.3, ...), custom_call_target="tpu_custom_call" | custom-call | flops 536870912 | tf_op jit(solution)/shard_map/pallas_call | solution.py:297
  10.5 0.0 collective-permute-done.got_ref
  10.5 1.6 %shard_map.57 = bf16[64,136,128]{2,1,0:T(8,128)(2,1)} custom-call(s32[1]{0:T(128)} %bitcast.group_ref.core_ref, bf16[64,128,128]{2,1,0:T(8,128)(2,1)S(1)} %get-tuple-element.12.own_ref, bf16[65,128,128]{2,1,0:T(8,128)(2,1)S(1)} %collective-permute-done.got_ref, f32[16,128]{1,0:T(8,128)S(1)} %get-tuple-element.13.total_ref), custom_call_target="tpu_custom_call" | custom-call | flops 67108864 | tf_op jit(solution)/shard_map/pallas_call | solution.py:302
  12.1 42.2 %all_to_all.10.in_ref = bf16[64,136,128]{2,1,0:T(8,128)(2,1)S(1)} all-to-all(bf16[64,136,128]{2,1,0:T(8,128)(2,1)} %shard_map.57), channel_id=1, replica_groups=mesh['seq'=4,'chip'=16,'core'=2] {'seq','chip'}, dimensions={0} | all-to-all | bytes 4456448 | tf_op jit(solution)/shard_map/all_to_all | solution.py:310
  54.4 0.5 prefix.1
  54.9 0.0 copy-start
  54.9 1.3 %copy-done = bf16[64,128,128]{2,1,0:T(8,128)(2,1)} copy-done((bf16[64,128,128]{2,1,0:T(8,128)(2,1)}, bf16[64,128,128]{2,1,0:T(8,128)(2,1)S(1)}, u32[]{:S(2)}) %copy-start) | copy-done | bytes 2097176
  56.2 0.0 copy-start.1
  56.2 5.8 %all-to-all-start.1 = ((bf16[64,128,128]{2,1,0:T(8,128)(2,1)}), bf16[64,128,128]{2,1,0:T(8,128)(2,1)S(1)}, u32[]{:S(2)}, u32[]{:S(2)}) async-start(bf16[64,128,128]{2,1,0:T(8,128)(2,1)} %copy-done), calls=%async_computation.1 | async-start | bytes 4194304 | tf_op jit(solution)/shard_map/all_to_all | solution.py:335
  62.0 1.7 %collective-permute-start.2 = (bf16[64,128,128]{2,1,0:T(8,128)(2,1)}, bf16[64,128,128]{2,1,0:T(8,128)(2,1)}, u32[]{:S(2)}, u32[]{:S(2)}) collective-permute-start(bf16[64,128,128]{2,1,0:T(8,128)(2,1)} %get-tuple-element.14), channel_id=1, source_target_pairs={{0,1},{1,0},{2,3},{3,2},{4,5},{5,4},{6,7},{7,6},{8,9},{9,8},{10,11... | collective-permute-start | bytes 6291464 | tf_op jit(solution)/shard_map/ppermute | solution.py:312
  63.7 0.1 collective-permute-start.3
  63.8 24.9 %all-to-all-done.1.start_ref = bf16[64,128,128]{2,1,0:T(8,128)(2,1)S(1)} async-done(((bf16[64,128,128]{2,1,0:T(8,128)(2,1)}), bf16[64,128,128]{2,1,0:T(8,128)(2,1)S(1)}, u32[]{:S(2)}, u32[]{:S(2)}) %all-to-all-start.1) | async-done | bytes 2097184 | tf_op jit(solution)/shard_map/all_to_all | solution.py:335
  88.7 4.0 %collective-permute-start.1 = (bf16[64,128,128]{2,1,0:T(8,128)(2,1)S(1)}, bf16[64,128,128]{2,1,0:T(8,128)(2,1)S(1)}, u32[]{:S(2)}, u32[]{:S(2)}) collective-permute-start(bf16[64,128,128]{2,1,0:T(8,128)(2,1)S(1)} %all-to-all-done.1.start_ref), channel_id=1, source_target_pairs={{0,1},{1,0},{2,3},{3,2},{4,5},{5,4},{6,7},{7,6},{8,9},{9,8},{10,11... | collective-permute-start | bytes 6291464 | tf_op jit(solution)/shard_map/ppermute | solution.py:336
  92.7 0.0 copy-done.1
  92.7 0.0 collective-permute-start.4
  92.7 3.8 %collective-permute-done.4.refs_9_ = bf16[16,256]{1,0:T(8,128)(2,1)S(1)} collective-permute-done((bf16[16,256]{1,0:T(8,128)(2,1)S(1)}, bf16[16,256]{1,0:T(8,128)(2,1)S(1)}, u32[]{:S(2)}, u32[]{:S(2)}) %collective-permute-start.4) | collective-permute-done | bytes 8224 | tf_op jit(solution)/shard_map/ppermute | solution.py:313
  96.5 0.0 collective-permute-done.2.refs_6_
  96.5 0.0 collective-permute-done.3.refs_7_
  96.5 11.7 %shard_map.58 = (f32[8,256,512]{2,1,0:T(8,128)}, f32[8,256,512]{2,1,0:T(8,128)}, f32[256,16]{1,0:T(8,128)}) custom-call(s32[1]{0:T(128)} %bitcast.group_ref.core_ref, bf16[256,4096]{1,0:T(8,128)(2,1)} %query_ref.3, bf16[256,4096]{1,0:T(8,128)(2,1)} %refs_4_.1, bf16[256,8192]{1,0:T(8,128)(2,1)} %refs_5_.1, bf16[256,4096]{1,0:T(8,128)(2,1)} %query_ref.3, ...), custom_call_target="tpu_custom_call" | custom-call | flops 2147483648 | tf_op jit(solution)/shard_map/pallas_call | solution.py:316
  108.2 7.0 %shard_map.59.rest_0_ = bf16[256,8192]{1,0:T(8,128)(2,1)} custom-call(s32[1]{0:T(128)} %bitcast.group_ref.core_ref, bf16[64,128,128]{2,1,0:T(8,128)(2,1)S(1)} %all-to-all-done.1.start_ref, f32[256,16]{1,0:T(8,128)} %get-tuple-element.16.reach_ref, bf16[256,4096]{1,0:T(8,128)(2,1)} %query_ref.3, f32[8,256,512]{2,1,0:T(8,128)} %get-tuple-element.18.within_ref, ...), custom_call_target="tpu_custom_call" | custom-call | flops 536870912 | tf_op jit(solution)/shard_map/pallas_call | solution.py:345
  115.1 0.0 collective-permute-done.1.start_ref
  115.2 7.0 %shard_map.60 = bf16[256,8192]{1,0:T(8,128)(2,1)} custom-call(s32[1]{0:T(128)S(6)} %sub.3.group_ref, bf16[64,128,128]{2,1,0:T(8,128)(2,1)S(1)} %collective-permute-done.1.start_ref, f32[256,16]{1,0:T(8,128)} %get-tuple-element.16.reach_ref, bf16[256,4096]{1,0:T(8,128)(2,1)} %query_ref.3, ...), custom_call_target="tpu_custom_call", output_to_operand_aliasing={{}: (6, {})} | custom-call | flops 536870912 | tf_op jit(solution)/shard_map/pallas_call | solution.py:348
Async XLA Ops:
  4.0 6.6 %collective-permute-start = (bf16[65,128,128]{2,1,0:T(8,128)(2,1)S(1)}, bf16[65,128,128]{2,1,0:T(8,128)(2,1)S(1)}, u32[]{:S(2)}, u32[]{:S(2)}) collective-permute-start(bf16[65,128,128]{2,1,0:T(8,128)(2,1)S(1)} %shard_map.55.theirs_ref), channel_id=1, source_target_pairs={{0,1},{1,0},{2,3},{3,2},{4,5},{5,4},{6,7},{7,6},{8,9},{9,8},{10,11... | collective-permute-start | bytes 6389768 | tf_op jit(solution)/shard_map/ppermute | solution.py:296
  54.9 1.3 %copy-start = (bf16[64,128,128]{2,1,0:T(8,128)(2,1)}, bf16[64,128,128]{2,1,0:T(8,128)(2,1)S(1)}, u32[]{:S(2)}) copy-start(bf16[64,128,128]{2,1,0:T(8,128)(2,1)S(1)} %prefix.1) | copy-start | bytes 6291460
  56.2 36.4 %copy-start.1 = (bf16[256,16]{0,1:T(8,128)(2,1)S(1)}, bf16[256,16]{0,1:T(8,128)(2,1)}, u32[]{:S(2)}) copy-start(bf16[256,16]{0,1:T(8,128)(2,1)} %param.8) | copy-start | bytes 24580
  56.2 32.5 %all-to-all-start.1 = ((bf16[64,128,128]{2,1,0:T(8,128)(2,1)}), bf16[64,128,128]{2,1,0:T(8,128)(2,1)S(1)}, u32[]{:S(2)}, u32[]{:S(2)}) async-start(bf16[64,128,128]{2,1,0:T(8,128)(2,1)} %copy-done), calls=%async_computation.1 | async-start | bytes 4194304 | tf_op jit(solution)/shard_map/all_to_all | solution.py:335
  62.0 34.4 %collective-permute-start.2 = (bf16[64,128,128]{2,1,0:T(8,128)(2,1)}, bf16[64,128,128]{2,1,0:T(8,128)(2,1)}, u32[]{:S(2)}, u32[]{:S(2)}) collective-permute-start(bf16[64,128,128]{2,1,0:T(8,128)(2,1)} %get-tuple-element.14), channel_id=1, source_target_pairs={{0,1},{1,0},{2,3},{3,2},{4,5},{5,4},{6,7},{7,6},{8,9},{9,8},{10,11... | collective-permute-start | bytes 6291464 | tf_op jit(solution)/shard_map/ppermute | solution.py:312
  63.7 32.8 %collective-permute-start.3 = (bf16[64,128,128]{2,1,0:T(8,128)(2,1)}, bf16[64,128,128]{2,1,0:T(8,128)(2,1)}, u32[]{:S(2)}, u32[]{:S(2)}) collective-permute-start(bf16[64,128,128]{2,1,0:T(8,128)(2,1)} %get-tuple-element.15), channel_id=1, source_target_pairs={{0,1},{1,0},{2,3},{3,2},{4,5},{5,4},{6,7},{7,6},{8,9},{9,8},{10,11... | collective-permute-start | bytes 6291464 | tf_op jit(solution)/shard_map/ppermute | solution.py:311
  88.7 26.5 %collective-permute-start.1 = (bf16[64,128,128]{2,1,0:T(8,128)(2,1)S(1)}, bf16[64,128,128]{2,1,0:T(8,128)(2,1)S(1)}, u32[]{:S(2)}, u32[]{:S(2)}) collective-permute-start(bf16[64,128,128]{2,1,0:T(8,128)(2,1)S(1)} %all-to-all-done.1.start_ref), channel_id=1, source_target_pairs={{0,1},{1,0},{2,3},{3,2},{4,5},{5,4},{6,7},{7,6},{8,9},{9,8},{10,11... | collective-permute-start | bytes 6291464 | tf_op jit(solution)/shard_map/ppermute | solution.py:336
  92.7 3.8 %collective-permute-start.4 = (bf16[16,256]{1,0:T(8,128)(2,1)S(1)}, bf16[16,256]{1,0:T(8,128)(2,1)S(1)}, u32[]{:S(2)}, u32[]{:S(2)}) collective-permute-start(bf16[16,256]{1,0:T(8,128)(2,1)S(1)} %bitcast.5), channel_id=1, source_target_pairs={{0,1},{1,0},{2,3},{3,2},{4,5},{5,4},{6,7},{7,6},{8,9},{9,8},{10,11... | collective-permute-start | bytes 24584 | tf_op jit(solution)/shard_map/ppermute | solution.py:313

commit v6 on v5

--- a/solution.py
+++ b/solution.py
@@ -1,3 +1,5 @@
+from functools import partial
+
 import jax
 import jax.numpy as jnp
 from jax import lax
@@ -17,6 +19,7 @@
 TILES = DV // 128
 SLICE = PIECE * TILES
 SENT = SLICE + 8
+PER_STEP = 4
 MIB = 2**20
 LIMIT = 20
 
@@ -61,36 +64,28 @@
     return jnp.concatenate(cols, axis=1)
 
 
-def columns_of(ref, head, width):
-    return ref.at[:, pl.ds(pl.multiple_of(head * width, width), width)]
-
-
 def start_all(copies):
     for copy in copies:
         copy.start()
     return copies
 
 
-def states_into(out_ref, group, key_ref, value_ref, run, key_buf, value_buf, sems, done=None):
-    copies = []
-    for n in range(HALF):
-        head = group * HALF + n
-        copies.append(start_all((
-            pltpu.make_async_copy(columns_of(key_ref, head, DK), key_buf.at[n], sems.at[0, n]),
-            pltpu.make_async_copy(columns_of(value_ref, head, DV), value_buf.at[n], sems.at[1, n]),
-        )))
-    fades = jnp.exp(run[ROWS - 1 : ROWS, :] - run)
-    for n in range(HALF):
-        fade = column(fades, group * HALF + n)
-        for copy in copies[n]:
-            copy.wait()
-        faded = (key_buf[n].astype(f32) * fade).astype(bf16)
+def states_into(refs, group, step, key_ref, value_ref, fade_ref):
+    for n in range(PER_STEP):
+        at = step * PER_STEP + n
+        fade = column(fade_ref[...], group * HALF + at)
+        faded = (key_ref[:, n * DK : (n + 1) * DK].astype(f32) * fade).astype(bf16)
         state = lax.dot_general(
-            faded, value_buf[n], (((0,), (0,)), ((), ())), preferred_element_type=f32
-        )
-        put_slices(out_ref, n, state.astype(bf16))
-        if done is not None:
-            done(n)
+            faded, value_ref[:, n * DV : (n + 1) * DV], (((0,), (0,)), ((), ())),
+            preferred_element_type=f32,
+        ).astype(bf16)
+        for ref, place in zip(refs, (at, n)):
+            put_slices(ref, place, state)
+
+
+def fades_of(decay):
+    run = running_of(decay)
+    return jnp.exp(run[ROWS - 1 : ROWS, :] - run)
 
 
 def totals_of(decay):
@@ -105,37 +100,32 @@
     return high, middle, rest - middle
 
 
-def theirs_kernel(group_ref, key_ref, value_ref, decay_ref, out_ref, key_buf, value_buf, sems):
-    run = running_of(decay_ref[...])
-    states_into(out_ref, group_ref[0], key_ref, value_ref, run, key_buf, value_buf, sems)
-    for k, third in enumerate(thirds_of(totals_of(decay_ref[...]))):
-        out_ref[CHIPS, k * HEADS : (k + 1) * HEADS, :] = third.astype(bf16)
+def theirs_kernel(group_ref, key_ref, value_ref, decay_ref, out_ref, fade_ref):
+    step = pl.program_id(0)
+
+    @pl.when(step == 0)
+    def _():
+        fade_ref[...] = fades_of(decay_ref[...])
+        for k, third in enumerate(thirds_of(totals_of(decay_ref[...]))):
+            out_ref[CHIPS, k * HEADS : (k + 1) * HEADS, :] = third.astype(bf16)
+
+    states_into((out_ref,), group_ref[0], step, key_ref, value_ref, fade_ref)
 
 
 def own_kernel(
     group_ref, key_ref, value_ref, decay_ref, theirs_ref,
-    out_ref, total_ref, own_copy_ref, theirs_copy_ref, key_buf, value_buf, sems, out_sems,
+    out_ref, total_ref, own_copy_ref, theirs_copy_ref, fade_ref,
 ):
-    theirs_copy = pltpu.make_async_copy(
-        theirs_ref.at[pl.ds(0, CHIPS)], theirs_copy_ref, out_sems.at[HALF]
-    )
-    theirs_copy.start()
-    decay = decay_ref[...]
-    total_ref[...] = totals_of(decay)
-    copies = []
-
-    def done(n):
-        rows = pl.ds(n * SLICES, SLICES)
-        copies.extend(start_all((
-            pltpu.make_async_copy(out_ref.at[rows], own_copy_ref.at[rows], out_sems.at[n]),
-        )))
-
-    states_into(
-        out_ref, group_ref[0], key_ref, value_ref, running_of(decay), key_buf, value_buf, sems, done
-    )
-    theirs_copy.wait()
-    for copy in copies:
-        copy.wait()
+    step = pl.program_id(0)
+
+    @pl.when(step == 0)
+    def _():
+        fade_ref[...] = fades_of(decay_ref[...])
+        total_ref[...] = totals_of(decay_ref[...])
+
+    size = PER_STEP * SLICES
+    theirs_copy_ref[...] = theirs_ref[pl.ds(step * size, size)]
+    states_into((out_ref, own_copy_ref), group_ref[0], step, key_ref, value_ref, fade_ref)
 
 
 def combine_kernel(core_ref, own_ref, got_ref, total_ref, out_ref, buf_ref, rate_ref, sems):
@@ -169,7 +159,7 @@
 
 def within_kernel(core_ref, *refs):
     own, theirs, (got_ref, first_ref, decay_ref, other_ref) = refs[0:3], refs[3:6], refs[6:10]
-    outs, (reach_out, run_ref, rows_ref, reach_ref) = refs[10:12], refs[12:]
+    out_ref, reach_out, run_ref, rows_ref, reach_ref = refs[10:]
     step = pl.program_id(0)
     core = core_ref[0]
 
@@ -183,10 +173,9 @@
         reach_out[...] = reach
         reach_ref[...] = jnp.where(core == 0, 0.0, jnp.exp(run))
 
-    for group, ins, state_ref, out_ref in (
-        (core, own, got_ref, outs[0]),
-        (1 - core, theirs, first_ref, outs[1]),
-    ):
+    for side, (group, ins, state_ref) in enumerate((
+        (core, own, got_ref), (1 - core, theirs, first_ref),
+    )):
         query_ref, key_ref, value_ref = ins
         head = group * HALF + step
         query = query_ref[...]
@@ -198,7 +187,7 @@
         weights = (scores * factor).astype(bf16)
         local = jnp.dot(weights, value_ref[...], preferred_element_type=f32)
         before = jnp.dot(query, get_slices(state_ref, 0), preferred_element_type=f32)
-        out_ref[0] = local + before * column(reach_ref[...], head)
+        out_ref[side, 0] = local + before * column(reach_ref[...], head)
 
 
 def prefix_kernel(in_ref, out_ref):
@@ -210,34 +199,19 @@
         state = damping * state + in_ref[b, :SLICE, :].astype(f32)
 
 
-def finish_kernel(group_ref, start_ref, reach_ref, query_ref, within_ref, gate_ref, *rest):
-    out_ref, query_buf, within_buf, gate_buf, out_buf, sems = rest[-6:]
-    copies, writes = [], []
-    for n in range(HALF):
-        head = group_ref[0] * HALF + n
-        copies.append(start_all((
-            pltpu.make_async_copy(columns_of(query_ref, head, DK), query_buf.at[n], sems.at[0, n]),
-            pltpu.make_async_copy(within_ref.at[n], within_buf.at[n], sems.at[1, n]),
-            pltpu.make_async_copy(columns_of(gate_ref, head, DV), gate_buf.at[n], sems.at[2, n]),
-        )))
-    for n in range(HALF):
-        head = group_ref[0] * HALF + n
-        reach = column(reach_ref[...], head)
-        for copy in copies[n]:
-            copy.wait()
-        across = jnp.dot(query_buf[n], get_slices(start_ref, n), preferred_element_type=f32)
-        retained = within_buf[n] + across * reach
+def finish_kernel(side, group_ref, start_ref, reach_ref, query_ref, within_ref, gate_ref, *rest):
+    out_ref = rest[-1]
+    for n in range(PER_STEP):
+        at = pl.program_id(0) * PER_STEP + n
+        head = group_ref[0] * HALF + at
+        across = jnp.dot(query_ref[:, n * DK : (n + 1) * DK], get_slices(start_ref, at), preferred_element_type=f32)
+        retained = within_ref[side, at] + across * column(reach_ref[...], head)
         average = jnp.mean(retained, axis=1, keepdims=True)
         centered = retained - average
         variance = jnp.mean(centered * centered, axis=1, keepdims=True)
         normed = centered * lax.rsqrt(variance + 1e-06)
-        gate = gate_buf[n].astype(f32)
-        out_buf[n] = (gate / (1.0 + jnp.exp(-gate)) * normed).astype(bf16)
-        writes.extend(start_all((
-            pltpu.make_async_copy(out_buf.at[n], columns_of(out_ref, head, DV), sems.at[3, n]),
-        )))
-    for copy in writes:
-        copy.wait()
+        gate = 0.5 * gate_ref[:, n * DV : (n + 1) * DV].astype(f32)
+        out_ref[:, n * DV : (n + 1) * DV] = ((gate + gate * jnp.tanh(gate)) * normed).astype(bf16)
 
 
 def call(kernel, grid, in_specs, out_specs, out_shape, scratch, flops, aliases=None):
@@ -274,6 +248,7 @@
     everyone = ("seq", "chip")
     decay = decay_log.T
 
+    steps = HALF // PER_STEP
     here = pl.BlockSpec(memory_space=pltpu.VMEM)
     decays = pl.BlockSpec((HEADS, ROWS), lambda i, c: (0, 0))
     heads = lambda width: pl.BlockSpec((ROWS, width), lambda i, c: (0, c[0] * HALF + i))
@@ -285,19 +260,20 @@
     away = pl.BlockSpec(memory_space=pl.ANY)
     key_far, value_far, decay_far = far(key_vectors), far(values), far(decay)
     stored = pltpu.HBM((CHIPS, SLICE, 128), bf16)
-    buffers = [
-        pltpu.VMEM((HALF, ROWS, DK), bf16), pltpu.VMEM((HALF, ROWS, DV), bf16),
-        pltpu.SemaphoreType.DMA((2, HALF)),
-    ]
+    wide = lambda width: pl.BlockSpec(
+        (ROWS, width * PER_STEP), lambda i, c: (0, c[0] * steps + i)
+    )
+    pieces = pl.BlockSpec((SLICES * PER_STEP, SLICE, 128), lambda i, c: (i, 0, 0))
     theirs_state = call(
-        theirs_kernel, 1, [away, away, decays], here,
-        pltpu.VMEM((CHIPS + 1, SLICE, 128), bf16), buffers, flops
+        theirs_kernel, steps, [wide(DK), wide(DV), decays], here,
+        pltpu.VMEM((CHIPS + 1, SLICE, 128), bf16), [table], flops
     )(other, key_far, value_far, decay_far)
     got = lax.ppermute(theirs_state, "core", swap)
     own_state, totals, late_own, late_theirs = call(
-        own_kernel, 1, [away, away, decays, here], [here, here, away, away],
+        own_kernel, steps, [wide(DK), wide(DV), decays, here],
+        [here, here, pieces, pieces],
         [slices, pltpu.VMEM((HEADS, 128), f32), stored, stored],
-        buffers + [pltpu.SemaphoreType.DMA((HALF + 1,))], flops,
+        [table], flops,
     )(core, key_far, value_far, decay_far, near(theirs_state))
     block_state = call(
         combine_kernel, 1, [here, here, here], away,
@@ -312,14 +288,14 @@
     own_first = lax.ppermute(late_theirs, "core", swap)
     other_decay = lax.ppermute(decay, "core", swap)
 
-    block = lambda: pl.BlockSpec((1, ROWS, DV), lambda i, c: (i, 0, 0))
-    own_within, their_within, reach = call(
+    block = pl.BlockSpec((2, 1, ROWS, DV), lambda i, c: (0, i, 0, 0))
+    within, reach = call(
         within_kernel, HALF,
         [heads(DK), heads(DK), heads(DV), theirs(DK), theirs(DK), theirs(DV),
          pl.BlockSpec((SLICES, SLICE, 128), lambda i, c: (i, 0, 0)),
          pl.BlockSpec((SLICES, SLICE, 128), lambda i, c: (i, 0, 0)), decays, decays],
-        [block(), block(), pl.BlockSpec((ROWS, HEADS), lambda i, c: (0, 0))],
-        [pltpu.HBM((HALF, ROWS, DV), f32)] * 2 + [pltpu.HBM((ROWS, HEADS), f32)],
+        [block, pl.BlockSpec((ROWS, HEADS), lambda i, c: (0, 0))],
+        [pltpu.HBM((2, HALF, ROWS, DV), f32), pltpu.HBM((ROWS, HEADS), f32)],
         [table, pltpu.VMEM((HEADS, ROWS), f32), table], 4 * flops,
     )(core, far(queries), key_far, value_far, far(queries), key_far, value_far,
       far(own_first), far(their_first), decay_far, other_decay)
@@ -335,19 +311,19 @@
     start = lax.all_to_all(starts, everyone, 0, 0, tiled=True)
     their_start = lax.ppermute(start, "core", swap)
 
-    specs = [here, pl.BlockSpec((ROWS, HEADS), lambda i, c: (0, 0)), away, away, away]
+    specs = [
+        here, pl.BlockSpec((ROWS, HEADS), lambda i, c: (0, 0)),
+        wide(DK),
+        here,
+        wide(DV),
+    ]
     result = pltpu.HBM((ROWS, HEADS * DV), bf16)
-    scratch = [
-        pltpu.VMEM((HALF, ROWS, DK), bf16), pltpu.VMEM((HALF, ROWS, DV), f32),
-        pltpu.VMEM((HALF, ROWS, DV), bf16), pltpu.VMEM((HALF, ROWS, DV), bf16),
-        pltpu.SemaphoreType.DMA((4, HALF)),
-    ]
-    done = call(finish_kernel, 1, specs, away, result, scratch, flops)(
-        core, near(start), far(reach), far(queries), far(own_within), far(gate_input)
+    done = call(partial(finish_kernel, 0), steps, specs, wide(DV), result, [], flops)(
+        core, near(start), far(reach), far(queries), near(within), far(gate_input)
     )
     return call(
-        finish_kernel, 1, specs + [away], away, result, scratch, flops, {6: 0},
-    )(other, near(their_start), far(reach), far(queries), far(their_within), far(gate_input), done)
+        partial(finish_kernel, 1), steps, specs + [away], wide(DV), result, [], flops, {6: 0},
+    )(other, near(their_start), far(reach), far(queries), near(within), far(gate_input), done)
 
 
 def solution(mesh):

time: 123 us -> 121 us (0.984)
  Pallas kernels: 36.8 us -> 31.7 us
  local copies, waits for them, and re-layouts: 1.32 us -> 4.69 us
    pallas_call x4, Pallas kernels: 23 us -> 17.1 us  [the longest x1 4.85 us: shards(): call(partial(finish_kernel, 1), steps, specs + [away], wide(DV), result,...]
    unnamed x4 -> x6, local copies, waits for them, and re-layouts: 1.32 us -> 4.69 us
  transfers between devices with their start and end apart: 6 -> 6, of which waited for: 2 -> 2; matrix products, arithmetic and copies ran while one was open for 0% -> 0% of each run, Pallas kernels for 19% -> 18%
where the time goes in v6:
time: 121 us; the launch traced here: 120 us
  blocking collectives  42.2 us (35%)
  Pallas kernels  31.7 us (26%)
  waiting for transfers between devices  28.4 us (23%)
  starting transfers between devices  13.2 us (11%)
  local copies, waits for them, and re-layouts  4.69 us (4%)
    all_to_all x1, blocking collectives, shards(): collected = lax.all_to_all(block_state, everyone, 0, 0, tiled=True)  42.2 us
    all_to_all x1, waiting for transfers between devices, shards(): start = lax.all_to_all(starts, everyone, 0, 0, tiled=True)  24.6 us
    pallas_call x1, Pallas kernels, shards(): call(within_kernel, HALF, [heads(DK), heads(DK), heads(DV), theirs(DK), t...  12.5 us
    all_to_all x1, starting transfers between devices, shards(): start = lax.all_to_all(starts, everyone, 0, 0, tiled=True)  5.74 us
    pallas_call x1, Pallas kernels, shards(): call(partial(finish_kernel, 1), steps, specs + [away], wide(DV), result,...  4.85 us
    pallas_call x1, Pallas kernels, shards(): call(partial(finish_kernel, 0), steps, specs, wide(DV), result, [], flops)  4.83 us
    unnamed x6, local copies, waits for them, and re-layouts  4.69 us
    pallas_call x1, Pallas kernels, shards(): call(own_kernel, steps, [wide(DK), wide(DV), decays, here], [here, here,...  4.36 us
  transfers between devices with their start and end apart: 6, of which 2 were waited for; matrix products, arithmetic and copies ran while one was open for 0% of the time, Pallas kernels for 18%

profile of v6, /device:TPU:1, one launch (start us, length us, event | category | flops | bytes accessed | tf_op | source)
XLA Modules:
  0.0 120.2 jit_solution(16895579910795156460)
XLA Ops:
  0.0 3.0 %shard_map.55.theirs_ref = bf16[65,128,128]{2,1,0:T(8,128)(2,1)S(1)} custom-call(s32[1]{0:T(128)S(6)} %sub.3.group_ref, bf16[256,4096]{1,0:T(8,128)(2,1)} %refs_4_.1, bf16[256,8192]{1,0:T(8,128)(2,1)} %refs_5_.1, bf16[16,256]{1,0:T(8,128)(2,1)} %bitcast.2), custom_call_target="tpu_custom_call" | custom-call | flops 536870912 | tf_op jit(solution)/shard_map/pallas_call | solution.py:267
  3.0 1.5 %collective-permute-start = (bf16[65,128,128]{2,1,0:T(8,128)(2,1)S(1)}, bf16[65,128,128]{2,1,0:T(8,128)(2,1)S(1)}, u32[]{:S(2)}, u32[]{:S(2)}) collective-permute-start(bf16[65,128,128]{2,1,0:T(8,128)(2,1)S(1)} %shard_map.55.theirs_ref), channel_id=1, source_target_pairs={{0,1},{1,0},{2,3},{3,2},{4,5},{5,4},{6,7},{7,6},{8,9},{9,8},{10,11... | collective-permute-start | bytes 6389768 | tf_op jit(solution)/shard_map/ppermute | solution.py:271
  4.5 4.4 %shard_map.56 = (bf16[64,128,128]{2,1,0:T(8,128)(2,1)S(1)}, f32[16,128]{1,0:T(8,128)S(1)}, bf16[64,128,128]{2,1,0:T(8,128)(2,1)}, bf16[64,128,128]{2,1,0:T(8,128)(2,1)}) custom-call(s32[1]{0:T(128)} %bitcast.group_ref.core_ref, bf16[256,4096]{1,0:T(8,128)(2,1)} %refs_4_.1, bf16[256,8192]{1,0:T(8,128)(2,1)} %refs_5_.1, bf16[16,256]{1,0:T(8,128)(2,1)} %bitcast.3, ...), custom_call_target="tpu_custom_call" | custom-call | flops 536870912 | tf_op jit(solution)/shard_map/pallas_call | solution.py:272
  8.9 0.0 collective-permute-done.got_ref
  8.9 1.6 %shard_map.57 = bf16[64,136,128]{2,1,0:T(8,128)(2,1)} custom-call(s32[1]{0:T(128)} %bitcast.group_ref.core_ref, bf16[64,128,128]{2,1,0:T(8,128)(2,1)S(1)} %get-tuple-element.11.own_ref, bf16[65,128,128]{2,1,0:T(8,128)(2,1)S(1)} %collective-permute-done.got_ref, f32[16,128]{1,0:T(8,128)S(1)} %get-tuple-element.12.total_ref), custom_call_target="tpu_custom_call" | custom-call | flops 67108864 | tf_op jit(solution)/shard_map/pallas_call | solution.py:278
  10.4 42.2 %all_to_all.10.in_ref = bf16[64,136,128]{2,1,0:T(8,128)(2,1)S(1)} all-to-all(bf16[64,136,128]{2,1,0:T(8,128)(2,1)} %shard_map.57), channel_id=1, replica_groups=mesh['seq'=4,'chip'=16,'core'=2] {'seq','chip'}, dimensions={0} | all-to-all | bytes 4456448 | tf_op jit(solution)/shard_map/all_to_all | solution.py:286
  52.6 0.5 prefix.1
  53.2 0.0 copy-start.1
  53.2 1.3 %copy-done.1 = bf16[64,128,128]{2,1,0:T(8,128)(2,1)} copy-done((bf16[64,128,128]{2,1,0:T(8,128)(2,1)}, bf16[64,128,128]{2,1,0:T(8,128)(2,1)S(1)}, u32[]{:S(2)}) %copy-start.1) | copy-done | bytes 2097176
  54.5 0.0 copy-start.2
  54.5 5.7 %all-to-all-start.1 = ((bf16[64,128,128]{2,1,0:T(8,128)(2,1)}), bf16[64,128,128]{2,1,0:T(8,128)(2,1)S(1)}, u32[]{:S(2)}, u32[]{:S(2)}) async-start(bf16[64,128,128]{2,1,0:T(8,128)(2,1)} %copy-done.1), calls=%async_computation.1 | async-start | bytes 4194304 | tf_op jit(solution)/shard_map/all_to_all | solution.py:311
  60.2 1.8 %collective-permute-start.2 = (bf16[64,128,128]{2,1,0:T(8,128)(2,1)}, bf16[64,128,128]{2,1,0:T(8,128)(2,1)}, u32[]{:S(2)}, u32[]{:S(2)}) collective-permute-start(bf16[64,128,128]{2,1,0:T(8,128)(2,1)} %get-tuple-element.13), channel_id=1, source_target_pairs={{0,1},{1,0},{2,3},{3,2},{4,5},{5,4},{6,7},{7,6},{8,9},{9,8},{10,11... | collective-permute-start | bytes 6291464 | tf_op jit(solution)/shard_map/ppermute | solution.py:288
  62.0 0.1 collective-permute-start.3
  62.1 24.6 %all-to-all-done.1.start_ref = bf16[64,128,128]{2,1,0:T(8,128)(2,1)S(1)} async-done(((bf16[64,128,128]{2,1,0:T(8,128)(2,1)}), bf16[64,128,128]{2,1,0:T(8,128)(2,1)S(1)}, u32[]{:S(2)}, u32[]{:S(2)}) %all-to-all-start.1) | async-done | bytes 2097184 | tf_op jit(solution)/shard_map/all_to_all | solution.py:311
  86.7 4.2 %collective-permute-start.1 = (bf16[64,128,128]{2,1,0:T(8,128)(2,1)S(1)}, bf16[64,128,128]{2,1,0:T(8,128)(2,1)S(1)}, u32[]{:S(2)}, u32[]{:S(2)}) collective-permute-start(bf16[64,128,128]{2,1,0:T(8,128)(2,1)S(1)} %all-to-all-done.1.start_ref), channel_id=1, source_target_pairs={{0,1},{1,0},{2,3},{3,2},{4,5},{5,4},{6,7},{7,6},{8,9},{9,8},{10,11... | collective-permute-start | bytes 6291464 | tf_op jit(solution)/shard_map/ppermute | solution.py:312
  90.9 0.0 copy-done.2
  90.9 0.0 collective-permute-start.4
  90.9 3.8 %collective-permute-done.4.refs_9_ = bf16[16,256]{1,0:T(8,128)(2,1)S(1)} collective-permute-done((bf16[16,256]{1,0:T(8,128)(2,1)S(1)}, bf16[16,256]{1,0:T(8,128)(2,1)S(1)}, u32[]{:S(2)}, u32[]{:S(2)}) %collective-permute-start.4) | collective-permute-done | bytes 8224 | tf_op jit(solution)/shard_map/ppermute | solution.py:289
  94.7 0.0 collective-permute-done.2.refs_6_
  94.7 0.0 collective-permute-done.3.refs_7_
  94.7 12.5 %shard_map.58 = (f32[2,8,256,512]{3,2,1,0:T(8,128)}, f32[256,16]{1,0:T(8,128)}) custom-call(s32[1]{0:T(128)} %bitcast.group_ref.core_ref, bf16[256,4096]{1,0:T(8,128)(2,1)} %query_ref.3, bf16[256,4096]{1,0:T(8,128)(2,1)} %refs_4_.1, bf16[256,8192]{1,0:T(8,128)(2,1)} %refs_5_.1, bf16[256,4096]{1,0:T(8,128)(2,1)} %query_ref.3, bf16[256,4096]{1,0:T(8,128)(2,1)} %refs_4_.1, ...), custom_call_target="tpu_custom_call" | custom-call | flops 2147483648 | tf_op jit(solution)/shard_map/pallas_call | solution.py:292
  107.2 0.0 copy-start
  107.2 3.4 %copy-done = f32[2,8,256,512]{3,2,1,0:T(8,128)S(1)} copy-done((f32[2,8,256,512]{3,2,1,0:T(8,128)S(1)}, f32[2,8,256,512]{3,2,1,0:T(8,128)}, u32[]{:S(2)}) %copy-start) | copy-done | bytes 8388632
  110.6 4.8 %shard_map.59.rest_0_ = bf16[256,8192]{1,0:T(8,128)(2,1)} custom-call(s32[1]{0:T(128)} %bitcast.group_ref.core_ref, bf16[64,128,128]{2,1,0:T(8,128)(2,1)S(1)} %all-to-all-done.1.start_ref, f32[256,16]{1,0:T(8,128)} %get-tuple-element.15.reach_ref, bf16[256,4096]{1,0:T(8,128)(2,1)} %query_ref.3, f32[2,8,256,512]{3,2,1,0:T(8,128)S(1)} %copy-done, ...), custom_call_target="tpu_custom_call" | custom-call | flops 536870912 | tf_op jit(solution)/shard_map/pallas_call | solution.py:321
  115.4 0.0 collective-permute-done.1.start_ref
  115.4 4.8 %shard_map.60 = bf16[256,8192]{1,0:T(8,128)(2,1)} custom-call(s32[1]{0:T(128)S(6)} %sub.3.group_ref, bf16[64,128,128]{2,1,0:T(8,128)(2,1)S(1)} %collective-permute-done.1.start_ref, f32[256,16]{1,0:T(8,128)} %get-tuple-element.15.reach_ref, bf16[256,4096]{1,0:T(8,128)(2,1)} %query_ref.3, ...), custom_call_target="tpu_custom_call", output_to_operand_aliasing={{}: (6, {})} | custom-call | flops 536870912 | tf_op jit(solution)/shard_map/pallas_call | solution.py:324
Async XLA Ops:
  3.0 5.8 %collective-permute-start = (bf16[65,128,128]{2,1,0:T(8,128)(2,1)S(1)}, bf16[65,128,128]{2,1,0:T(8,128)(2,1)S(1)}, u32[]{:S(2)}, u32[]{:S(2)}) collective-permute-start(bf16[65,128,128]{2,1,0:T(8,128)(2,1)S(1)} %shard_map.55.theirs_ref), channel_id=1, source_target_pairs={{0,1},{1,0},{2,3},{3,2},{4,5},{5,4},{6,7},{7,6},{8,9},{9,8},{10,11... | collective-permute-start | bytes 6389768 | tf_op jit(solution)/shard_map/ppermute | solution.py:271
  53.2 1.3 %copy-start.1 = (bf16[64,128,128]{2,1,0:T(8,128)(2,1)}, bf16[64,128,128]{2,1,0:T(8,128)(2,1)S(1)}, u32[]{:S(2)}) copy-start(bf16[64,128,128]{2,1,0:T(8,128)(2,1)S(1)} %prefix.1) | copy-start | bytes 6291460
  54.5 36.4 %copy-start.2 = (bf16[256,16]{0,1:T(8,128)(2,1)S(1)}, bf16[256,16]{0,1:T(8,128)(2,1)}, u32[]{:S(2)}) copy-start(bf16[256,16]{0,1:T(8,128)(2,1)} %param.8) | copy-start | bytes 24580
  54.5 32.2 %all-to-all-start.1 = ((bf16[64,128,128]{2,1,0:T(8,128)(2,1)}), bf16[64,128,128]{2,1,0:T(8,128)(2,1)S(1)}, u32[]{:S(2)}, u32[]{:S(2)}) async-start(bf16[64,128,128]{2,1,0:T(8,128)(2,1)} %copy-done.1), calls=%async_computation.1 | async-start | bytes 4194304 | tf_op jit(solution)/shard_map/all_to_all | solution.py:311
  60.2 34.4 %collective-permute-start.2 = (bf16[64,128,128]{2,1,0:T(8,128)(2,1)}, bf16[64,128,128]{2,1,0:T(8,128)(2,1)}, u32[]{:S(2)}, u32[]{:S(2)}) collective-permute-start(bf16[64,128,128]{2,1,0:T(8,128)(2,1)} %get-tuple-element.13), channel_id=1, source_target_pairs={{0,1},{1,0},{2,3},{3,2},{4,5},{5,4},{6,7},{7,6},{8,9},{9,8},{10,11... | collective-permute-start | bytes 6291464 | tf_op jit(solution)/shard_map/ppermute | solution.py:288
  62.0 32.6 %collective-permute-start.3 = (bf16[64,128,128]{2,1,0:T(8,128)(2,1)}, bf16[64,128,128]{2,1,0:T(8,128)(2,1)}, u32[]{:S(2)}, u32[]{:S(2)}) collective-permute-start(bf16[64,128,128]{2,1,0:T(8,128)(2,1)} %get-tuple-element.14), channel_id=1, source_target_pairs={{0,1},{1,0},{2,3},{3,2},{4,5},{5,4},{6,7},{7,6},{8,9},{9,8},{10,11... | collective-permute-start | bytes 6291464 | tf_op jit(solution)/shard_map/ppermute | solution.py:287
  86.7 28.7 %collective-permute-start.1 = (bf16[64,128,128]{2,1,0:T(8,128)(2,1)S(1)}, bf16[64,128,128]{2,1,0:T(8,128)(2,1)S(1)}, u32[]{:S(2)}, u32[]{:S(2)}) collective-permute-start(bf16[64,128,128]{2,1,0:T(8,128)(2,1)S(1)} %all-to-all-done.1.start_ref), channel_id=1, source_target_pairs={{0,1},{1,0},{2,3},{3,2},{4,5},{5,4},{6,7},{7,6},{8,9},{9,8},{10,11... | collective-permute-start | bytes 6291464 | tf_op jit(solution)/shard_map/ppermute | solution.py:312
  90.9 3.8 %collective-permute-start.4 = (bf16[16,256]{1,0:T(8,128)(2,1)S(1)}, bf16[16,256]{1,0:T(8,128)(2,1)S(1)}, u32[]{:S(2)}, u32[]{:S(2)}) collective-permute-start(bf16[16,256]{1,0:T(8,128)(2,1)S(1)} %bitcast.5), channel_id=1, source_target_pairs={{0,1},{1,0},{2,3},{3,2},{4,5},{5,4},{6,7},{7,6},{8,9},{9,8},{10,11... | collective-permute-start | bytes 24584 | tf_op jit(solution)/shard_map/ppermute | solution.py:289
  107.2 3.4 %copy-start = (f32[2,8,256,512]{3,2,1,0:T(8,128)S(1)}, f32[2,8,256,512]{3,2,1,0:T(8,128)}, u32[]{:S(2)}) copy-start(f32[2,8,256,512]{3,2,1,0:T(8,128)} %get-tuple-element.16.within_ref) | copy-start | bytes 25165828

commit v7 on v6

--- a/solution.py
+++ b/solution.py
@@ -158,8 +158,8 @@
 
 
 def within_kernel(core_ref, *refs):
-    own, theirs, (got_ref, first_ref, decay_ref, other_ref) = refs[0:3], refs[3:6], refs[6:10]
-    out_ref, reach_out, run_ref, rows_ref, reach_ref = refs[10:]
+    own, theirs, (got_ref, first_ref, decay_ref, other_ref) = refs[0:4], refs[4:8], refs[8:12]
+    out_ref, reach_out, run_ref, rows_ref, reach_ref = refs[12:]
     step = pl.program_id(0)
     core = core_ref[0]
 
@@ -176,7 +176,7 @@
     for side, (group, ins, state_ref) in enumerate((
         (core, own, got_ref), (1 - core, theirs, first_ref),
     )):
-        query_ref, key_ref, value_ref = ins
+        query_ref, key_ref, value_ref, gate_ref = ins
         head = group * HALF + step
         query = query_ref[...]
         scores = lax.dot_general(
@@ -186,8 +186,11 @@
         factor = jnp.exp(jnp.where(triangle(), spread, -jnp.inf))
         weights = (scores * factor).astype(bf16)
         local = jnp.dot(weights, value_ref[...], preferred_element_type=f32)
-        before = jnp.dot(query, get_slices(state_ref, 0), preferred_element_type=f32)
-        out_ref[side, 0] = local + before * column(reach_ref[...], head)
+        before = jnp.dot(query, get_slices(state_ref, step), preferred_element_type=f32)
+        inner = local + before * column(reach_ref[...], head)
+        out_ref[side, 0, :, :DV] = inner.astype(bf16)
+        gate = 0.5 * gate_ref[...].astype(f32)
+        out_ref[side, 0, :, DV:] = (gate + gate * jnp.tanh(gate)).astype(bf16)
 
 
 def prefix_kernel(in_ref, out_ref):
@@ -199,19 +202,22 @@
         state = damping * state + in_ref[b, :SLICE, :].astype(f32)
 
 
-def finish_kernel(side, group_ref, start_ref, reach_ref, query_ref, within_ref, gate_ref, *rest):
+def finish_kernel(side, group_ref, start_ref, reach_ref, query_ref, ready_ref, *rest):
     out_ref = rest[-1]
     for n in range(PER_STEP):
         at = pl.program_id(0) * PER_STEP + n
-        head = group_ref[0] * HALF + at
-        across = jnp.dot(query_ref[:, n * DK : (n + 1) * DK], get_slices(start_ref, at), preferred_element_type=f32)
-        retained = within_ref[side, at] + across * column(reach_ref[...], head)
+        across = jnp.dot(
+            query_ref[:, n * DK : (n + 1) * DK], get_slices(start_ref, at),
+            preferred_element_type=f32,
+        )
+        reach = column(reach_ref[...], group_ref[0] * HALF + at)
+        retained = ready_ref[side, at, :, :DV].astype(f32) + across * reach
         average = jnp.mean(retained, axis=1, keepdims=True)
         centered = retained - average
         variance = jnp.mean(centered * centered, axis=1, keepdims=True)
         normed = centered * lax.rsqrt(variance + 1e-06)
-        gate = 0.5 * gate_ref[:, n * DV : (n + 1) * DV].astype(f32)
-        out_ref[:, n * DV : (n + 1) * DV] = ((gate + gate * jnp.tanh(gate)) * normed).astype(bf16)
+        gated = ready_ref[side, at, :, DV:].astype(f32)
+        out_ref[:, n * DV : (n + 1) * DV] = (gated * normed).astype(bf16)
 
 
 def call(kernel, grid, in_specs, out_specs, out_shape, scratch, flops, aliases=None):
@@ -288,17 +294,16 @@
     own_first = lax.ppermute(late_theirs, "core", swap)
     other_decay = lax.ppermute(decay, "core", swap)
 
-    block = pl.BlockSpec((2, 1, ROWS, DV), lambda i, c: (0, i, 0, 0))
+    block = pl.BlockSpec((2, 1, ROWS, 2 * DV), lambda i, c: (0, i, 0, 0))
     within, reach = call(
         within_kernel, HALF,
-        [heads(DK), heads(DK), heads(DV), theirs(DK), theirs(DK), theirs(DV),
-         pl.BlockSpec((SLICES, SLICE, 128), lambda i, c: (i, 0, 0)),
-         pl.BlockSpec((SLICES, SLICE, 128), lambda i, c: (i, 0, 0)), decays, decays],
+        [heads(DK), heads(DK), heads(DV), heads(DV),
+         theirs(DK), theirs(DK), theirs(DV), theirs(DV), here, here, decays, decays],
         [block, pl.BlockSpec((ROWS, HEADS), lambda i, c: (0, 0))],
-        [pltpu.HBM((2, HALF, ROWS, DV), f32), pltpu.HBM((ROWS, HEADS), f32)],
+        [pltpu.HBM((2, HALF, ROWS, 2 * DV), bf16), pltpu.HBM((ROWS, HEADS), f32)],
         [table, pltpu.VMEM((HEADS, ROWS), f32), table], 4 * flops,
-    )(core, far(queries), key_far, value_far, far(queries), key_far, value_far,
-      far(own_first), far(their_first), decay_far, other_decay)
+    )(core, far(queries), key_far, value_far, far(gate_input), far(queries), key_far, value_far,
+      far(gate_input), near(own_first), near(their_first), decay_far, other_decay)
 
     starts = pl.pallas_call(
         prefix_kernel,
@@ -311,19 +316,14 @@
     start = lax.all_to_all(starts, everyone, 0, 0, tiled=True)
     their_start = lax.ppermute(start, "core", swap)
 
-    specs = [
-        here, pl.BlockSpec((ROWS, HEADS), lambda i, c: (0, 0)),
-        wide(DK),
-        here,
-        wide(DV),
-    ]
+    specs = [here, pl.BlockSpec((ROWS, HEADS), lambda i, c: (0, 0)), wide(DK), here]
     result = pltpu.HBM((ROWS, HEADS * DV), bf16)
     done = call(partial(finish_kernel, 0), steps, specs, wide(DV), result, [], flops)(
-        core, near(start), far(reach), far(queries), near(within), far(gate_input)
+        core, near(start), far(reach), far(queries), near(within)
     )
     return call(
-        partial(finish_kernel, 1), steps, specs + [away], wide(DV), result, [], flops, {6: 0},
-    )(other, near(their_start), far(reach), far(queries), near(within), far(gate_input), done)
+        partial(finish_kernel, 1), steps, specs + [away], wide(DV), result, [], flops, {5: 0},
+    )(other, near(their_start), far(reach), far(queries), near(within), done)
 
 
 def solution(mesh):

time: 121 us -> 121 us (level)
    pallas_call x1, Pallas kernels: 12.5 us -> 13.9 us  [shards(): call(within_kernel, HALF, [heads(DK), heads(DK), heads(DV), heads(DV), th...]
  transfers between devices with their start and end apart: 6 -> 6, of which waited for: 2 -> 2; matrix products, arithmetic and copies ran while one was open for 0% -> 0% of each run, Pallas kernels for 18% -> 19%
where the time goes in v7:
time: 121 us; the launch traced here: 120 us
  blocking collectives  42.2 us (35%)
  Pallas kernels  31.6 us (26%)
  waiting for transfers between devices  28.4 us (23%)
  starting transfers between devices  13.2 us (11%)
  local copies, waits for them, and re-layouts  4.69 us (4%)
    all_to_all x1, blocking collectives, shards(): collected = lax.all_to_all(block_state, everyone, 0, 0, tiled=True)  42.2 us
    all_to_all x1, waiting for transfers between devices, shards(): start = lax.all_to_all(starts, everyone, 0, 0, tiled=True)  24.6 us
    pallas_call x1, Pallas kernels, shards(): call(within_kernel, HALF, [heads(DK), heads(DK), heads(DV), heads(DV), th...  13.9 us
    all_to_all x1, starting transfers between devices, shards(): start = lax.all_to_all(starts, everyone, 0, 0, tiled=True)  5.74 us
    unnamed x6, local copies, waits for them, and re-layouts  4.69 us
    pallas_call x1, Pallas kernels, shards(): call(own_kernel, steps, [wide(DK), wide(DV), decays, here], [here, here,...  4.36 us
    ppermute x1, starting transfers between devices, shards(): their_start = lax.ppermute(start, 'core', swap)  4.15 us
    pallas_call x1, Pallas kernels, shards(): call(partial(finish_kernel, 1), steps, specs + [away], wide(DV), result,...  4.12 us
  transfers between devices with their start and end apart: 6, of which 2 were waited for; matrix products, arithmetic and copies ran while one was open for 0% of the time, Pallas kernels for 19%

profile of v7, /device:TPU:1, one launch (start us, length us, event | category | flops | bytes accessed | tf_op | source)
XLA Modules:
  0.0 120.2 jit_solution(1675844240406312359)
XLA Ops:
  0.0 3.0 %shard_map.55.theirs_ref = bf16[65,128,128]{2,1,0:T(8,128)(2,1)S(1)} custom-call(s32[1]{0:T(128)S(6)} %sub.3.group_ref, bf16[256,4096]{1,0:T(8,128)(2,1)} %refs_5_.1, bf16[256,8192]{1,0:T(8,128)(2,1)} %refs_6_.1, bf16[16,256]{1,0:T(8,128)(2,1)} %bitcast.2), custom_call_target="tpu_custom_call" | custom-call | flops 536870912 | tf_op jit(solution)/shard_map/pallas_call | solution.py:273
  3.0 1.5 %collective-permute-start = (bf16[65,128,128]{2,1,0:T(8,128)(2,1)S(1)}, bf16[65,128,128]{2,1,0:T(8,128)(2,1)S(1)}, u32[]{:S(2)}, u32[]{:S(2)}) collective-permute-start(bf16[65,128,128]{2,1,0:T(8,128)(2,1)S(1)} %shard_map.55.theirs_ref), channel_id=1, source_target_pairs={{0,1},{1,0},{2,3},{3,2},{4,5},{5,4},{6,7},{7,6},{8,9},{9,8},{10,11... | collective-permute-start | bytes 6389768 | tf_op jit(solution)/shard_map/ppermute | solution.py:277
  4.5 4.4 %shard_map.56 = (bf16[64,128,128]{2,1,0:T(8,128)(2,1)S(1)}, f32[16,128]{1,0:T(8,128)S(1)}, bf16[64,128,128]{2,1,0:T(8,128)(2,1)}, bf16[64,128,128]{2,1,0:T(8,128)(2,1)}) custom-call(s32[1]{0:T(128)} %bitcast.group_ref.core_ref, bf16[256,4096]{1,0:T(8,128)(2,1)} %refs_5_.1, bf16[256,8192]{1,0:T(8,128)(2,1)} %refs_6_.1, bf16[16,256]{1,0:T(8,128)(2,1)} %bitcast.3, ...), custom_call_target="tpu_custom_call" | custom-call | flops 536870912 | tf_op jit(solution)/shard_map/pallas_call | solution.py:278
  8.9 0.0 collective-permute-done.got_ref
  8.9 1.6 %shard_map.57 = bf16[64,136,128]{2,1,0:T(8,128)(2,1)} custom-call(s32[1]{0:T(128)} %bitcast.group_ref.core_ref, bf16[64,128,128]{2,1,0:T(8,128)(2,1)S(1)} %get-tuple-element.11.own_ref, bf16[65,128,128]{2,1,0:T(8,128)(2,1)S(1)} %collective-permute-done.got_ref, f32[16,128]{1,0:T(8,128)S(1)} %get-tuple-element.12.total_ref), custom_call_target="tpu_custom_call" | custom-call | flops 67108864 | tf_op jit(solution)/shard_map/pallas_call | solution.py:284
  10.4 42.2 %all_to_all.10.in_ref = bf16[64,136,128]{2,1,0:T(8,128)(2,1)S(1)} all-to-all(bf16[64,136,128]{2,1,0:T(8,128)(2,1)} %shard_map.57), channel_id=1, replica_groups=mesh['seq'=4,'chip'=16,'core'=2] {'seq','chip'}, dimensions={0} | all-to-all | bytes 4456448 | tf_op jit(solution)/shard_map/all_to_all | solution.py:292
  52.6 0.5 prefix.1
  53.2 0.0 copy-start.1
  53.2 1.3 %copy-done.1 = bf16[64,128,128]{2,1,0:T(8,128)(2,1)} copy-done((bf16[64,128,128]{2,1,0:T(8,128)(2,1)}, bf16[64,128,128]{2,1,0:T(8,128)(2,1)S(1)}, u32[]{:S(2)}) %copy-start.1) | copy-done | bytes 2097176
  54.5 0.0 copy-start.2
  54.5 5.7 %all-to-all-start.1 = ((bf16[64,128,128]{2,1,0:T(8,128)(2,1)}), bf16[64,128,128]{2,1,0:T(8,128)(2,1)S(1)}, u32[]{:S(2)}, u32[]{:S(2)}) async-start(bf16[64,128,128]{2,1,0:T(8,128)(2,1)} %copy-done.1), calls=%async_computation.1 | async-start | bytes 4194304 | tf_op jit(solution)/shard_map/all_to_all | solution.py:316
  60.2 1.8 %collective-permute-start.2 = (bf16[64,128,128]{2,1,0:T(8,128)(2,1)}, bf16[64,128,128]{2,1,0:T(8,128)(2,1)}, u32[]{:S(2)}, u32[]{:S(2)}) collective-permute-start(bf16[64,128,128]{2,1,0:T(8,128)(2,1)} %get-tuple-element.13), channel_id=1, source_target_pairs={{0,1},{1,0},{2,3},{3,2},{4,5},{5,4},{6,7},{7,6},{8,9},{9,8},{10,11... | collective-permute-start | bytes 6291464 | tf_op jit(solution)/shard_map/ppermute | solution.py:294
  62.0 0.1 collective-permute-start.3
  62.1 24.6 %all-to-all-done.1.start_ref = bf16[64,128,128]{2,1,0:T(8,128)(2,1)S(1)} async-done(((bf16[64,128,128]{2,1,0:T(8,128)(2,1)}), bf16[64,128,128]{2,1,0:T(8,128)(2,1)S(1)}, u32[]{:S(2)}, u32[]{:S(2)}) %all-to-all-start.1) | async-done | bytes 2097184 | tf_op jit(solution)/shard_map/all_to_all | solution.py:316
  86.7 4.2 %collective-permute-start.1 = (bf16[64,128,128]{2,1,0:T(8,128)(2,1)S(1)}, bf16[64,128,128]{2,1,0:T(8,128)(2,1)S(1)}, u32[]{:S(2)}, u32[]{:S(2)}) collective-permute-start(bf16[64,128,128]{2,1,0:T(8,128)(2,1)S(1)} %all-to-all-done.1.start_ref), channel_id=1, source_target_pairs={{0,1},{1,0},{2,3},{3,2},{4,5},{5,4},{6,7},{7,6},{8,9},{9,8},{10,11... | collective-permute-start | bytes 6291464 | tf_op jit(solution)/shard_map/ppermute | solution.py:317
  90.9 0.0 copy-done.2
  90.9 0.0 collective-permute-start.4
  90.9 3.8 %collective-permute-done.4.refs_11_ = bf16[16,256]{1,0:T(8,128)(2,1)S(1)} collective-permute-done((bf16[16,256]{1,0:T(8,128)(2,1)S(1)}, bf16[16,256]{1,0:T(8,128)(2,1)S(1)}, u32[]{:S(2)}, u32[]{:S(2)}) %collective-permute-start.4) | collective-permute-done | bytes 8224 | tf_op jit(solution)/shard_map/ppermute | solution.py:295
  94.7 0.0 collective-permute-done.2.refs_8_
  94.7 0.0 collective-permute-done.3.refs_9_
  94.7 13.9 %shard_map.58 = (bf16[2,8,256,1024]{3,2,1,0:T(8,128)(2,1)}, f32[256,16]{1,0:T(8,128)}) custom-call(s32[1]{0:T(128)} %bitcast.group_ref.core_ref, bf16[256,4096]{1,0:T(8,128)(2,1)} %query_ref.3, bf16[256,4096]{1,0:T(8,128)(2,1)} %refs_5_.1, bf16[256,8192]{1,0:T(8,128)(2,1)} %refs_6_.1, bf16[256,8192]{1,0:T(8,128)(2,1)} %refs_7_.1, ...), custom_call_target="tpu_custom_call" | custom-call | flops 2147483648 | tf_op jit(solution)/shard_map/pallas_call | solution.py:298
  108.6 0.0 copy-start
  108.6 3.4 %copy-done = bf16[2,8,256,1024]{3,2,1,0:T(8,128)(2,1)S(1)} copy-done((bf16[2,8,256,1024]{3,2,1,0:T(8,128)(2,1)S(1)}, bf16[2,8,256,1024]{3,2,1,0:T(8,128)(2,1)}, u32[]{:S(2)}) %copy-start) | copy-done | bytes 8388632
  112.0 4.1 %shard_map.59.rest_0_ = bf16[256,8192]{1,0:T(8,128)(2,1)} custom-call(s32[1]{0:T(128)} %bitcast.group_ref.core_ref, bf16[64,128,128]{2,1,0:T(8,128)(2,1)S(1)} %all-to-all-done.1.start_ref, f32[256,16]{1,0:T(8,128)} %get-tuple-element.15.reach_ref, bf16[256,4096]{1,0:T(8,128)(2,1)} %query_ref.3, bf16[2,8,256,1024]{3,2,1,0:T(8,128)(2,1)S(1)} %copy-done), custom_call_target="tpu_custom_call" | custom-call | flops 536870912 | tf_op jit(solution)/shard_map/pallas_call | solution.py:321
  116.1 0.0 collective-permute-done.1.start_ref
  116.1 4.1 %shard_map.60 = bf16[256,8192]{1,0:T(8,128)(2,1)} custom-call(s32[1]{0:T(128)S(6)} %sub.3.group_ref, bf16[64,128,128]{2,1,0:T(8,128)(2,1)S(1)} %collective-permute-done.1.start_ref, f32[256,16]{1,0:T(8,128)} %get-tuple-element.15.reach_ref, bf16[256,4096]{1,0:T(8,128)(2,1)} %query_ref.3, ...), custom_call_target="tpu_custom_call", output_to_operand_aliasing={{}: (5, {})} | custom-call | flops 536870912 | tf_op jit(solution)/shard_map/pallas_call | solution.py:324
Async XLA Ops:
  3.0 5.8 %collective-permute-start = (bf16[65,128,128]{2,1,0:T(8,128)(2,1)S(1)}, bf16[65,128,128]{2,1,0:T(8,128)(2,1)S(1)}, u32[]{:S(2)}, u32[]{:S(2)}) collective-permute-start(bf16[65,128,128]{2,1,0:T(8,128)(2,1)S(1)} %shard_map.55.theirs_ref), channel_id=1, source_target_pairs={{0,1},{1,0},{2,3},{3,2},{4,5},{5,4},{6,7},{7,6},{8,9},{9,8},{10,11... | collective-permute-start | bytes 6389768 | tf_op jit(solution)/shard_map/ppermute | solution.py:277
  53.2 1.3 %copy-start.1 = (bf16[64,128,128]{2,1,0:T(8,128)(2,1)}, bf16[64,128,128]{2,1,0:T(8,128)(2,1)S(1)}, u32[]{:S(2)}) copy-start(bf16[64,128,128]{2,1,0:T(8,128)(2,1)S(1)} %prefix.1) | copy-start | bytes 6291460
  54.5 36.4 %copy-start.2 = (bf16[256,16]{0,1:T(8,128)(2,1)S(1)}, bf16[256,16]{0,1:T(8,128)(2,1)}, u32[]{:S(2)}) copy-start(bf16[256,16]{0,1:T(8,128)(2,1)} %param.8) | copy-start | bytes 24580
  54.5 32.2 %all-to-all-start.1 = ((bf16[64,128,128]{2,1,0:T(8,128)(2,1)}), bf16[64,128,128]{2,1,0:T(8,128)(2,1)S(1)}, u32[]{:S(2)}, u32[]{:S(2)}) async-start(bf16[64,128,128]{2,1,0:T(8,128)(2,1)} %copy-done.1), calls=%async_computation.1 | async-start | bytes 4194304 | tf_op jit(solution)/shard_map/all_to_all | solution.py:316
  60.2 34.4 %collective-permute-start.2 = (bf16[64,128,128]{2,1,0:T(8,128)(2,1)}, bf16[64,128,128]{2,1,0:T(8,128)(2,1)}, u32[]{:S(2)}, u32[]{:S(2)}) collective-permute-start(bf16[64,128,128]{2,1,0:T(8,128)(2,1)} %get-tuple-element.13), channel_id=1, source_target_pairs={{0,1},{1,0},{2,3},{3,2},{4,5},{5,4},{6,7},{7,6},{8,9},{9,8},{10,11... | collective-permute-start | bytes 6291464 | tf_op jit(solution)/shard_map/ppermute | solution.py:294
  62.0 32.6 %collective-permute-start.3 = (bf16[64,128,128]{2,1,0:T(8,128)(2,1)}, bf16[64,128,128]{2,1,0:T(8,128)(2,1)}, u32[]{:S(2)}, u32[]{:S(2)}) collective-permute-start(bf16[64,128,128]{2,1,0:T(8,128)(2,1)} %get-tuple-element.14), channel_id=1, source_target_pairs={{0,1},{1,0},{2,3},{3,2},{4,5},{5,4},{6,7},{7,6},{8,9},{9,8},{10,11... | collective-permute-start | bytes 6291464 | tf_op jit(solution)/shard_map/ppermute | solution.py:293
  86.7 29.4 %collective-permute-start.1 = (bf16[64,128,128]{2,1,0:T(8,128)(2,1)S(1)}, bf16[64,128,128]{2,1,0:T(8,128)(2,1)S(1)}, u32[]{:S(2)}, u32[]{:S(2)}) collective-permute-start(bf16[64,128,128]{2,1,0:T(8,128)(2,1)S(1)} %all-to-all-done.1.start_ref), channel_id=1, source_target_pairs={{0,1},{1,0},{2,3},{3,2},{4,5},{5,4},{6,7},{7,6},{8,9},{9,8},{10,11... | collective-permute-start | bytes 6291464 | tf_op jit(solution)/shard_map/ppermute | solution.py:317
  90.9 3.8 %collective-permute-start.4 = (bf16[16,256]{1,0:T(8,128)(2,1)S(1)}, bf16[16,256]{1,0:T(8,128)(2,1)S(1)}, u32[]{:S(2)}, u32[]{:S(2)}) collective-permute-start(bf16[16,256]{1,0:T(8,128)(2,1)S(1)} %bitcast.5), channel_id=1, source_target_pairs={{0,1},{1,0},{2,3},{3,2},{4,5},{5,4},{6,7},{7,6},{8,9},{9,8},{10,11... | collective-permute-start | bytes 24584 | tf_op jit(solution)/shard_map/ppermute | solution.py:295
  108.6 3.4 %copy-start = (bf16[2,8,256,1024]{3,2,1,0:T(8,128)(2,1)S(1)}, bf16[2,8,256,1024]{3,2,1,0:T(8,128)(2,1)}, u32[]{:S(2)}) copy-start(bf16[2,8,256,1024]{3,2,1,0:T(8,128)(2,1)} %get-tuple-element.16.ready_ref) | copy-start | bytes 25165828

commit v8 on v7

--- a/solution.py
+++ b/solution.py
@@ -188,9 +188,9 @@
         local = jnp.dot(weights, value_ref[...], preferred_element_type=f32)
         before = jnp.dot(query, get_slices(state_ref, step), preferred_element_type=f32)
         inner = local + before * column(reach_ref[...], head)
-        out_ref[side, 0, :, :DV] = inner.astype(bf16)
+        out_ref[side, 0, :, :DV] = inner
         gate = 0.5 * gate_ref[...].astype(f32)
-        out_ref[side, 0, :, DV:] = (gate + gate * jnp.tanh(gate)).astype(bf16)
+        out_ref[side, 0, :, DV:] = gate + gate * jnp.tanh(gate)
 
 
 def prefix_kernel(in_ref, out_ref):
@@ -206,17 +206,18 @@
     out_ref = rest[-1]
     for n in range(PER_STEP):
         at = pl.program_id(0) * PER_STEP + n
+        head = group_ref[0] * HALF + at
         across = jnp.dot(
-            query_ref[:, n * DK : (n + 1) * DK], get_slices(start_ref, at),
+            query_ref[:, pl.ds(pl.multiple_of(head * DK, DK), DK)], get_slices(start_ref, at),
             preferred_element_type=f32,
         )
-        reach = column(reach_ref[...], group_ref[0] * HALF + at)
-        retained = ready_ref[side, at, :, :DV].astype(f32) + across * reach
+        reach = column(reach_ref[...], head)
+        retained = ready_ref[side, at, :, :DV] + across * reach
         average = jnp.mean(retained, axis=1, keepdims=True)
         centered = retained - average
         variance = jnp.mean(centered * centered, axis=1, keepdims=True)
         normed = centered * lax.rsqrt(variance + 1e-06)
-        gated = ready_ref[side, at, :, DV:].astype(f32)
+        gated = ready_ref[side, at, :, DV:]
         out_ref[:, n * DV : (n + 1) * DV] = (gated * normed).astype(bf16)
 
 
@@ -300,7 +301,7 @@
         [heads(DK), heads(DK), heads(DV), heads(DV),
          theirs(DK), theirs(DK), theirs(DV), theirs(DV), here, here, decays, decays],
         [block, pl.BlockSpec((ROWS, HEADS), lambda i, c: (0, 0))],
-        [pltpu.HBM((2, HALF, ROWS, 2 * DV), bf16), pltpu.HBM((ROWS, HEADS), f32)],
+        [pltpu.HBM((2, HALF, ROWS, 2 * DV), f32), pltpu.HBM((ROWS, HEADS), f32)],
         [table, pltpu.VMEM((HEADS, ROWS), f32), table], 4 * flops,
     )(core, far(queries), key_far, value_far, far(gate_input), far(queries), key_far, value_far,
       far(gate_input), near(own_first), near(their_first), decay_far, other_decay)
@@ -311,19 +312,20 @@
         in_specs=[here],
         out_specs=here,
         compiler_params=pltpu.CompilerParams(vmem_limit_bytes=LIMIT * MIB),
+        cost_estimate=pl.CostEstimate(flops=10**10, transcendentals=0, bytes_accessed=0),
         name="prefix",
     )(near(collected))
     start = lax.all_to_all(starts, everyone, 0, 0, tiled=True)
     their_start = lax.ppermute(start, "core", swap)
 
-    specs = [here, pl.BlockSpec((ROWS, HEADS), lambda i, c: (0, 0)), wide(DK), here]
+    specs = [here, pl.BlockSpec((ROWS, HEADS), lambda i, c: (0, 0)), here, here]
     result = pltpu.HBM((ROWS, HEADS * DV), bf16)
     done = call(partial(finish_kernel, 0), steps, specs, wide(DV), result, [], flops)(
-        core, near(start), far(reach), far(queries), near(within)
+        core, near(start), far(reach), near(queries), near(within)
     )
     return call(
         partial(finish_kernel, 1), steps, specs + [away], wide(DV), result, [], flops, {5: 0},
-    )(other, near(their_start), far(reach), far(queries), near(within), done)
+    )(other, near(their_start), far(reach), near(queries), near(within), done)
 
 
 def solution(mesh):

time: 121 us -> 126 us (1.041)
  Pallas kernels: 31.6 us -> 35.9 us
    pallas_call x1, Pallas kernels: 13.9 us -> 16.9 us  [shards(): call(within_kernel, HALF, [heads(DK), heads(DK), heads(DV), heads(DV), th...]
    pallas_call x1, Pallas kernels: 0.52 us -> 1.84 us  [shards(): pl.pallas_call(prefix_kernel, out_shape=slices, in_specs=[here], out_spec...]
  transfers between devices with their start and end apart: 6 -> 6, of which waited for: 2 -> 2; matrix products, arithmetic and copies ran while one was open for 0% -> 0% of each run, Pallas kernels for 19% -> 20%
where the time goes in v8:
time: 126 us
  blocking collectives  42.2 us (33%)
  Pallas kernels  35.9 us (28%)
  waiting for transfers between devices  28.4 us (23%)
  starting transfers between devices  13.5 us (11%)
  local copies, waits for them, and re-layouts  5.77 us (5%)
    all_to_all x1, blocking collectives, shards(): collected = lax.all_to_all(block_state, everyone, 0, 0, tiled=True)  42.2 us
    all_to_all x1, waiting for transfers between devices, shards(): start = lax.all_to_all(starts, everyone, 0, 0, tiled=True)  24.4 us
    pallas_call x1, Pallas kernels, shards(): call(within_kernel, HALF, [heads(DK), heads(DK), heads(DV), heads(DV), th...  16.9 us
    all_to_all x1, starting transfers between devices, shards(): start = lax.all_to_all(starts, everyone, 0, 0, tiled=True)  6 us
    unnamed x6, local copies, waits for them, and re-layouts  5.77 us
    pallas_call x1, Pallas kernels, shards(): call(partial(finish_kernel, 0), steps, specs, wide(DV), result, [], flops)  4.44 us
    pallas_call x1, Pallas kernels, shards(): call(own_kernel, steps, [wide(DK), wide(DV), decays, here], [here, here,...  4.36 us
    ppermute x1, starting transfers between devices, shards(): their_start = lax.ppermute(start, 'core', swap)  4.15 us
  transfers between devices with their start and end apart: 6, of which 2 were waited for; matrix products, arithmetic and copies ran while one was open for 0% of the time, Pallas kernels for 20%

profile of v8, /device:TPU:1, one launch (start us, length us, event | category | flops | bytes accessed | tf_op | source)
XLA Modules:
  0.0 125.9 jit_solution(7900306389248872738)
XLA Ops:
  0.0 3.0 %shard_map.55.theirs_ref = bf16[65,128,128]{2,1,0:T(8,128)(2,1)S(1)} custom-call(s32[1]{0:T(128)S(6)} %sub.3.group_ref, bf16[256,4096]{1,0:T(8,128)(2,1)} %refs_5_.1, bf16[256,8192]{1,0:T(8,128)(2,1)} %refs_6_.1, bf16[16,256]{1,0:T(8,128)(2,1)} %bitcast.2), custom_call_target="tpu_custom_call" | custom-call | flops 536870912 | tf_op jit(solution)/shard_map/pallas_call | solution.py:274
  3.0 1.5 %collective-permute-start = (bf16[65,128,128]{2,1,0:T(8,128)(2,1)S(1)}, bf16[65,128,128]{2,1,0:T(8,128)(2,1)S(1)}, u32[]{:S(2)}, u32[]{:S(2)}) collective-permute-start(bf16[65,128,128]{2,1,0:T(8,128)(2,1)S(1)} %shard_map.55.theirs_ref), channel_id=1, source_target_pairs={{0,1},{1,0},{2,3},{3,2},{4,5},{5,4},{6,7},{7,6},{8,9},{9,8},{10,11... | collective-permute-start | bytes 6389768 | tf_op jit(solution)/shard_map/ppermute | solution.py:278
  4.5 4.4 %shard_map.56 = (bf16[64,128,128]{2,1,0:T(8,128)(2,1)S(1)}, f32[16,128]{1,0:T(8,128)S(1)}, bf16[64,128,128]{2,1,0:T(8,128)(2,1)}, bf16[64,128,128]{2,1,0:T(8,128)(2,1)}) custom-call(s32[1]{0:T(128)} %bitcast.group_ref.core_ref, bf16[256,4096]{1,0:T(8,128)(2,1)} %refs_5_.1, bf16[256,8192]{1,0:T(8,128)(2,1)} %refs_6_.1, bf16[16,256]{1,0:T(8,128)(2,1)} %bitcast.3, ...), custom_call_target="tpu_custom_call" | custom-call | flops 536870912 | tf_op jit(solution)/shard_map/pallas_call | solution.py:279
  8.9 0.0 collective-permute-done.got_ref
  8.9 1.6 %shard_map.57 = bf16[64,136,128]{2,1,0:T(8,128)(2,1)} custom-call(s32[1]{0:T(128)} %bitcast.group_ref.core_ref, bf16[64,128,128]{2,1,0:T(8,128)(2,1)S(1)} %get-tuple-element.11.own_ref, bf16[65,128,128]{2,1,0:T(8,128)(2,1)S(1)} %collective-permute-done.got_ref, f32[16,128]{1,0:T(8,128)S(1)} %get-tuple-element.12.total_ref), custom_call_target="tpu_custom_call" | custom-call | flops 67108864 | tf_op jit(solution)/shard_map/pallas_call | solution.py:285
  10.4 42.2 %all_to_all.10.in_ref = bf16[64,136,128]{2,1,0:T(8,128)(2,1)S(1)} all-to-all(bf16[64,136,128]{2,1,0:T(8,128)(2,1)} %shard_map.57), channel_id=1, replica_groups=mesh['seq'=4,'chip'=16,'core'=2] {'seq','chip'}, dimensions={0} | all-to-all | bytes 4456448 | tf_op jit(solution)/shard_map/all_to_all | solution.py:293
  52.6 1.8 %prefix.1 = bf16[64,128,128]{2,1,0:T(8,128)(2,1)} custom-call(bf16[64,136,128]{2,1,0:T(8,128)(2,1)S(1)} %all_to_all.10.in_ref), custom_call_target="tpu_custom_call" | custom-call | flops 10000000000 | tf_op jit(solution)/shard_map/prefix/pallas_call | solution.py:309
  54.5 0.0 copy-start.2
  54.5 6.0 %all-to-all-start.1 = ((bf16[64,128,128]{2,1,0:T(8,128)(2,1)}), bf16[64,128,128]{2,1,0:T(8,128)(2,1)}, u32[]{:S(2)}, u32[]{:S(2)}) async-start(bf16[64,128,128]{2,1,0:T(8,128)(2,1)} %prefix.1), calls=%async_computation.1 | async-start | bytes 4194304 | tf_op jit(solution)/shard_map/all_to_all | solution.py:318
  60.5 1.8 %collective-permute-start.2 = (bf16[64,128,128]{2,1,0:T(8,128)(2,1)}, bf16[64,128,128]{2,1,0:T(8,128)(2,1)}, u32[]{:S(2)}, u32[]{:S(2)}) collective-permute-start(bf16[64,128,128]{2,1,0:T(8,128)(2,1)} %get-tuple-element.13), channel_id=1, source_target_pairs={{0,1},{1,0},{2,3},{3,2},{4,5},{5,4},{6,7},{7,6},{8,9},{9,8},{10,11... | collective-permute-start | bytes 6291464 | tf_op jit(solution)/shard_map/ppermute | solution.py:295
  62.3 0.0 copy-start.1
  62.3 0.1 collective-permute-start.3
  62.4 24.4 %all-to-all-done.1.start_ref = bf16[64,128,128]{2,1,0:T(8,128)(2,1)} async-done(((bf16[64,128,128]{2,1,0:T(8,128)(2,1)}), bf16[64,128,128]{2,1,0:T(8,128)(2,1)}, u32[]{:S(2)}, u32[]{:S(2)}) %all-to-all-start.1) | async-done | bytes 2097184 | tf_op jit(solution)/shard_map/all_to_all | solution.py:318
  86.8 4.2 %collective-permute-start.1 = (bf16[64,128,128]{2,1,0:T(8,128)(2,1)}, bf16[64,128,128]{2,1,0:T(8,128)(2,1)S(1)}, u32[]{:S(2)}, u32[]{:S(2)}) collective-permute-start(bf16[64,128,128]{2,1,0:T(8,128)(2,1)} %all-to-all-done.1.start_ref), channel_id=1, source_target_pairs={{0,1},{1,0},{2,3},{3,2},{4,5},{5,4},{6,7},{7,6},{8,9},{9,8},{10,11... | collective-permute-start | bytes 6291464 | tf_op jit(solution)/shard_map/ppermute | solution.py:319
  91.0 0.0 copy-done.2
  91.0 0.0 collective-permute-start.4
  91.0 4.0 %collective-permute-done.4.refs_11_ = bf16[16,256]{1,0:T(8,128)(2,1)S(1)} collective-permute-done((bf16[16,256]{1,0:T(8,128)(2,1)S(1)}, bf16[16,256]{1,0:T(8,128)(2,1)S(1)}, u32[]{:S(2)}, u32[]{:S(2)}) %collective-permute-start.4) | collective-permute-done | bytes 8224 | tf_op jit(solution)/shard_map/ppermute | solution.py:296
  95.0 0.0 collective-permute-done.2.refs_8_
  95.0 0.0 collective-permute-done.3.refs_9_
  95.0 16.9 %shard_map.58 = (f32[2,8,256,1024]{3,2,1,0:T(8,128)}, f32[256,16]{1,0:T(8,128)}) custom-call(s32[1]{0:T(128)} %bitcast.group_ref.core_ref, bf16[256,4096]{1,0:T(8,128)(2,1)} %query_ref.3, bf16[256,4096]{1,0:T(8,128)(2,1)} %refs_5_.1, bf16[256,8192]{1,0:T(8,128)(2,1)} %refs_6_.1, bf16[256,8192]{1,0:T(8,128)(2,1)} %refs_7_.1, bf16[256,4096]{1,0:T(8,128)(2,1)} %query_ref.3, ...), custom_call_target="tpu_custom_call" | custom-call | flops 2147483648 | tf_op jit(solution)/shard_map/pallas_call | solution.py:299
  111.9 0.0 copy-done.1
  111.9 0.0 copy-start
  111.9 5.8 %copy-done = f32[2,8,256,1024]{3,2,1,0:T(8,128)S(1)} copy-done((f32[2,8,256,1024]{3,2,1,0:T(8,128)S(1)}, f32[2,8,256,1024]{3,2,1,0:T(8,128)}, u32[]{:S(2)}) %copy-start) | copy-done | bytes 16777240
  117.7 4.4 %shard_map.59.rest_0_ = bf16[256,8192]{1,0:T(8,128)(2,1)} custom-call(s32[1]{0:T(128)} %bitcast.group_ref.core_ref, bf16[64,128,128]{2,1,0:T(8,128)(2,1)} %all-to-all-done.1.start_ref, f32[256,16]{1,0:T(8,128)} %get-tuple-element.15.reach_ref, bf16[256,4096]{1,0:T(8,128)(2,1)S(1)} %copy-done.1, f32[2,8,256,1024]{3,2,1,0:T(8,128)S(1)} %copy-done), custom_call_target="tpu_custom_call" | custom-call | flops 536870912 | tf_op jit(solution)/shard_map/pallas_call | solution.py:323
  122.1 0.0 collective-permute-done.1.start_ref
  122.1 3.7 %shard_map.60 = bf16[256,8192]{1,0:T(8,128)(2,1)} custom-call(s32[1]{0:T(128)S(6)} %sub.3.group_ref, bf16[64,128,128]{2,1,0:T(8,128)(2,1)S(1)} %collective-permute-done.1.start_ref, f32[256,16]{1,0:T(8,128)} %get-tuple-element.15.reach_ref, bf16[256,4096]{1,0:T(8,128)(2,1)S(1)} %copy-done.1, ...), custom_call_target="tpu_custom_call", output_to_operand_aliasing={{}: (5, {})} | custom-call | flops 536870912 | tf_op jit(solution)/shard_map/pallas_call | solution.py:326
Async XLA Ops:
  3.0 5.8 %collective-permute-start = (bf16[65,128,128]{2,1,0:T(8,128)(2,1)S(1)}, bf16[65,128,128]{2,1,0:T(8,128)(2,1)S(1)}, u32[]{:S(2)}, u32[]{:S(2)}) collective-permute-start(bf16[65,128,128]{2,1,0:T(8,128)(2,1)S(1)} %shard_map.55.theirs_ref), channel_id=1, source_target_pairs={{0,1},{1,0},{2,3},{3,2},{4,5},{5,4},{6,7},{7,6},{8,9},{9,8},{10,11... | collective-permute-start | bytes 6389768 | tf_op jit(solution)/shard_map/ppermute | solution.py:278
  54.5 36.5 %copy-start.2 = (bf16[256,16]{0,1:T(8,128)(2,1)S(1)}, bf16[256,16]{0,1:T(8,128)(2,1)}, u32[]{:S(2)}) copy-start(bf16[256,16]{0,1:T(8,128)(2,1)} %param.8) | copy-start | bytes 24580
  54.5 32.3 %all-to-all-start.1 = ((bf16[64,128,128]{2,1,0:T(8,128)(2,1)}), bf16[64,128,128]{2,1,0:T(8,128)(2,1)}, u32[]{:S(2)}, u32[]{:S(2)}) async-start(bf16[64,128,128]{2,1,0:T(8,128)(2,1)} %prefix.1), calls=%async_computation.1 | async-start | bytes 4194304 | tf_op jit(solution)/shard_map/all_to_all | solution.py:318
  60.5 34.5 %collective-permute-start.2 = (bf16[64,128,128]{2,1,0:T(8,128)(2,1)}, bf16[64,128,128]{2,1,0:T(8,128)(2,1)}, u32[]{:S(2)}, u32[]{:S(2)}) collective-permute-start(bf16[64,128,128]{2,1,0:T(8,128)(2,1)} %get-tuple-element.13), channel_id=1, source_target_pairs={{0,1},{1,0},{2,3},{3,2},{4,5},{5,4},{6,7},{7,6},{8,9},{9,8},{10,11... | collective-permute-start | bytes 6291464 | tf_op jit(solution)/shard_map/ppermute | solution.py:295
  62.3 49.6 %copy-start.1 = (bf16[256,4096]{1,0:T(8,128)(2,1)S(1)}, bf16[256,4096]{1,0:T(8,128)(2,1)}, u32[]{:S(2)}) copy-start(bf16[256,4096]{1,0:T(8,128)(2,1)} %query_ref.3) | copy-start | bytes 6291460
  62.3 32.7 %collective-permute-start.3 = (bf16[64,128,128]{2,1,0:T(8,128)(2,1)}, bf16[64,128,128]{2,1,0:T(8,128)(2,1)}, u32[]{:S(2)}, u32[]{:S(2)}) collective-permute-start(bf16[64,128,128]{2,1,0:T(8,128)(2,1)} %get-tuple-element.14), channel_id=1, source_target_pairs={{0,1},{1,0},{2,3},{3,2},{4,5},{5,4},{6,7},{7,6},{8,9},{9,8},{10,11... | collective-permute-start | bytes 6291464 | tf_op jit(solution)/shard_map/ppermute | solution.py:294
  86.8 35.3 %collective-permute-start.1 = (bf16[64,128,128]{2,1,0:T(8,128)(2,1)}, bf16[64,128,128]{2,1,0:T(8,128)(2,1)S(1)}, u32[]{:S(2)}, u32[]{:S(2)}) collective-permute-start(bf16[64,128,128]{2,1,0:T(8,128)(2,1)} %all-to-all-done.1.start_ref), channel_id=1, source_target_pairs={{0,1},{1,0},{2,3},{3,2},{4,5},{5,4},{6,7},{7,6},{8,9},{9,8},{10,11... | collective-permute-start | bytes 6291464 | tf_op jit(solution)/shard_map/ppermute | solution.py:319
  91.0 4.0 %collective-permute-start.4 = (bf16[16,256]{1,0:T(8,128)(2,1)S(1)}, bf16[16,256]{1,0:T(8,128)(2,1)S(1)}, u32[]{:S(2)}, u32[]{:S(2)}) collective-permute-start(bf16[16,256]{1,0:T(8,128)(2,1)S(1)} %bitcast.5), channel_id=1, source_target_pairs={{0,1},{1,0},{2,3},{3,2},{4,5},{5,4},{6,7},{7,6},{8,9},{9,8},{10,11... | collective-permute-start | bytes 24584 | tf_op jit(solution)/shard_map/ppermute | solution.py:296
  111.9 5.8 %copy-start = (f32[2,8,256,1024]{3,2,1,0:T(8,128)S(1)}, f32[2,8,256,1024]{3,2,1,0:T(8,128)}, u32[]{:S(2)}) copy-start(f32[2,8,256,1024]{3,2,1,0:T(8,128)} %get-tuple-element.16.ready_ref) | copy-start | bytes 50331652

commit v9 on v8

--- a/solution.py
+++ b/solution.py
@@ -170,7 +170,8 @@
         rows_ref[...] = running_rows(decay_ref[...])
         other = running_of(other_ref[...])[ROWS - 1 : ROWS, :]
         reach = jnp.exp(run + jnp.where(core == 0, 0.0, other))
-        reach_out[...] = reach
+        for h in range(HEADS):
+            reach_out[h] = jnp.broadcast_to(reach[:, h : h + 1], (ROWS, 128))
         reach_ref[...] = jnp.where(core == 0, 0.0, jnp.exp(run))
 
     for side, (group, ins, state_ref) in enumerate((
@@ -203,22 +204,27 @@
 
 
 def finish_kernel(side, group_ref, start_ref, reach_ref, query_ref, ready_ref, *rest):
-    out_ref = rest[-1]
-    for n in range(PER_STEP):
-        at = pl.program_id(0) * PER_STEP + n
-        head = group_ref[0] * HALF + at
-        across = jnp.dot(
-            query_ref[:, pl.ds(pl.multiple_of(head * DK, DK), DK)], get_slices(start_ref, at),
-            preferred_element_type=f32,
-        )
-        reach = column(reach_ref[...], head)
-        retained = ready_ref[side, at, :, :DV] + across * reach
+    out_ref, buf_ref, sems = rest[-3:]
+    copies = []
+    for n in range(HALF):
+        head = group_ref[0] * HALF + n
+        query = query_ref[:, pl.ds(pl.multiple_of(head * DK, DK), DK)]
+        across = jnp.dot(query, get_slices(start_ref, n), preferred_element_type=f32)
+        reach = jnp.concatenate([reach_ref[head]] * TILES, axis=1)
+        retained = ready_ref[side, n, :, :DV] + across * reach
         average = jnp.mean(retained, axis=1, keepdims=True)
         centered = retained - average
         variance = jnp.mean(centered * centered, axis=1, keepdims=True)
         normed = centered * lax.rsqrt(variance + 1e-06)
-        gated = ready_ref[side, at, :, DV:]
-        out_ref[:, n * DV : (n + 1) * DV] = (gated * normed).astype(bf16)
+        buf_ref[:, n * DV : (n + 1) * DV] = (ready_ref[side, n, :, DV:] * normed).astype(bf16)
+        place = pl.ds(pl.multiple_of(head * DV, DV), DV)
+        copies.extend(start_all((
+            pltpu.make_async_copy(
+                buf_ref.at[:, pl.ds(n * DV, DV)], out_ref.at[:, place], sems.at[n]
+            ),
+        )))
+    for copy in copies:
+        copy.wait()
 
 
 def call(kernel, grid, in_specs, out_specs, out_shape, scratch, flops, aliases=None):
@@ -300,8 +306,8 @@
         within_kernel, HALF,
         [heads(DK), heads(DK), heads(DV), heads(DV),
          theirs(DK), theirs(DK), theirs(DV), theirs(DV), here, here, decays, decays],
-        [block, pl.BlockSpec((ROWS, HEADS), lambda i, c: (0, 0))],
-        [pltpu.HBM((2, HALF, ROWS, 2 * DV), f32), pltpu.HBM((ROWS, HEADS), f32)],
+        [block, pl.BlockSpec((HEADS, ROWS, 128), lambda i, c: (0, 0, 0))],
+        [pltpu.HBM((2, HALF, ROWS, 2 * DV), f32), pltpu.HBM((HEADS, ROWS, 128), f32)],
         [table, pltpu.VMEM((HEADS, ROWS), f32), table], 4 * flops,
     )(core, far(queries), key_far, value_far, far(gate_input), far(queries), key_far, value_far,
       far(gate_input), near(own_first), near(their_first), decay_far, other_decay)
@@ -318,14 +324,17 @@
     start = lax.all_to_all(starts, everyone, 0, 0, tiled=True)
     their_start = lax.ppermute(start, "core", swap)
 
-    specs = [here, pl.BlockSpec((ROWS, HEADS), lambda i, c: (0, 0)), here, here]
+    specs = [here] * 4
     result = pltpu.HBM((ROWS, HEADS * DV), bf16)
-    done = call(partial(finish_kernel, 0), steps, specs, wide(DV), result, [], flops)(
-        core, near(start), far(reach), near(queries), near(within)
+    scratch = [pltpu.VMEM((ROWS, HALF * DV), bf16), pltpu.SemaphoreType.DMA((HALF,))]
+    ready = [near(reach), near(queries), near(within)]
+    done = call(partial(finish_kernel, 0), 1, specs, away, result, scratch, flops)(
+        core, near(start), *ready
     )
     return call(
-        partial(finish_kernel, 1), steps, specs + [away], wide(DV), result, [], flops, {5: 0},
-    )(other, near(their_start), far(reach), near(queries), near(within), done)
+        partial(finish_kernel, 1), 1, specs + [away], away, result, scratch, flops,
+        {5: 0},
+    )(other, near(their_start), *ready, done)
 
 
 def solution(mesh):

time: 126 us -> 128 us (1.016)
  local copies, waits for them, and re-layouts: 5.77 us -> 7.36 us
    pallas_call x2, Pallas kernels: 8.19 us -> 6.47 us  [the longest x1 4.03 us: shards(): call(partial(finish_kernel, 0), 1, specs, away, result, scratch, flops)]
    unnamed x6 -> x8, local copies, waits for them, and re-layouts: 5.77 us -> 7.36 us
  transfers between devices with their start and end apart: 6 -> 6, of which waited for: 2 -> 2; matrix products, arithmetic and copies ran while one was open for 0% -> 0% of each run, Pallas kernels for 20% -> 21%
where the time goes in v9:
time: 128 us; the launch traced here: 127 us
  blocking collectives  42.2 us (33%)
  Pallas kernels  35.4 us (28%)
  waiting for transfers between devices  28.4 us (22%)
  starting transfers between devices  13.5 us (11%)
  local copies, waits for them, and re-layouts  7.36 us (6%)
    all_to_all x1, blocking collectives, shards(): collected = lax.all_to_all(block_state, everyone, 0, 0, tiled=True)  42.2 us
    all_to_all x1, waiting for transfers between devices, shards(): start = lax.all_to_all(starts, everyone, 0, 0, tiled=True)  24.4 us
    pallas_call x1, Pallas kernels, shards(): call(within_kernel, HALF, [heads(DK), heads(DK), heads(DV), heads(DV), th...  18.2 us
    unnamed x8, local copies, waits for them, and re-layouts  7.36 us
    all_to_all x1, starting transfers between devices, shards(): start = lax.all_to_all(starts, everyone, 0, 0, tiled=True)  6 us
    pallas_call x1, Pallas kernels, shards(): call(own_kernel, steps, [wide(DK), wide(DV), decays, here], [here, here,...  4.37 us
    ppermute x1, starting transfers between devices, shards(): their_start = lax.ppermute(start, 'core', swap)  4.15 us
    pallas_call x1, Pallas kernels, shards(): call(partial(finish_kernel, 0), 1, specs, away, result, scratch, flops)  4.03 us
  transfers between devices with their start and end apart: 6, of which 2 were waited for; matrix products, arithmetic and copies ran while one was open for 0% of the time, Pallas kernels for 21%

profile of v9, /device:TPU:1, one launch (start us, length us, event | category | flops | bytes accessed | tf_op | source)
XLA Modules:
  0.0 127.0 jit_solution(9449522515877604023)
XLA Ops:
  0.0 3.0 %shard_map.55.theirs_ref = bf16[65,128,128]{2,1,0:T(8,128)(2,1)S(1)} custom-call(s32[1]{0:T(128)S(6)} %sub.3.group_ref, bf16[256,4096]{1,0:T(8,128)(2,1)} %refs_5_.1, bf16[256,8192]{1,0:T(8,128)(2,1)} %refs_6_.1, bf16[16,256]{1,0:T(8,128)(2,1)} %bitcast.2), custom_call_target="tpu_custom_call" | custom-call | flops 536870912 | tf_op jit(solution)/shard_map/pallas_call | solution.py:280
  3.0 1.5 %collective-permute-start = (bf16[65,128,128]{2,1,0:T(8,128)(2,1)S(1)}, bf16[65,128,128]{2,1,0:T(8,128)(2,1)S(1)}, u32[]{:S(2)}, u32[]{:S(2)}) collective-permute-start(bf16[65,128,128]{2,1,0:T(8,128)(2,1)S(1)} %shard_map.55.theirs_ref), channel_id=1, source_target_pairs={{0,1},{1,0},{2,3},{3,2},{4,5},{5,4},{6,7},{7,6},{8,9},{9,8},{10,11... | collective-permute-start | bytes 6389768 | tf_op jit(solution)/shard_map/ppermute | solution.py:284
  4.5 4.4 %shard_map.56 = (bf16[64,128,128]{2,1,0:T(8,128)(2,1)S(1)}, f32[16,128]{1,0:T(8,128)S(1)}, bf16[64,128,128]{2,1,0:T(8,128)(2,1)}, bf16[64,128,128]{2,1,0:T(8,128)(2,1)}) custom-call(s32[1]{0:T(128)} %bitcast.group_ref.core_ref, bf16[256,4096]{1,0:T(8,128)(2,1)} %refs_5_.1, bf16[256,8192]{1,0:T(8,128)(2,1)} %refs_6_.1, bf16[16,256]{1,0:T(8,128)(2,1)} %bitcast.3, ...), custom_call_target="tpu_custom_call" | custom-call | flops 536870912 | tf_op jit(solution)/shard_map/pallas_call | solution.py:285
  8.9 0.0 collective-permute-done.got_ref
  8.9 1.6 %shard_map.57 = bf16[64,136,128]{2,1,0:T(8,128)(2,1)} custom-call(s32[1]{0:T(128)} %bitcast.group_ref.core_ref, bf16[64,128,128]{2,1,0:T(8,128)(2,1)S(1)} %get-tuple-element.11.own_ref, bf16[65,128,128]{2,1,0:T(8,128)(2,1)S(1)} %collective-permute-done.got_ref, f32[16,128]{1,0:T(8,128)S(1)} %get-tuple-element.12.total_ref), custom_call_target="tpu_custom_call" | custom-call | flops 67108864 | tf_op jit(solution)/shard_map/pallas_call | solution.py:291
  10.5 42.2 %all_to_all.10.in_ref = bf16[64,136,128]{2,1,0:T(8,128)(2,1)S(1)} all-to-all(bf16[64,136,128]{2,1,0:T(8,128)(2,1)} %shard_map.57), channel_id=1, replica_groups=mesh['seq'=4,'chip'=16,'core'=2] {'seq','chip'}, dimensions={0} | all-to-all | bytes 4456448 | tf_op jit(solution)/shard_map/all_to_all | solution.py:299
  52.7 1.8 %prefix.1 = bf16[64,128,128]{2,1,0:T(8,128)(2,1)} custom-call(bf16[64,136,128]{2,1,0:T(8,128)(2,1)S(1)} %all_to_all.10.in_ref), custom_call_target="tpu_custom_call" | custom-call | flops 10000000000 | tf_op jit(solution)/shard_map/prefix/pallas_call | solution.py:315
  54.5 0.0 copy-start.3
  54.5 6.0 %all-to-all-start.1 = ((bf16[64,128,128]{2,1,0:T(8,128)(2,1)}), bf16[64,128,128]{2,1,0:T(8,128)(2,1)}, u32[]{:S(2)}, u32[]{:S(2)}) async-start(bf16[64,128,128]{2,1,0:T(8,128)(2,1)} %prefix.1), calls=%async_computation.1 | async-start | bytes 4194304 | tf_op jit(solution)/shard_map/all_to_all | solution.py:324
  60.5 1.8 %collective-permute-start.2 = (bf16[64,128,128]{2,1,0:T(8,128)(2,1)}, bf16[64,128,128]{2,1,0:T(8,128)(2,1)}, u32[]{:S(2)}, u32[]{:S(2)}) collective-permute-start(bf16[64,128,128]{2,1,0:T(8,128)(2,1)} %get-tuple-element.13), channel_id=1, source_target_pairs={{0,1},{1,0},{2,3},{3,2},{4,5},{5,4},{6,7},{7,6},{8,9},{9,8},{10,11... | collective-permute-start | bytes 6291464 | tf_op jit(solution)/shard_map/ppermute | solution.py:301
  62.3 0.0 copy-start.1
  62.3 0.1 collective-permute-start.3
  62.4 24.4 %all-to-all-done.1.start_ref = bf16[64,128,128]{2,1,0:T(8,128)(2,1)} async-done(((bf16[64,128,128]{2,1,0:T(8,128)(2,1)}), bf16[64,128,128]{2,1,0:T(8,128)(2,1)}, u32[]{:S(2)}, u32[]{:S(2)}) %all-to-all-start.1) | async-done | bytes 2097184 | tf_op jit(solution)/shard_map/all_to_all | solution.py:324
  86.8 4.2 %collective-permute-start.1 = (bf16[64,128,128]{2,1,0:T(8,128)(2,1)}, bf16[64,128,128]{2,1,0:T(8,128)(2,1)S(1)}, u32[]{:S(2)}, u32[]{:S(2)}) collective-permute-start(bf16[64,128,128]{2,1,0:T(8,128)(2,1)} %all-to-all-done.1.start_ref), channel_id=1, source_target_pairs={{0,1},{1,0},{2,3},{3,2},{4,5},{5,4},{6,7},{7,6},{8,9},{9,8},{10,11... | collective-permute-start | bytes 6291464 | tf_op jit(solution)/shard_map/ppermute | solution.py:325
  91.0 0.0 copy-done.3
  91.0 0.0 collective-permute-start.4
  91.0 4.0 %collective-permute-done.4.refs_11_ = bf16[16,256]{1,0:T(8,128)(2,1)S(1)} collective-permute-done((bf16[16,256]{1,0:T(8,128)(2,1)S(1)}, bf16[16,256]{1,0:T(8,128)(2,1)S(1)}, u32[]{:S(2)}, u32[]{:S(2)}) %collective-permute-start.4) | collective-permute-done | bytes 8224 | tf_op jit(solution)/shard_map/ppermute | solution.py:302
  95.0 0.0 collective-permute-done.2.refs_8_
  95.0 0.0 collective-permute-done.3.refs_9_
  95.0 18.2 %shard_map.58 = (f32[2,8,256,1024]{3,2,1,0:T(8,128)}, f32[16,256,128]{2,1,0:T(8,128)}) custom-call(s32[1]{0:T(128)} %bitcast.group_ref.core_ref, bf16[256,4096]{1,0:T(8,128)(2,1)} %query_ref.3, bf16[256,4096]{1,0:T(8,128)(2,1)} %refs_5_.1, bf16[256,8192]{1,0:T(8,128)(2,1)} %refs_6_.1, bf16[256,8192]{1,0:T(8,128)(2,1)} %refs_7_.1, ...), custom_call_target="tpu_custom_call" | custom-call | flops 2147483648 | tf_op jit(solution)/shard_map/pallas_call | solution.py:305
  113.2 0.0 copy-done.1
  113.2 0.0 copy-start
  113.2 5.8 %copy-done = f32[2,8,256,1024]{3,2,1,0:T(8,128)S(1)} copy-done((f32[2,8,256,1024]{3,2,1,0:T(8,128)S(1)}, f32[2,8,256,1024]{3,2,1,0:T(8,128)}, u32[]{:S(2)}) %copy-start) | copy-done | bytes 16777240
  118.9 0.0 copy-start.2
  118.9 1.6 %copy-done.2 = f32[16,256,128]{2,1,0:T(8,128)S(1)} copy-done((f32[16,256,128]{2,1,0:T(8,128)S(1)}, f32[16,256,128]{2,1,0:T(8,128)}, u32[]{:S(2)}) %copy-start.2) | copy-done | bytes 2097176
  120.5 4.0 %shard_map.59.rest_0_ = bf16[256,8192]{1,0:T(8,128)(2,1)} custom-call(s32[1]{0:T(128)} %bitcast.group_ref.core_ref, bf16[64,128,128]{2,1,0:T(8,128)(2,1)} %all-to-all-done.1.start_ref, f32[16,256,128]{2,1,0:T(8,128)S(1)} %copy-done.2, bf16[256,4096]{1,0:T(8,128)(2,1)S(1)} %copy-done.1, f32[2,8,256,1024]{3,2,1,0:T(8,128)S(1)} %copy-done), custom_call_target="tpu_custom_call" | custom-call | flops 536870912 | tf_op jit(solution)/shard_map/pallas_call | solution.py:331
  124.6 0.0 collective-permute-done.1.start_ref
  124.6 2.4 %shard_map.60 = bf16[256,8192]{1,0:T(8,128)(2,1)} custom-call(s32[1]{0:T(128)S(6)} %sub.3.group_ref, bf16[64,128,128]{2,1,0:T(8,128)(2,1)S(1)} %collective-permute-done.1.start_ref, f32[16,256,128]{2,1,0:T(8,128)S(1)} %copy-done.2, bf16[256,4096]{1,0:T(8,128)(2,1)S(1)} %copy-done.1, f32[2,8,256,1024]{3,2,1,0:T(8,128)S(1)} %copy-done, ...), custom_call_target="tpu_custom_call", output_to_operand_aliasing={{}: (5, {})} | custom-call | flops 536870912 | tf_op jit(solution)/shard_map/pallas_call | solution.py:334
Async XLA Ops:
  3.0 5.8 %collective-permute-start = (bf16[65,128,128]{2,1,0:T(8,128)(2,1)S(1)}, bf16[65,128,128]{2,1,0:T(8,128)(2,1)S(1)}, u32[]{:S(2)}, u32[]{:S(2)}) collective-permute-start(bf16[65,128,128]{2,1,0:T(8,128)(2,1)S(1)} %shard_map.55.theirs_ref), channel_id=1, source_target_pairs={{0,1},{1,0},{2,3},{3,2},{4,5},{5,4},{6,7},{7,6},{8,9},{9,8},{10,11... | collective-permute-start | bytes 6389768 | tf_op jit(solution)/shard_map/ppermute | solution.py:284
  54.5 36.5 %copy-start.3 = (bf16[256,16]{0,1:T(8,128)(2,1)S(1)}, bf16[256,16]{0,1:T(8,128)(2,1)}, u32[]{:S(2)}) copy-start(bf16[256,16]{0,1:T(8,128)(2,1)} %param.8) | copy-start | bytes 24580
  54.5 32.3 %all-to-all-start.1 = ((bf16[64,128,128]{2,1,0:T(8,128)(2,1)}), bf16[64,128,128]{2,1,0:T(8,128)(2,1)}, u32[]{:S(2)}, u32[]{:S(2)}) async-start(bf16[64,128,128]{2,1,0:T(8,128)(2,1)} %prefix.1), calls=%async_computation.1 | async-start | bytes 4194304 | tf_op jit(solution)/shard_map/all_to_all | solution.py:324
  60.5 34.5 %collective-permute-start.2 = (bf16[64,128,128]{2,1,0:T(8,128)(2,1)}, bf16[64,128,128]{2,1,0:T(8,128)(2,1)}, u32[]{:S(2)}, u32[]{:S(2)}) collective-permute-start(bf16[64,128,128]{2,1,0:T(8,128)(2,1)} %get-tuple-element.13), channel_id=1, source_target_pairs={{0,1},{1,0},{2,3},{3,2},{4,5},{5,4},{6,7},{7,6},{8,9},{9,8},{10,11... | collective-permute-start | bytes 6291464 | tf_op jit(solution)/shard_map/ppermute | solution.py:301
  62.3 50.9 %copy-start.1 = (bf16[256,4096]{1,0:T(8,128)(2,1)S(1)}, bf16[256,4096]{1,0:T(8,128)(2,1)}, u32[]{:S(2)}) copy-start(bf16[256,4096]{1,0:T(8,128)(2,1)} %query_ref.3) | copy-start | bytes 6291460
  62.3 32.7 %collective-permute-start.3 = (bf16[64,128,128]{2,1,0:T(8,128)(2,1)}, bf16[64,128,128]{2,1,0:T(8,128)(2,1)}, u32[]{:S(2)}, u32[]{:S(2)}) collective-permute-start(bf16[64,128,128]{2,1,0:T(8,128)(2,1)} %get-tuple-element.14), channel_id=1, source_target_pairs={{0,1},{1,0},{2,3},{3,2},{4,5},{5,4},{6,7},{7,6},{8,9},{9,8},{10,11... | collective-permute-start | bytes 6291464 | tf_op jit(solution)/shard_map/ppermute | solution.py:300
  86.8 37.7 %collective-permute-start.1 = (bf16[64,128,128]{2,1,0:T(8,128)(2,1)}, bf16[64,128,128]{2,1,0:T(8,128)(2,1)S(1)}, u32[]{:S(2)}, u32[]{:S(2)}) collective-permute-start(bf16[64,128,128]{2,1,0:T(8,128)(2,1)} %all-to-all-done.1.start_ref), channel_id=1, source_target_pairs={{0,1},{1,0},{2,3},{3,2},{4,5},{5,4},{6,7},{7,6},{8,9},{9,8},{10,11... | collective-permute-start | bytes 6291464 | tf_op jit(solution)/shard_map/ppermute | solution.py:325
  91.0 4.0 %collective-permute-start.4 = (bf16[16,256]{1,0:T(8,128)(2,1)S(1)}, bf16[16,256]{1,0:T(8,128)(2,1)S(1)}, u32[]{:S(2)}, u32[]{:S(2)}) collective-permute-start(bf16[16,256]{1,0:T(8,128)(2,1)S(1)} %bitcast.5), channel_id=1, source_target_pairs={{0,1},{1,0},{2,3},{3,2},{4,5},{5,4},{6,7},{7,6},{8,9},{9,8},{10,11... | collective-permute-start | bytes 24584 | tf_op jit(solution)/shard_map/ppermute | solution.py:302
  113.2 5.8 %copy-start = (f32[2,8,256,1024]{3,2,1,0:T(8,128)S(1)}, f32[2,8,256,1024]{3,2,1,0:T(8,128)}, u32[]{:S(2)}) copy-start(f32[2,8,256,1024]{3,2,1,0:T(8,128)} %get-tuple-element.16.ready_ref) | copy-start | bytes 50331652
  118.9 1.6 %copy-start.2 = (f32[16,256,128]{2,1,0:T(8,128)S(1)}, f32[16,256,128]{2,1,0:T(8,128)}, u32[]{:S(2)}) copy-start(f32[16,256,128]{2,1,0:T(8,128)} %get-tuple-element.15.reach_ref) | copy-start | bytes 6291460

commit v10 on v9

--- a/solution.py
+++ b/solution.py
@@ -18,7 +18,7 @@
 PIECE = DK // SLICES
 TILES = DV // 128
 SLICE = PIECE * TILES
-SENT = SLICE + 8
+LINE = 4
 PER_STEP = 4
 MIB = 2**20
 LIMIT = 20
@@ -128,7 +128,7 @@
     states_into((out_ref, own_copy_ref), group_ref[0], step, key_ref, value_ref, fade_ref)
 
 
-def combine_kernel(core_ref, own_ref, got_ref, total_ref, out_ref, buf_ref, rate_ref, sems):
+def combine_kernel(core_ref, own_ref, got_ref, total_ref, out_ref, damp_ref, buf_ref, rate_ref, sems):
     is_first = core_ref[0] == 0
     total = total_ref[...]
     thirds = [got_ref[CHIPS, k * HEADS : (k + 1) * HEADS, :].astype(f32) for k in range(3)]
@@ -136,19 +136,15 @@
     rate_ref[0] = jnp.exp(jnp.where(is_first, other, 0.0))
     rate_ref[1] = jnp.exp(jnp.where(is_first, 0.0, total))
     rate_ref[2] = jnp.exp(total + other)
-    rows = lax.broadcasted_iota(jnp.int32, (8, 128), 0)
+    damp_ref[...] = rate_ref[2, pl.ds(pl.multiple_of(core_ref[0] * HALF, HALF), HALF), :]
     copies = []
     for n in range(HALF):
         head = pl.ds(core_ref[0] * HALF + n, 1)
         own_rate = rate_ref[0, head, :]
         got_rate = rate_ref[1, head, :]
-        high, middle, low = thirds_of(rate_ref[2, head, :])
-        parts = jnp.where(rows == 0, high, jnp.where(rows == 1, middle, low))
-        parts = parts.astype(bf16)
         for o in range(n * SLICES, (n + 1) * SLICES):
             both = own_ref[o].astype(f32) * own_rate + got_ref[o].astype(f32) * got_rate
-            buf_ref[o, :SLICE, :] = both.astype(bf16)
-            buf_ref[o, SLICE:SENT, :] = parts
+            buf_ref[o] = both.astype(bf16)
         block = pl.ds(n * SLICES, SLICES)
         copies.extend(start_all((
             pltpu.make_async_copy(buf_ref.at[block], out_ref.at[block], sems.at[n]),
@@ -158,8 +154,8 @@
 
 
 def within_kernel(core_ref, *refs):
-    own, theirs, (got_ref, first_ref, decay_ref, other_ref) = refs[0:4], refs[4:8], refs[8:12]
-    out_ref, reach_out, run_ref, rows_ref, reach_ref = refs[12:]
+    own, theirs, (got_ref, first_ref, decay_ref, other_ref) = refs[0:3], refs[3:6], refs[6:10]
+    out_ref, reach_out, run_ref, rows_ref, reach_ref = refs[10:]
     step = pl.program_id(0)
     core = core_ref[0]
 
@@ -177,7 +173,7 @@
     for side, (group, ins, state_ref) in enumerate((
         (core, own, got_ref), (1 - core, theirs, first_ref),
     )):
-        query_ref, key_ref, value_ref, gate_ref = ins
+        query_ref, key_ref, value_ref = ins
         head = group * HALF + step
         query = query_ref[...]
         scores = lax.dot_general(
@@ -189,21 +185,24 @@
         local = jnp.dot(weights, value_ref[...], preferred_element_type=f32)
         before = jnp.dot(query, get_slices(state_ref, step), preferred_element_type=f32)
         inner = local + before * column(reach_ref[...], head)
-        out_ref[side, 0, :, :DV] = inner
-        gate = 0.5 * gate_ref[...].astype(f32)
-        out_ref[side, 0, :, DV:] = gate + gate * jnp.tanh(gate)
-
-
-def prefix_kernel(in_ref, out_ref):
+        out_ref[side, 0] = inner
+
+
+def prefix_kernel(place_ref, in_ref, *refs):
+    ins, out_ref, damp_ref = refs[:LINE], refs[LINE], refs[LINE + 1]
+    for d in range(LINE):
+        damp_ref[d * LINE * LINE : (d + 1) * LINE * LINE] = ins[d][...]
+    x, y, z = place_ref[0], place_ref[1], place_ref[2]
+    head = pl.ds((x * LINE * LINE + y * LINE + z) // SLICES, 1)
     state = jnp.zeros((SLICE, 128), f32)
     for b in range(CHIPS):
-        parts = in_ref[b, SLICE:SENT, :].astype(f32)
-        damping = parts[0:1] + parts[1:2] + parts[2:3]
+        apart = [(here + LINE - b // far % LINE) % LINE for here, far in ((x, 16), (y, 4), (z, 1))]
+        damping = damp_ref[apart[0] * LINE * LINE + apart[1] * LINE + apart[2], head, :]
         out_ref[b] = state.astype(bf16)
-        state = damping * state + in_ref[b, :SLICE, :].astype(f32)
-
-
-def finish_kernel(side, group_ref, start_ref, reach_ref, query_ref, ready_ref, *rest):
+        state = damping * state + in_ref[b].astype(f32)
+
+
+def finish_kernel(side, group_ref, start_ref, reach_ref, query_ref, ready_ref, gate_ref, *rest):
     out_ref, buf_ref, sems = rest[-3:]
     copies = []
     for n in range(HALF):
@@ -211,13 +210,15 @@
         query = query_ref[:, pl.ds(pl.multiple_of(head * DK, DK), DK)]
         across = jnp.dot(query, get_slices(start_ref, n), preferred_element_type=f32)
         reach = jnp.concatenate([reach_ref[head]] * TILES, axis=1)
-        retained = ready_ref[side, n, :, :DV] + across * reach
+        retained = ready_ref[side, n] + across * reach
         average = jnp.mean(retained, axis=1, keepdims=True)
         centered = retained - average
         variance = jnp.mean(centered * centered, axis=1, keepdims=True)
         normed = centered * lax.rsqrt(variance + 1e-06)
-        buf_ref[:, n * DV : (n + 1) * DV] = (ready_ref[side, n, :, DV:] * normed).astype(bf16)
         place = pl.ds(pl.multiple_of(head * DV, DV), DV)
+        gate = 0.5 * gate_ref[:, place].astype(f32)
+        gated = (gate + gate * jnp.tanh(gate)) * normed
+        buf_ref[:, n * DV : (n + 1) * DV] = gated.astype(bf16)
         copies.extend(start_all((
             pltpu.make_async_copy(
                 buf_ref.at[:, pl.ds(n * DV, DV)], out_ref.at[:, place], sems.at[n]
@@ -254,11 +255,34 @@
     return pltpu.with_memory_space_constraint(value, pltpu.VMEM)
 
 
+def shifted(value, axis):
+    shifts = [[(i, (i + d) % LINE) for i in range(LINE)] for d in range(1, LINE)]
+    return [value] + [lax.ppermute(value, axis, pairs) for pairs in shifts]
+
+
+def join_kernel(*refs):
+    size = refs[0].shape[0]
+    for d, ref in enumerate(refs[:LINE]):
+        refs[LINE][d * size : (d + 1) * size] = ref[...]
+
+
+def joined(parts):
+    here = pl.BlockSpec(memory_space=pltpu.VMEM)
+    return pl.pallas_call(
+        join_kernel,
+        out_shape=pltpu.VMEM((LINE * parts[0].shape[0], *parts[0].shape[1:]), f32),
+        in_specs=[here] * LINE,
+        out_specs=here,
+        compiler_params=pltpu.CompilerParams(vmem_limit_bytes=LIMIT * MIB),
+        name="join",
+    )(*map(near, parts))
+
+
 def shards(queries, key_vectors, values, decay_log, gate_input):
     core = lax.axis_index("core").astype(jnp.int32).reshape(1)
     other = 1 - core
     swap = [(0, 1), (1, 0)]
-    everyone = ("seq", "chip")
+    everyone = ("x", "y", "z")
     decay = decay_log.T
 
     steps = HALF // PER_STEP
@@ -288,57 +312,55 @@
         [slices, pltpu.VMEM((HEADS, 128), f32), stored, stored],
         [table], flops,
     )(core, key_far, value_far, decay_far, near(theirs_state))
-    block_state = call(
-        combine_kernel, 1, [here, here, here], away,
-        pltpu.HBM((CHIPS, SENT, 128), bf16),
+    block_state, damping = call(
+        combine_kernel, 1, [here, here, here], [away, here],
+        [pltpu.HBM((CHIPS, SLICE, 128), bf16), pltpu.VMEM((HALF, 128), f32)],
         [
-            pltpu.VMEM((CHIPS, SENT, 128), bf16), pltpu.VMEM((3, HEADS, 128), f32),
+            pltpu.VMEM((CHIPS, SLICE, 128), bf16), pltpu.VMEM((3, HEADS, 128), f32),
             pltpu.SemaphoreType.DMA((HALF,)),
         ], flops // 8,
     )(core, near(own_state), near(got), near(totals))
     collected = lax.all_to_all(block_state, everyone, 0, 0, tiled=True)
+    along_line = joined(shifted(damping[None], "z"))
+    along_plane = joined(shifted(along_line, "y"))
+    dampings = shifted(along_plane, "x")
     their_first = lax.ppermute(late_own, "core", swap)
     own_first = lax.ppermute(late_theirs, "core", swap)
     other_decay = lax.ppermute(decay, "core", swap)
 
-    block = pl.BlockSpec((2, 1, ROWS, 2 * DV), lambda i, c: (0, i, 0, 0))
+    block = pl.BlockSpec((2, 1, ROWS, DV), lambda i, c: (0, i, 0, 0))
     within, reach = call(
         within_kernel, HALF,
-        [heads(DK), heads(DK), heads(DV), heads(DV),
-         theirs(DK), theirs(DK), theirs(DV), theirs(DV), here, here, decays, decays],
+        [heads(DK), heads(DK), heads(DV), theirs(DK), theirs(DK), theirs(DV), here, here, decays, decays],
         [block, pl.BlockSpec((HEADS, ROWS, 128), lambda i, c: (0, 0, 0))],
-        [pltpu.HBM((2, HALF, ROWS, 2 * DV), f32), pltpu.HBM((HEADS, ROWS, 128), f32)],
+        [pltpu.HBM((2, HALF, ROWS, DV), f32), pltpu.HBM((HEADS, ROWS, 128), f32)],
         [table, pltpu.VMEM((HEADS, ROWS), f32), table], 4 * flops,
-    )(core, far(queries), key_far, value_far, far(gate_input), far(queries), key_far, value_far,
-      far(gate_input), near(own_first), near(their_first), decay_far, other_decay)
-
-    starts = pl.pallas_call(
-        prefix_kernel,
-        out_shape=slices,
-        in_specs=[here],
-        out_specs=here,
-        compiler_params=pltpu.CompilerParams(vmem_limit_bytes=LIMIT * MIB),
-        cost_estimate=pl.CostEstimate(flops=10**10, transcendentals=0, bytes_accessed=0),
-        name="prefix",
-    )(near(collected))
+    )(core, far(queries), key_far, value_far, far(queries), key_far, value_far,
+      near(own_first), near(their_first), decay_far, other_decay)
+
+    place = jnp.stack([lax.axis_index(a) for a in ("x", "y", "z")]).astype(jnp.int32)
+    starts = call(
+        prefix_kernel, 1, [here] * (1 + LINE), here, slices,
+        [pltpu.VMEM((CHIPS, HALF, 128), f32)], 10**10,
+    )(place, near(collected), *map(near, dampings))
     start = lax.all_to_all(starts, everyone, 0, 0, tiled=True)
     their_start = lax.ppermute(start, "core", swap)
 
-    specs = [here] * 4
+    specs = [here] * 5
     result = pltpu.HBM((ROWS, HEADS * DV), bf16)
     scratch = [pltpu.VMEM((ROWS, HALF * DV), bf16), pltpu.SemaphoreType.DMA((HALF,))]
-    ready = [near(reach), near(queries), near(within)]
+    ready = [near(reach), near(queries), near(within), near(gate_input)]
     done = call(partial(finish_kernel, 0), 1, specs, away, result, scratch, flops)(
         core, near(start), *ready
     )
     return call(
         partial(finish_kernel, 1), 1, specs + [away], away, result, scratch, flops,
-        {5: 0},
+        {6: 0},
     )(other, near(their_start), *ready, done)
 
 
 def solution(mesh):
-    mesh = Mesh(mesh.devices.reshape(4, 16, 2), ("seq", "chip", "core"))
-    spec = P(("seq", "chip", "core"), None)
+    mesh = Mesh(mesh.devices.reshape(4, 4, 4, 2), ("x", "y", "z", "core"))
+    spec = P(("x", "y", "z", "core"), None)
 
     return jax.shard_map(shards, mesh=mesh, in_specs=(spec,) * 5, out_specs=spec, check_vma=False)

time: 128 us -> 133 us (1.039)
  blocking collectives: 42.2 us -> 0 us
  starting transfers between devices: 13.5 us -> 49.5 us
  waiting for transfers between devices: 28.4 us -> 44.6 us
  Pallas kernels: 35.4 us -> 31.7 us
    all_to_all x1 -> x0, blocking collectives: 42.2 us -> none  [shards(): collected = lax.all_to_all(block_state, everyone, 0, 0, tiled=True)]
    ppermute x0 -> x9, starting transfers between devices: none -> 21.9 us  [shifted(): return [value] + [lax.ppermute(value, axis, pairs) for pairs in shifts]]
    ppermute x0 -> x9, waiting for transfers between devices: none -> 19.3 us  [shifted(): return [value] + [lax.ppermute(value, axis, pairs) for pairs in shifts]]
    all_to_all x0 -> x1, starting transfers between devices: none -> 11.3 us  [shards(): collected = lax.all_to_all(block_state, everyone, 0, 0, tiled=True)]
    pallas_call x3 -> x5, Pallas kernels: 21.6 us -> 16.6 us  [the longest x1 14 us: shards(): call(within_kernel, HALF, [heads(DK), heads(DK), heads(DV), theirs(DK), t...]
    all_to_all x1, waiting for transfers between devices: 24.4 us -> 21.3 us  [shards(): start = lax.all_to_all(starts, everyone, 0, 0, tiled=True)]
    ppermute x1, starting transfers between devices: 1.8 us -> 3.7 us  [shards(): own_first = lax.ppermute(late_theirs, 'core', swap)]
    unnamed x8 -> x12, local copies, waits for them, and re-layouts: 7.36 us -> 6.27 us
  transfers between devices with their start and end apart: 6 -> 16, of which waited for: 2 -> 9; matrix products, arithmetic and copies ran while one was open for 0% -> 0% of each run, Pallas kernels for 21% -> 17%
where the time goes in v10:
time: 133 us; the launch traced here: 132 us
  starting transfers between devices  49.5 us (37%)
  waiting for transfers between devices  44.6 us (34%)
  Pallas kernels  31.7 us (24%)
  local copies, waits for them, and re-layouts  6.27 us (5%)
    ppermute x9, starting transfers between devices, shifted(): return [value] + [lax.ppermute(value, axis, pairs) for pairs in shifts]  21.9 us
    all_to_all x1, waiting for transfers between devices, shards(): start = lax.all_to_all(starts, everyone, 0, 0, tiled=True)  21.3 us
    ppermute x9, waiting for transfers between devices, shifted(): return [value] + [lax.ppermute(value, axis, pairs) for pairs in shifts]  19.3 us
    pallas_call x1, Pallas kernels, shards(): call(within_kernel, HALF, [heads(DK), heads(DK), heads(DV), theirs(DK), t...  14 us
    all_to_all x1, starting transfers between devices, shards(): collected = lax.all_to_all(block_state, everyone, 0, 0, tiled=True)  11.3 us
    unnamed x12, local copies, waits for them, and re-layouts  6.27 us
    all_to_all x1, starting transfers between devices, shards(): start = lax.all_to_all(starts, everyone, 0, 0, tiled=True)  5.7 us
    ppermute x1, starting transfers between devices, shards(): their_start = lax.ppermute(start, 'core', swap)  5.33 us
  transfers between devices with their start and end apart: 16, of which 9 were waited for; matrix products, arithmetic and copies ran while one was open for 0% of the time, Pallas kernels for 17%

profile of v10, /device:TPU:1, one launch (start us, length us, event | category | flops | bytes accessed | tf_op | source)
XLA Modules:
  0.0 132.5 jit_solution(10995151634835195971)
XLA Ops:
  0.0 3.0 %shard_map.55.theirs_ref = bf16[65,128,128]{2,1,0:T(8,128)(2,1)S(1)} custom-call(s32[1]{0:T(128)S(6)} %sub.3.group_ref, bf16[256,4096]{1,0:T(8,128)(2,1)} %refs_4_.1, bf16[256,8192]{1,0:T(8,128)(2,1)} %refs_5_.1, bf16[16,256]{1,0:T(8,128)(2,1)} %bitcast.10), custom_call_target="tpu_custom_call" | custom-call | flops 536870912 | tf_op jit(solution)/shard_map/pallas_call | solution.py:304
  3.0 1.5 %collective-permute-start = (bf16[65,128,128]{2,1,0:T(8,128)(2,1)S(1)}, bf16[65,128,128]{2,1,0:T(8,128)(2,1)S(1)}, u32[]{:S(2)}, u32[]{:S(2)}) collective-permute-start(bf16[65,128,128]{2,1,0:T(8,128)(2,1)S(1)} %shard_map.55.theirs_ref), channel_id=1, source_target_pairs={{0,1},{1,0},{2,3},{3,2},{4,5},{5,4},{6,7},{7,6},{8,9},{9,8},{10,11... | collective-permute-start | bytes 6389768 | tf_op jit(solution)/shard_map/ppermute | solution.py:308
  4.5 4.4 %shard_map.56 = (bf16[64,128,128]{2,1,0:T(8,128)(2,1)S(1)}, f32[16,128]{1,0:T(8,128)S(1)}, bf16[64,128,128]{2,1,0:T(8,128)(2,1)}, bf16[64,128,128]{2,1,0:T(8,128)(2,1)}) custom-call(s32[1]{0:T(128)} %bitcast.group_ref.core_ref, bf16[256,4096]{1,0:T(8,128)(2,1)} %refs_4_.1, bf16[256,8192]{1,0:T(8,128)(2,1)} %refs_5_.1, bf16[16,256]{1,0:T(8,128)(2,1)} %bitcast.11, ...), custom_call_target="tpu_custom_call" | custom-call | flops 536870912 | tf_op jit(solution)/shard_map/pallas_call | solution.py:309
  8.9 0.0 collective-permute-done.got_ref
  8.9 1.5 %shard_map.57 = (bf16[64,128,128]{2,1,0:T(8,128)(2,1)}, f32[8,128]{1,0:T(8,128)S(1)}) custom-call(s32[1]{0:T(128)} %bitcast.group_ref.core_ref, bf16[64,128,128]{2,1,0:T(8,128)(2,1)S(1)} %get-tuple-element.13.own_ref, bf16[65,128,128]{2,1,0:T(8,128)(2,1)S(1)} %collective-permute-done.got_ref, f32[16,128]{1,0:T(8,128)S(1)} %get-tuple-element.14.total_ref), custom_call_target="tpu_custom_call" | custom-call | flops 67108864 | tf_op jit(solution)/shard_map/pallas_call | solution.py:315
  10.4 11.3 %all-to-all-start = ((bf16[64,128,128]{2,1,0:T(8,128)(2,1)}), bf16[64,128,128]{2,1,0:T(8,128)(2,1)S(1)}, u32[]{:S(2)}, u32[]{:S(2)}) async-start(bf16[64,128,128]{2,1,0:T(8,128)(2,1)} %get-tuple-element.15), calls=%async_computation | async-start | bytes 4194304 | tf_op jit(solution)/shard_map/all_to_all | solution.py:323
  21.7 2.3 %collective-permute-start.3 = (f32[1,8,128]{2,1,0:T(8,128)S(1)}, f32[1,8,128]{2,1,0:T(8,128)S(1)}, u32[]{:S(2)}, u32[]{:S(2)}) collective-permute-start(f32[1,8,128]{2,1,0:T(8,128)S(1)} %bitcast.6), channel_id=1, source_target_pairs={{0,6},{2,0},{4,2},{6,4},{1,7},{3,1},{5,3},{7,5},{8,14},{10,8},{12,... | collective-permute-start | bytes 12296 | tf_op jit(solution)/shard_map/ppermute | solution.py:260
  24.0 0.6 collective-permute-start.2
  24.5 0.6 collective-permute-start.1
  25.1 0.0 collective-permute-done.3.refs_3_
  25.1 7.8 %collective-permute-done.2.refs_2_ = f32[1,8,128]{2,1,0:T(8,128)S(1)} collective-permute-done((f32[1,8,128]{2,1,0:T(8,128)S(1)}, f32[1,8,128]{2,1,0:T(8,128)S(1)}, u32[]{:S(2)}, u32[]{:S(2)}) %collective-permute-start.2) | collective-permute-done | bytes 4128 | tf_op jit(solution)/shard_map/ppermute | solution.py:260
  32.9 3.9 %collective-permute-done.1.refs_1_ = f32[1,8,128]{2,1,0:T(8,128)S(1)} collective-permute-done((f32[1,8,128]{2,1,0:T(8,128)S(1)}, f32[1,8,128]{2,1,0:T(8,128)S(1)}, u32[]{:S(2)}, u32[]{:S(2)}) %collective-permute-start.1) | collective-permute-done | bytes 4128 | tf_op jit(solution)/shard_map/ppermute | solution.py:260
  36.8 13.5 %collective-permute-start.6 = (f32[4,8,128]{2,1,0:T(8,128)S(1)}, f32[4,8,128]{2,1,0:T(8,128)S(1)}, u32[]{:S(2)}, u32[]{:S(2)}) collective-permute-start(f32[4,8,128]{2,1,0:T(8,128)S(1)} %join.2.refs_0_), channel_id=1, source_target_pairs={{0,24},{8,0},{16,8},{24,16},{1,25},{9,1},{17,9},{25,17},{2,26},{10... | collective-permute-start | bytes 49160 | tf_op jit(solution)/shard_map/ppermute | solution.py:260
  50.2 0.0 collective-permute-start.5
  50.2 0.7 collective-permute-start.4
  50.9 0.2 collective-permute-done.6.refs_3_
  51.1 3.2 %collective-permute-done.5.refs_2_ = f32[4,8,128]{2,1,0:T(8,128)S(1)} collective-permute-done((f32[4,8,128]{2,1,0:T(8,128)S(1)}, f32[4,8,128]{2,1,0:T(8,128)S(1)}, u32[]{:S(2)}, u32[]{:S(2)}) %collective-permute-start.5) | collective-permute-done | bytes 16416 | tf_op jit(solution)/shard_map/ppermute | solution.py:260
  54.3 0.0 collective-permute-done.4.refs_1_
  54.3 3.5 %collective-permute-start.9 = (f32[16,8,128]{2,1,0:T(8,128)S(1)}, f32[16,8,128]{2,1,0:T(8,128)S(1)}, u32[]{:S(2)}, u32[]{:S(2)}) collective-permute-start(f32[16,8,128]{2,1,0:T(8,128)S(1)} %join.3.refs_0_), channel_id=1, source_target_pairs={{0,96},{32,0},{64,32},{96,64},{1,97},{33,1},{65,33},{97,65},{2,98}... | collective-permute-start | bytes 196616 | tf_op jit(solution)/shard_map/ppermute | solution.py:260
  57.9 0.0 collective-permute-start.8
  57.9 0.8 collective-permute-start.7
  58.7 0.1 pad_add_fusion.place_ref
  58.8 0.4 collective-permute-done.9.refs_3_
  59.2 3.4 %collective-permute-done.8.refs_2_ = f32[16,8,128]{2,1,0:T(8,128)S(1)} collective-permute-done((f32[16,8,128]{2,1,0:T(8,128)S(1)}, f32[16,8,128]{2,1,0:T(8,128)S(1)}, u32[]{:S(2)}, u32[]{:S(2)}) %collective-permute-start.8) | collective-permute-done | bytes 65568 | tf_op jit(solution)/shard_map/ppermute | solution.py:260
  62.6 0.3 collective-permute-done.7.refs_1_
  63.0 0.0 all-to-all-done.in_ref
  63.0 1.0 shard_map.58
  64.0 0.0 copy-start.4
  64.0 1.3 copy-done.4
  65.3 0.0 copy-start.5
  65.3 5.7 %all-to-all-start.1 = ((bf16[64,128,128]{2,1,0:T(8,128)(2,1)}), bf16[64,128,128]{2,1,0:T(8,128)(2,1)}, u32[]{:S(2)}, u32[]{:S(2)}) async-start(bf16[64,128,128]{2,1,0:T(8,128)(2,1)} %copy-done.4), calls=%async_computation.1 | async-start | bytes 4194304 | tf_op jit(solution)/shard_map/all_to_all | solution.py:346
  71.0 3.7 %collective-permute-start.11 = (bf16[64,128,128]{2,1,0:T(8,128)(2,1)}, bf16[64,128,128]{2,1,0:T(8,128)(2,1)}, u32[]{:S(2)}, u32[]{:S(2)}) collective-permute-start(bf16[64,128,128]{2,1,0:T(8,128)(2,1)} %get-tuple-element.17), channel_id=1, source_target_pairs={{0,1},{1,0},{2,3},{3,2},{4,5},{5,4},{6,7},{7,6},{8,9},{9,8},{10,11... | collective-permute-start | bytes 6291464 | tf_op jit(solution)/shard_map/ppermute | solution.py:328
  74.7 0.0 copy-start.1
  74.7 0.1 collective-permute-start.12
  74.8 21.3 %all-to-all-done.1.start_ref = bf16[64,128,128]{2,1,0:T(8,128)(2,1)} async-done(((bf16[64,128,128]{2,1,0:T(8,128)(2,1)}), bf16[64,128,128]{2,1,0:T(8,128)(2,1)}, u32[]{:S(2)}, u32[]{:S(2)}) %all-to-all-start.1) | async-done | bytes 2097184 | tf_op jit(solution)/shard_map/all_to_all | solution.py:346
  96.2 5.3 %collective-permute-start.10 = (bf16[64,128,128]{2,1,0:T(8,128)(2,1)}, bf16[64,128,128]{2,1,0:T(8,128)(2,1)S(1)}, u32[]{:S(2)}, u32[]{:S(2)}) collective-permute-start(bf16[64,128,128]{2,1,0:T(8,128)(2,1)} %all-to-all-done.1.start_ref), channel_id=1, source_target_pairs={{0,1},{1,0},{2,3},{3,2},{4,5},{5,4},{6,7},{7,6},{8,9},{9,8},{10,11... | collective-permute-start | bytes 6291464 | tf_op jit(solution)/shard_map/ppermute | solution.py:347
  101.5 0.0 copy-done.5
  101.5 0.0 collective-permute-start.13
  101.5 4.0 %collective-permute-done.13.refs_9_ = bf16[16,256]{1,0:T(8,128)(2,1)S(1)} collective-permute-done((bf16[16,256]{1,0:T(8,128)(2,1)S(1)}, bf16[16,256]{1,0:T(8,128)(2,1)S(1)}, u32[]{:S(2)}, u32[]{:S(2)}) %collective-permute-start.13) | collective-permute-done | bytes 8224 | tf_op jit(solution)/shard_map/ppermute | solution.py:329
  105.5 0.0 collective-permute-done.11.refs_6_
  105.5 0.0 collective-permute-done.12.refs_7_
  105.5 0.0 copy-start.2
  105.5 14.0 %shard_map.59 = (f32[2,8,256,512]{3,2,1,0:T(8,128)}, f32[16,256,128]{2,1,0:T(8,128)}) custom-call(s32[1]{0:T(128)} %bitcast.group_ref.core_ref, bf16[256,4096]{1,0:T(8,128)(2,1)} %query_ref.3, bf16[256,4096]{1,0:T(8,128)(2,1)} %refs_4_.1, bf16[256,8192]{1,0:T(8,128)(2,1)} %refs_5_.1, bf16[256,4096]{1,0:T(8,128)(2,1)} %query_ref.3, ...), custom_call_target="tpu_custom_call" | custom-call | flops 2147483648 | tf_op jit(solution)/shard_map/pallas_call | solution.py:332
  119.5 0.0 copy-done.1
  119.5 0.0 copy-done.2
  119.5 0.0 copy-start
  119.5 3.4 %copy-done = f32[2,8,256,512]{3,2,1,0:T(8,128)S(1)} copy-done((f32[2,8,256,512]{3,2,1,0:T(8,128)S(1)}, f32[2,8,256,512]{3,2,1,0:T(8,128)}, u32[]{:S(2)}) %copy-start) | copy-done | bytes 8388632
  122.9 0.0 copy-start.3
  122.9 1.6 %copy-done.3 = f32[16,256,128]{2,1,0:T(8,128)S(1)} copy-done((f32[16,256,128]{2,1,0:T(8,128)S(1)}, f32[16,256,128]{2,1,0:T(8,128)}, u32[]{:S(2)}) %copy-start.3) | copy-done | bytes 2097176
  124.5 4.7 %shard_map.60.rest_0_ = bf16[256,8192]{1,0:T(8,128)(2,1)} custom-call(s32[1]{0:T(128)} %bitcast.group_ref.core_ref, bf16[64,128,128]{2,1,0:T(8,128)(2,1)} %all-to-all-done.1.start_ref, f32[16,256,128]{2,1,0:T(8,128)S(1)} %copy-done.3, bf16[256,4096]{1,0:T(8,128)(2,1)S(1)} %copy-done.1, f32[2,8,256,512]{3,2,1,0:T(8,128)S(1)} %copy-done, ...), custom_call_target="tpu_custom_call" | custom-call | flops 536870912 | tf_op jit(solution)/shard_map/pallas_call | solution.py:353
  129.2 0.0 collective-permute-done.10.start_ref
  129.2 3.1 %shard_map.61 = bf16[256,8192]{1,0:T(8,128)(2,1)} custom-call(s32[1]{0:T(128)S(6)} %sub.3.group_ref, bf16[64,128,128]{2,1,0:T(8,128)(2,1)S(1)} %collective-permute-done.10.start_ref, f32[16,256,128]{2,1,0:T(8,128)S(1)} %copy-done.3, bf16[256,4096]{1,0:T(8,128)(2,1)S(1)} %copy-done.1, f32[2,8,256,512]{3,2,1,0:T(8,128)S(1)} %copy-done, ...), custom_call_target="tpu_custom_call", output_to_operand_aliasing={{}: (6, {})} | custom-call | flops 536870912 | tf_op jit(solution)/shard_map/pallas_call | solution.py:356
  (2 shorter events, 0.0 us)
Async XLA Ops:
  3.0 5.8 %collective-permute-start = (bf16[65,128,128]{2,1,0:T(8,128)(2,1)S(1)}, bf16[65,128,128]{2,1,0:T(8,128)(2,1)S(1)}, u32[]{:S(2)}, u32[]{:S(2)}) collective-permute-start(bf16[65,128,128]{2,1,0:T(8,128)(2,1)S(1)} %shard_map.55.theirs_ref), channel_id=1, source_target_pairs={{0,1},{1,0},{2,3},{3,2},{4,5},{5,4},{6,7},{7,6},{8,9},{9,8},{10,11... | collective-permute-start | bytes 6389768 | tf_op jit(solution)/shard_map/ppermute | solution.py:308
  10.4 52.6 %all-to-all-start = ((bf16[64,128,128]{2,1,0:T(8,128)(2,1)}), bf16[64,128,128]{2,1,0:T(8,128)(2,1)S(1)}, u32[]{:S(2)}, u32[]{:S(2)}) async-start(bf16[64,128,128]{2,1,0:T(8,128)(2,1)} %get-tuple-element.15), calls=%async_computation | async-start | bytes 4194304 | tf_op jit(solution)/shard_map/all_to_all | solution.py:323
  21.7 3.4 %collective-permute-start.3 = (f32[1,8,128]{2,1,0:T(8,128)S(1)}, f32[1,8,128]{2,1,0:T(8,128)S(1)}, u32[]{:S(2)}, u32[]{:S(2)}) collective-permute-start(f32[1,8,128]{2,1,0:T(8,128)S(1)} %bitcast.6), channel_id=1, source_target_pairs={{0,6},{2,0},{4,2},{6,4},{1,7},{3,1},{5,3},{7,5},{8,14},{10,8},{12,... | collective-permute-start | bytes 12296 | tf_op jit(solution)/shard_map/ppermute | solution.py:260
  24.0 8.9 %collective-permute-start.2 = (f32[1,8,128]{2,1,0:T(8,128)S(1)}, f32[1,8,128]{2,1,0:T(8,128)S(1)}, u32[]{:S(2)}, u32[]{:S(2)}) collective-permute-start(f32[1,8,128]{2,1,0:T(8,128)S(1)} %bitcast.7), channel_id=1, source_target_pairs={{0,4},{2,6},{4,0},{6,2},{1,5},{3,7},{5,1},{7,3},{8,12},{10,14},{12... | collective-permute-start | bytes 12296 | tf_op jit(solution)/shard_map/ppermute | solution.py:260
  24.5 12.2 %collective-permute-start.1 = (f32[1,8,128]{2,1,0:T(8,128)S(1)}, f32[1,8,128]{2,1,0:T(8,128)S(1)}, u32[]{:S(2)}, u32[]{:S(2)}) collective-permute-start(f32[1,8,128]{2,1,0:T(8,128)S(1)} %bitcast.8), channel_id=1, source_target_pairs={{0,2},{2,4},{4,6},{6,0},{1,3},{3,5},{5,7},{7,1},{8,10},{10,12},{12... | collective-permute-start | bytes 12296 | tf_op jit(solution)/shard_map/ppermute | solution.py:260
  36.8 14.3 %collective-permute-start.6 = (f32[4,8,128]{2,1,0:T(8,128)S(1)}, f32[4,8,128]{2,1,0:T(8,128)S(1)}, u32[]{:S(2)}, u32[]{:S(2)}) collective-permute-start(f32[4,8,128]{2,1,0:T(8,128)S(1)} %join.2.refs_0_), channel_id=1, source_target_pairs={{0,24},{8,0},{16,8},{24,16},{1,25},{9,1},{17,9},{25,17},{2,26},{10... | collective-permute-start | bytes 49160 | tf_op jit(solution)/shard_map/ppermute | solution.py:260
  50.2 4.1 %collective-permute-start.5 = (f32[4,8,128]{2,1,0:T(8,128)S(1)}, f32[4,8,128]{2,1,0:T(8,128)S(1)}, u32[]{:S(2)}, u32[]{:S(2)}) collective-permute-start(f32[4,8,128]{2,1,0:T(8,128)S(1)} %join.2.refs_0_), channel_id=1, source_target_pairs={{0,16},{8,24},{16,0},{24,8},{1,17},{9,25},{17,1},{25,9},{2,18},{10... | collective-permute-start | bytes 49160 | tf_op jit(solution)/shard_map/ppermute | solution.py:260
  50.2 4.1 %collective-permute-start.4 = (f32[4,8,128]{2,1,0:T(8,128)S(1)}, f32[4,8,128]{2,1,0:T(8,128)S(1)}, u32[]{:S(2)}, u32[]{:S(2)}) collective-permute-start(f32[4,8,128]{2,1,0:T(8,128)S(1)} %join.2.refs_0_), channel_id=1, source_target_pairs={{0,8},{8,16},{16,24},{24,0},{1,9},{9,17},{17,25},{25,1},{2,10},{10... | collective-permute-start | bytes 49160 | tf_op jit(solution)/shard_map/ppermute | solution.py:260
  54.3 4.9 %collective-permute-start.9 = (f32[16,8,128]{2,1,0:T(8,128)S(1)}, f32[16,8,128]{2,1,0:T(8,128)S(1)}, u32[]{:S(2)}, u32[]{:S(2)}) collective-permute-start(f32[16,8,128]{2,1,0:T(8,128)S(1)} %join.3.refs_0_), channel_id=1, source_target_pairs={{0,96},{32,0},{64,32},{96,64},{1,97},{33,1},{65,33},{97,65},{2,98}... | collective-permute-start | bytes 196616 | tf_op jit(solution)/shard_map/ppermute | solution.py:260
  57.9 4.7 %collective-permute-start.8 = (f32[16,8,128]{2,1,0:T(8,128)S(1)}, f32[16,8,128]{2,1,0:T(8,128)S(1)}, u32[]{:S(2)}, u32[]{:S(2)}) collective-permute-start(f32[16,8,128]{2,1,0:T(8,128)S(1)} %join.3.refs_0_), channel_id=1, source_target_pairs={{0,64},{32,96},{64,0},{96,32},{1,65},{33,97},{65,1},{97,33},{2,66}... | collective-permute-start | bytes 196616 | tf_op jit(solution)/shard_map/ppermute | solution.py:260
  57.9 5.0 %collective-permute-start.7 = (f32[16,8,128]{2,1,0:T(8,128)S(1)}, f32[16,8,128]{2,1,0:T(8,128)S(1)}, u32[]{:S(2)}, u32[]{:S(2)}) collective-permute-start(f32[16,8,128]{2,1,0:T(8,128)S(1)} %join.3.refs_0_), channel_id=1, source_target_pairs={{0,32},{32,64},{64,96},{96,0},{1,33},{33,65},{65,97},{97,1},{2,34}... | collective-permute-start | bytes 196616 | tf_op jit(solution)/shard_map/ppermute | solution.py:260
  64.0 1.3 copy-start.4
  65.3 36.2 %copy-start.5 = (bf16[256,16]{0,1:T(8,128)(2,1)S(1)}, bf16[256,16]{0,1:T(8,128)(2,1)}, u32[]{:S(2)}) copy-start(bf16[256,16]{0,1:T(8,128)(2,1)} %param.8) | copy-start | bytes 24580
  65.3 30.9 %all-to-all-start.1 = ((bf16[64,128,128]{2,1,0:T(8,128)(2,1)}), bf16[64,128,128]{2,1,0:T(8,128)(2,1)}, u32[]{:S(2)}, u32[]{:S(2)}) async-start(bf16[64,128,128]{2,1,0:T(8,128)(2,1)} %copy-done.4), calls=%async_computation.1 | async-start | bytes 4194304 | tf_op jit(solution)/shard_map/all_to_all | solution.py:346
  71.0 34.5 %collective-permute-start.11 = (bf16[64,128,128]{2,1,0:T(8,128)(2,1)}, bf16[64,128,128]{2,1,0:T(8,128)(2,1)}, u32[]{:S(2)}, u32[]{:S(2)}) collective-permute-start(bf16[64,128,128]{2,1,0:T(8,128)(2,1)} %get-tuple-element.17), channel_id=1, source_target_pairs={{0,1},{1,0},{2,3},{3,2},{4,5},{5,4},{6,7},{7,6},{8,9},{9,8},{10,11... | collective-permute-start | bytes 6291464 | tf_op jit(solution)/shard_map/ppermute | solution.py:328
  74.7 44.8 %copy-start.1 = (bf16[256,4096]{1,0:T(8,128)(2,1)S(1)}, bf16[256,4096]{1,0:T(8,128)(2,1)}, u32[]{:S(2)}) copy-start(bf16[256,4096]{1,0:T(8,128)(2,1)} %query_ref.3) | copy-start | bytes 6291460
  74.7 30.8 %collective-permute-start.12 = (bf16[64,128,128]{2,1,0:T(8,128)(2,1)}, bf16[64,128,128]{2,1,0:T(8,128)(2,1)}, u32[]{:S(2)}, u32[]{:S(2)}) collective-permute-start(bf16[64,128,128]{2,1,0:T(8,128)(2,1)} %get-tuple-element.18), channel_id=1, source_target_pairs={{0,1},{1,0},{2,3},{3,2},{4,5},{5,4},{6,7},{7,6},{8,9},{9,8},{10,11... | collective-permute-start | bytes 6291464 | tf_op jit(solution)/shard_map/ppermute | solution.py:327
  96.2 33.0 %collective-permute-start.10 = (bf16[64,128,128]{2,1,0:T(8,128)(2,1)}, bf16[64,128,128]{2,1,0:T(8,128)(2,1)S(1)}, u32[]{:S(2)}, u32[]{:S(2)}) collective-permute-start(bf16[64,128,128]{2,1,0:T(8,128)(2,1)} %all-to-all-done.1.start_ref), channel_id=1, source_target_pairs={{0,1},{1,0},{2,3},{3,2},{4,5},{5,4},{6,7},{7,6},{8,9},{9,8},{10,11... | collective-permute-start | bytes 6291464 | tf_op jit(solution)/shard_map/ppermute | solution.py:347
  101.5 4.0 %collective-permute-start.13 = (bf16[16,256]{1,0:T(8,128)(2,1)S(1)}, bf16[16,256]{1,0:T(8,128)(2,1)S(1)}, u32[]{:S(2)}, u32[]{:S(2)}) collective-permute-start(bf16[16,256]{1,0:T(8,128)(2,1)S(1)} %bitcast.13), channel_id=1, source_target_pairs={{0,1},{1,0},{2,3},{3,2},{4,5},{5,4},{6,7},{7,6},{8,9},{9,8},{10,11... | collective-permute-start | bytes 24584 | tf_op jit(solution)/shard_map/ppermute | solution.py:329
  105.5 14.0 %copy-start.2 = (bf16[256,8192]{1,0:T(8,128)(2,1)S(1)}, bf16[256,8192]{1,0:T(8,128)(2,1)}, u32[]{:S(2)}) copy-start(bf16[256,8192]{1,0:T(8,128)(2,1)} %gate_ref.3) | copy-start | bytes 12582916
  119.5 3.4 %copy-start = (f32[2,8,256,512]{3,2,1,0:T(8,128)S(1)}, f32[2,8,256,512]{3,2,1,0:T(8,128)}, u32[]{:S(2)}) copy-start(f32[2,8,256,512]{3,2,1,0:T(8,128)} %get-tuple-element.20.ready_ref) | copy-start | bytes 25165828
  122.9 1.6 %copy-start.3 = (f32[16,256,128]{2,1,0:T(8,128)S(1)}, f32[16,256,128]{2,1,0:T(8,128)}, u32[]{:S(2)}) copy-start(f32[16,256,128]{2,1,0:T(8,128)} %get-tuple-element.19.reach_ref) | copy-start | bytes 6291460

commit v11 on v9

--- a/solution.py
+++ b/solution.py
@@ -70,10 +70,10 @@
     return copies
 
 
-def states_into(refs, group, step, key_ref, value_ref, fade_ref):
+def states_into(refs, step, key_ref, value_ref, fade_ref):
     for n in range(PER_STEP):
         at = step * PER_STEP + n
-        fade = column(fade_ref[...], group * HALF + at)
+        fade = jnp.concatenate([fade_ref[at]] * (DK // 128), axis=1)
         faded = (key_ref[:, n * DK : (n + 1) * DK].astype(f32) * fade).astype(bf16)
         state = lax.dot_general(
             faded, value_ref[:, n * DV : (n + 1) * DV], (((0,), (0,)), ((), ())),
@@ -83,9 +83,11 @@
             put_slices(ref, place, state)
 
 
-def fades_of(decay):
+def put_fades(ref, decay, group):
     run = running_of(decay)
-    return jnp.exp(run[ROWS - 1 : ROWS, :] - run)
+    fades = jnp.exp(run[ROWS - 1 : ROWS, :] - run)
+    for n in range(HALF):
+        ref[n] = jnp.broadcast_to(column(fades, group * HALF + n), (ROWS, 128))
 
 
 def totals_of(decay):
@@ -105,11 +107,11 @@
 
     @pl.when(step == 0)
     def _():
-        fade_ref[...] = fades_of(decay_ref[...])
+        put_fades(fade_ref, decay_ref[...], group_ref[0])
         for k, third in enumerate(thirds_of(totals_of(decay_ref[...]))):
             out_ref[CHIPS, k * HEADS : (k + 1) * HEADS, :] = third.astype(bf16)
 
-    states_into((out_ref,), group_ref[0], step, key_ref, value_ref, fade_ref)
+    states_into((out_ref,), step, key_ref, value_ref, fade_ref)
 
 
 def own_kernel(
@@ -120,12 +122,12 @@
 
     @pl.when(step == 0)
     def _():
-        fade_ref[...] = fades_of(decay_ref[...])
+        put_fades(fade_ref, decay_ref[...], group_ref[0])
         total_ref[...] = totals_of(decay_ref[...])
 
     size = PER_STEP * SLICES
     theirs_copy_ref[...] = theirs_ref[pl.ds(step * size, size)]
-    states_into((out_ref, own_copy_ref), group_ref[0], step, key_ref, value_ref, fade_ref)
+    states_into((out_ref, own_copy_ref), step, key_ref, value_ref, fade_ref)
 
 
 def combine_kernel(core_ref, own_ref, got_ref, total_ref, out_ref, buf_ref, rate_ref, sems):
@@ -149,7 +151,9 @@
             both = own_ref[o].astype(f32) * own_rate + got_ref[o].astype(f32) * got_rate
             buf_ref[o, :SLICE, :] = both.astype(bf16)
             buf_ref[o, SLICE:SENT, :] = parts
-        block = pl.ds(n * SLICES, SLICES)
+        if n % 2 == 0:
+            continue
+        block = pl.ds((n - 1) * SLICES, 2 * SLICES)
         copies.extend(start_all((
             pltpu.make_async_copy(buf_ref.at[block], out_ref.at[block], sems.at[n]),
         )))
@@ -271,6 +275,7 @@
     slices = pltpu.VMEM((CHIPS, SLICE, 128), bf16)
 
     away = pl.BlockSpec(memory_space=pl.ANY)
+    fades = pltpu.VMEM((HALF, ROWS, 128), f32)
     key_far, value_far, decay_far = far(key_vectors), far(values), far(decay)
     stored = pltpu.HBM((CHIPS, SLICE, 128), bf16)
     wide = lambda width: pl.BlockSpec(
@@ -279,14 +284,14 @@
     pieces = pl.BlockSpec((SLICES * PER_STEP, SLICE, 128), lambda i, c: (i, 0, 0))
     theirs_state = call(
         theirs_kernel, steps, [wide(DK), wide(DV), decays], here,
-        pltpu.VMEM((CHIPS + 1, SLICE, 128), bf16), [table], flops
+        pltpu.VMEM((CHIPS + 1, SLICE, 128), bf16), [fades], flops
     )(other, key_far, value_far, decay_far)
     got = lax.ppermute(theirs_state, "core", swap)
     own_state, totals, late_own, late_theirs = call(
         own_kernel, steps, [wide(DK), wide(DV), decays, here],
         [here, here, pieces, pieces],
         [slices, pltpu.VMEM((HEADS, 128), f32), stored, stored],
-        [table], flops,
+        [fades], flops,
     )(core, key_far, value_far, decay_far, near(theirs_state))
     block_state = call(
         combine_kernel, 1, [here, here, here], away,

time: 128 us -> 128 us (level)
  no operation moved by 1% of the time
where the time goes in v11:
time: 128 us; the launch traced here: 127 us
  blocking collectives  42.2 us (33%)
  Pallas kernels  35.5 us (28%)
  waiting for transfers between devices  28.4 us (22%)
  starting transfers between devices  13.5 us (11%)
  local copies, waits for them, and re-layouts  7.36 us (6%)
    all_to_all x1, blocking collectives, shards(): collected = lax.all_to_all(block_state, everyone, 0, 0, tiled=True)  42.2 us
    all_to_all x1, waiting for transfers between devices, shards(): start = lax.all_to_all(starts, everyone, 0, 0, tiled=True)  24.4 us
    pallas_call x1, Pallas kernels, shards(): call(within_kernel, HALF, [heads(DK), heads(DK), heads(DV), heads(DV), th...  18.2 us
    unnamed x8, local copies, waits for them, and re-layouts  7.36 us
    all_to_all x1, starting transfers between devices, shards(): start = lax.all_to_all(starts, everyone, 0, 0, tiled=True)  6 us
    pallas_call x1, Pallas kernels, shards(): call(own_kernel, steps, [wide(DK), wide(DV), decays, here], [here, here,...  4.41 us
    ppermute x1, starting transfers between devices, shards(): their_start = lax.ppermute(start, 'core', swap)  4.15 us
    pallas_call x1, Pallas kernels, shards(): call(partial(finish_kernel, 0), 1, specs, away, result, scratch, flops)  4.03 us
  transfers between devices with their start and end apart: 6, of which 2 were waited for; matrix products, arithmetic and copies ran while one was open for 0% of the time, Pallas kernels for 21%

profile of v11, /device:TPU:1, one launch (start us, length us, event | category | flops | bytes accessed | tf_op | source)
XLA Modules:
  0.0 127.1 jit_solution(14522185308403619357)
XLA Ops:
  0.0 3.0 %shard_map.55.theirs_ref = bf16[65,128,128]{2,1,0:T(8,128)(2,1)S(1)} custom-call(s32[1]{0:T(128)S(6)} %sub.3.group_ref, bf16[256,4096]{1,0:T(8,128)(2,1)} %refs_5_.1, bf16[256,8192]{1,0:T(8,128)(2,1)} %refs_6_.1, bf16[16,256]{1,0:T(8,128)(2,1)} %bitcast.2), custom_call_target="tpu_custom_call" | custom-call | flops 536870912 | tf_op jit(solution)/shard_map/pallas_call | solution.py:285
  3.0 1.5 %collective-permute-start = (bf16[65,128,128]{2,1,0:T(8,128)(2,1)S(1)}, bf16[65,128,128]{2,1,0:T(8,128)(2,1)S(1)}, u32[]{:S(2)}, u32[]{:S(2)}) collective-permute-start(bf16[65,128,128]{2,1,0:T(8,128)(2,1)S(1)} %shard_map.55.theirs_ref), channel_id=1, source_target_pairs={{0,1},{1,0},{2,3},{3,2},{4,5},{5,4},{6,7},{7,6},{8,9},{9,8},{10,11... | collective-permute-start | bytes 6389768 | tf_op jit(solution)/shard_map/ppermute | solution.py:289
  4.4 4.4 %shard_map.56 = (bf16[64,128,128]{2,1,0:T(8,128)(2,1)S(1)}, f32[16,128]{1,0:T(8,128)S(1)}, bf16[64,128,128]{2,1,0:T(8,128)(2,1)}, bf16[64,128,128]{2,1,0:T(8,128)(2,1)}) custom-call(s32[1]{0:T(128)} %bitcast.group_ref.core_ref, bf16[256,4096]{1,0:T(8,128)(2,1)} %refs_5_.1, bf16[256,8192]{1,0:T(8,128)(2,1)} %refs_6_.1, bf16[16,256]{1,0:T(8,128)(2,1)} %bitcast.3, ...), custom_call_target="tpu_custom_call" | custom-call | flops 536870912 | tf_op jit(solution)/shard_map/pallas_call | solution.py:290
  8.8 0.0 collective-permute-done.got_ref
  8.8 1.7 %shard_map.57 = bf16[64,136,128]{2,1,0:T(8,128)(2,1)} custom-call(s32[1]{0:T(128)} %bitcast.group_ref.core_ref, bf16[64,128,128]{2,1,0:T(8,128)(2,1)S(1)} %get-tuple-element.11.own_ref, bf16[65,128,128]{2,1,0:T(8,128)(2,1)S(1)} %collective-permute-done.got_ref, f32[16,128]{1,0:T(8,128)S(1)} %get-tuple-element.12.total_ref), custom_call_target="tpu_custom_call" | custom-call | flops 67108864 | tf_op jit(solution)/shard_map/pallas_call | solution.py:296
  10.5 42.2 %all_to_all.10.in_ref = bf16[64,136,128]{2,1,0:T(8,128)(2,1)S(1)} all-to-all(bf16[64,136,128]{2,1,0:T(8,128)(2,1)} %shard_map.57), channel_id=1, replica_groups=mesh['seq'=4,'chip'=16,'core'=2] {'seq','chip'}, dimensions={0} | all-to-all | bytes 4456448 | tf_op jit(solution)/shard_map/all_to_all | solution.py:304
  52.7 1.8 %prefix.1 = bf16[64,128,128]{2,1,0:T(8,128)(2,1)} custom-call(bf16[64,136,128]{2,1,0:T(8,128)(2,1)S(1)} %all_to_all.10.in_ref), custom_call_target="tpu_custom_call" | custom-call | flops 10000000000 | tf_op jit(solution)/shard_map/prefix/pallas_call | solution.py:320
  54.6 0.0 copy-start.3
  54.6 6.0 %all-to-all-start.1 = ((bf16[64,128,128]{2,1,0:T(8,128)(2,1)}), bf16[64,128,128]{2,1,0:T(8,128)(2,1)}, u32[]{:S(2)}, u32[]{:S(2)}) async-start(bf16[64,128,128]{2,1,0:T(8,128)(2,1)} %prefix.1), calls=%async_computation.1 | async-start | bytes 4194304 | tf_op jit(solution)/shard_map/all_to_all | solution.py:329
  60.6 1.8 %collective-permute-start.2 = (bf16[64,128,128]{2,1,0:T(8,128)(2,1)}, bf16[64,128,128]{2,1,0:T(8,128)(2,1)}, u32[]{:S(2)}, u32[]{:S(2)}) collective-permute-start(bf16[64,128,128]{2,1,0:T(8,128)(2,1)} %get-tuple-element.13), channel_id=1, source_target_pairs={{0,1},{1,0},{2,3},{3,2},{4,5},{5,4},{6,7},{7,6},{8,9},{9,8},{10,11... | collective-permute-start | bytes 6291464 | tf_op jit(solution)/shard_map/ppermute | solution.py:306
  62.4 0.0 copy-start.1
  62.4 0.1 collective-permute-start.3
  62.5 24.4 %all-to-all-done.1.start_ref = bf16[64,128,128]{2,1,0:T(8,128)(2,1)} async-done(((bf16[64,128,128]{2,1,0:T(8,128)(2,1)}), bf16[64,128,128]{2,1,0:T(8,128)(2,1)}, u32[]{:S(2)}, u32[]{:S(2)}) %all-to-all-start.1) | async-done | bytes 2097184 | tf_op jit(solution)/shard_map/all_to_all | solution.py:329
  86.9 4.2 %collective-permute-start.1 = (bf16[64,128,128]{2,1,0:T(8,128)(2,1)}, bf16[64,128,128]{2,1,0:T(8,128)(2,1)S(1)}, u32[]{:S(2)}, u32[]{:S(2)}) collective-permute-start(bf16[64,128,128]{2,1,0:T(8,128)(2,1)} %all-to-all-done.1.start_ref), channel_id=1, source_target_pairs={{0,1},{1,0},{2,3},{3,2},{4,5},{5,4},{6,7},{7,6},{8,9},{9,8},{10,11... | collective-permute-start | bytes 6291464 | tf_op jit(solution)/shard_map/ppermute | solution.py:330
  91.0 0.0 copy-done.3
  91.0 0.0 collective-permute-start.4
  91.0 4.0 %collective-permute-done.4.refs_11_ = bf16[16,256]{1,0:T(8,128)(2,1)S(1)} collective-permute-done((bf16[16,256]{1,0:T(8,128)(2,1)S(1)}, bf16[16,256]{1,0:T(8,128)(2,1)S(1)}, u32[]{:S(2)}, u32[]{:S(2)}) %collective-permute-start.4) | collective-permute-done | bytes 8224 | tf_op jit(solution)/shard_map/ppermute | solution.py:307
  95.1 0.0 collective-permute-done.2.refs_8_
  95.1 0.0 collective-permute-done.3.refs_9_
  95.1 18.2 %shard_map.58 = (f32[2,8,256,1024]{3,2,1,0:T(8,128)}, f32[16,256,128]{2,1,0:T(8,128)}) custom-call(s32[1]{0:T(128)} %bitcast.group_ref.core_ref, bf16[256,4096]{1,0:T(8,128)(2,1)} %query_ref.3, bf16[256,4096]{1,0:T(8,128)(2,1)} %refs_5_.1, bf16[256,8192]{1,0:T(8,128)(2,1)} %refs_6_.1, bf16[256,8192]{1,0:T(8,128)(2,1)} %refs_7_.1, ...), custom_call_target="tpu_custom_call" | custom-call | flops 2147483648 | tf_op jit(solution)/shard_map/pallas_call | solution.py:310
  113.2 0.0 copy-done.1
  113.2 0.0 copy-start
  113.2 5.8 %copy-done = f32[2,8,256,1024]{3,2,1,0:T(8,128)S(1)} copy-done((f32[2,8,256,1024]{3,2,1,0:T(8,128)S(1)}, f32[2,8,256,1024]{3,2,1,0:T(8,128)}, u32[]{:S(2)}) %copy-start) | copy-done | bytes 16777240
  119.0 0.0 copy-start.2
  119.0 1.6 %copy-done.2 = f32[16,256,128]{2,1,0:T(8,128)S(1)} copy-done((f32[16,256,128]{2,1,0:T(8,128)S(1)}, f32[16,256,128]{2,1,0:T(8,128)}, u32[]{:S(2)}) %copy-start.2) | copy-done | bytes 2097176
  120.6 4.0 %shard_map.59.rest_0_ = bf16[256,8192]{1,0:T(8,128)(2,1)} custom-call(s32[1]{0:T(128)} %bitcast.group_ref.core_ref, bf16[64,128,128]{2,1,0:T(8,128)(2,1)} %all-to-all-done.1.start_ref, f32[16,256,128]{2,1,0:T(8,128)S(1)} %copy-done.2, bf16[256,4096]{1,0:T(8,128)(2,1)S(1)} %copy-done.1, f32[2,8,256,1024]{3,2,1,0:T(8,128)S(1)} %copy-done), custom_call_target="tpu_custom_call" | custom-call | flops 536870912 | tf_op jit(solution)/shard_map/pallas_call | solution.py:336
  124.6 0.0 collective-permute-done.1.start_ref
  124.6 2.4 %shard_map.60 = bf16[256,8192]{1,0:T(8,128)(2,1)} custom-call(s32[1]{0:T(128)S(6)} %sub.3.group_ref, bf16[64,128,128]{2,1,0:T(8,128)(2,1)S(1)} %collective-permute-done.1.start_ref, f32[16,256,128]{2,1,0:T(8,128)S(1)} %copy-done.2, bf16[256,4096]{1,0:T(8,128)(2,1)S(1)} %copy-done.1, f32[2,8,256,1024]{3,2,1,0:T(8,128)S(1)} %copy-done, ...), custom_call_target="tpu_custom_call", output_to_operand_aliasing={{}: (5, {})} | custom-call | flops 536870912 | tf_op jit(solution)/shard_map/pallas_call | solution.py:339
Async XLA Ops:
  3.0 5.9 %collective-permute-start = (bf16[65,128,128]{2,1,0:T(8,128)(2,1)S(1)}, bf16[65,128,128]{2,1,0:T(8,128)(2,1)S(1)}, u32[]{:S(2)}, u32[]{:S(2)}) collective-permute-start(bf16[65,128,128]{2,1,0:T(8,128)(2,1)S(1)} %shard_map.55.theirs_ref), channel_id=1, source_target_pairs={{0,1},{1,0},{2,3},{3,2},{4,5},{5,4},{6,7},{7,6},{8,9},{9,8},{10,11... | collective-permute-start | bytes 6389768 | tf_op jit(solution)/shard_map/ppermute | solution.py:289
  54.6 36.5 %copy-start.3 = (bf16[256,16]{0,1:T(8,128)(2,1)S(1)}, bf16[256,16]{0,1:T(8,128)(2,1)}, u32[]{:S(2)}) copy-start(bf16[256,16]{0,1:T(8,128)(2,1)} %param.8) | copy-start | bytes 24580
  54.6 32.3 %all-to-all-start.1 = ((bf16[64,128,128]{2,1,0:T(8,128)(2,1)}), bf16[64,128,128]{2,1,0:T(8,128)(2,1)}, u32[]{:S(2)}, u32[]{:S(2)}) async-start(bf16[64,128,128]{2,1,0:T(8,128)(2,1)} %prefix.1), calls=%async_computation.1 | async-start | bytes 4194304 | tf_op jit(solution)/shard_map/all_to_all | solution.py:329
  60.6 34.5 %collective-permute-start.2 = (bf16[64,128,128]{2,1,0:T(8,128)(2,1)}, bf16[64,128,128]{2,1,0:T(8,128)(2,1)}, u32[]{:S(2)}, u32[]{:S(2)}) collective-permute-start(bf16[64,128,128]{2,1,0:T(8,128)(2,1)} %get-tuple-element.13), channel_id=1, source_target_pairs={{0,1},{1,0},{2,3},{3,2},{4,5},{5,4},{6,7},{7,6},{8,9},{9,8},{10,11... | collective-permute-start | bytes 6291464 | tf_op jit(solution)/shard_map/ppermute | solution.py:306
  62.4 50.9 %copy-start.1 = (bf16[256,4096]{1,0:T(8,128)(2,1)S(1)}, bf16[256,4096]{1,0:T(8,128)(2,1)}, u32[]{:S(2)}) copy-start(bf16[256,4096]{1,0:T(8,128)(2,1)} %query_ref.3) | copy-start | bytes 6291460
  62.4 32.7 %collective-permute-start.3 = (bf16[64,128,128]{2,1,0:T(8,128)(2,1)}, bf16[64,128,128]{2,1,0:T(8,128)(2,1)}, u32[]{:S(2)}, u32[]{:S(2)}) collective-permute-start(bf16[64,128,128]{2,1,0:T(8,128)(2,1)} %get-tuple-element.14), channel_id=1, source_target_pairs={{0,1},{1,0},{2,3},{3,2},{4,5},{5,4},{6,7},{7,6},{8,9},{9,8},{10,11... | collective-permute-start | bytes 6291464 | tf_op jit(solution)/shard_map/ppermute | solution.py:305
  86.9 37.7 %collective-permute-start.1 = (bf16[64,128,128]{2,1,0:T(8,128)(2,1)}, bf16[64,128,128]{2,1,0:T(8,128)(2,1)S(1)}, u32[]{:S(2)}, u32[]{:S(2)}) collective-permute-start(bf16[64,128,128]{2,1,0:T(8,128)(2,1)} %all-to-all-done.1.start_ref), channel_id=1, source_target_pairs={{0,1},{1,0},{2,3},{3,2},{4,5},{5,4},{6,7},{7,6},{8,9},{9,8},{10,11... | collective-permute-start | bytes 6291464 | tf_op jit(solution)/shard_map/ppermute | solution.py:330
  91.0 4.0 %collective-permute-start.4 = (bf16[16,256]{1,0:T(8,128)(2,1)S(1)}, bf16[16,256]{1,0:T(8,128)(2,1)S(1)}, u32[]{:S(2)}, u32[]{:S(2)}) collective-permute-start(bf16[16,256]{1,0:T(8,128)(2,1)S(1)} %bitcast.5), channel_id=1, source_target_pairs={{0,1},{1,0},{2,3},{3,2},{4,5},{5,4},{6,7},{7,6},{8,9},{9,8},{10,11... | collective-permute-start | bytes 24584 | tf_op jit(solution)/shard_map/ppermute | solution.py:307
  113.2 5.8 %copy-start = (f32[2,8,256,1024]{3,2,1,0:T(8,128)S(1)}, f32[2,8,256,1024]{3,2,1,0:T(8,128)}, u32[]{:S(2)}) copy-start(f32[2,8,256,1024]{3,2,1,0:T(8,128)} %get-tuple-element.16.ready_ref) | copy-start | bytes 50331652
  119.0 1.6 %copy-start.2 = (f32[16,256,128]{2,1,0:T(8,128)S(1)}, f32[16,256,128]{2,1,0:T(8,128)}, u32[]{:S(2)}) copy-start(f32[16,256,128]{2,1,0:T(8,128)} %get-tuple-element.15.reach_ref) | copy-start | bytes 6291460
